TPU v7x, 256 devices: a whole 4x4x8 slice. The times are simulated.
256 devices in a mesh: pipe: 2 (over x_hi), tensor: 8 (over y, core), seq: 16 (over z, x_lo).
Axes of the slice: x: 4 (x_hi: 2, x_lo: 2; x = x_hi * 2 + x_lo), y: 4, z: 8, core: 2. Of those that a mesh axis runs over, the one named last changes fastest.
Arguments:
- tokens: bfloat16 [2, 2048, 2560], P(None, 'seq', 'tensor'), may hold values from -6 to 6
- prenorm_gain: float32 [2, 2560], P('pipe'), may hold values from 0.5 to 1.5
- gate_weight: bfloat16 [2, 2560, 5120], P('pipe', None, 'tensor'), may hold values from -0.125 to 0.125
- inner_weight: bfloat16 [2, 2560, 5120], P('pipe', None, 'tensor'), may hold values from -0.125 to 0.125
- state_weight: bfloat16 [2, 2560, 256], P('pipe'), may hold values from -0.125 to 0.125
- step_weight: bfloat16 [2, 2560, 80], P('pipe', None, 'tensor'), may hold values from -0.125 to 0.125
- inner_taps: float32 [2, 5, 5120], P('pipe', None, 'tensor'), may hold values from -3 to 3
- state_taps: float32 [2, 5, 256], P('pipe'), may hold values from -3 to 3
- step_bias: float32 [2, 80], P('pipe', 'tensor'), may hold values from -5 to -2
- decay_rate: float32 [2, 80], P('pipe', 'tensor'), may hold values from 0.00048828125 to 1
- skip_scale: float32 [2, 80], P('pipe', 'tensor'), may hold values from 0.5 to 1.5
- inner_gain: float32 [2, 5120], P('pipe', 'tensor'), may hold values from 0.5 to 1.5
- out_weight: bfloat16 [2, 5120, 2560], P('pipe', 'tensor'), may hold values from -0.078125 to 0.078125
Outputs:
- layer_outputs: bfloat16 [2, 2, 2048, 2560], P('pipe', None, 'seq', 'tensor')
All inputs are finite; a program needn't handle non-finite values.
Results may differ from a plain program's by a relative error of at most 0.019.
Values may be sent and summed in bfloat16 or wider, within the bound.
No kernel may reach another device: no remote copies, remote signals or barrier semaphores. Data moves between devices by JAX's collectives and lax.ppermute only.
A program may use at most 64 MiB of HBM per device.

v0:
```python
import jax
import jax.numpy as jnp
from jax import lax
from jax.sharding import Mesh
from jax.sharding import PartitionSpec as P

BLOCK = 128
INNER = 5120
SEQ = ("seq_0", "seq_1")


EPS = 1e-05


def shifted(value, axis, steps):
    count = lax.axis_size(axis)
    first, last = (max(0, -steps), min(count, count - steps))
    return lax.ppermute(value, axis, [(source, source + steps) for source in range(first, last)])


def neutral_like(array, identity):
    return jax.tree.map(
        lambda part, zero: jnp.zeros_like(part) + jnp.asarray(zero, part.dtype), array, identity
    )


def entering_2(array, axes, combine, identity):
    before = start = neutral_like(array, identity)
    running = array
    for axis in reversed(axes):
        size, here = (lax.axis_size(axis), lax.axis_index(axis))
        pieces = jax.tree.map(
            lambda part, kind: lax.all_gather(part.astype(kind), axis),
            running,
            (jnp.bfloat16, jnp.bfloat16),
        )
        inside, running = (start, start)
        for k in range(size):
            passed = k < here
            running = combine(
                running, jax.tree.map(lambda part, own: part[k].astype(own.dtype), pieces, array)
            )
            inside = jax.tree.map(lambda new, old: jnp.where(passed, new, old), running, inside)
        before = combine(inside, before)
    return before


def from_everyone(array, axis):
    size = lax.axis_size(axis)
    return lax.all_to_all(
        jnp.broadcast_to(array[None], (size, *array.shape)), axis, 0, 0, tiled=True
    )


def of_everyone(array, axis):
    everything = from_everyone(array, axis)
    return jnp.sum(everything, axis=0)


def joined_along(parts, dim):
    shape = list(parts.shape[1:])
    shape[dim] *= parts.shape[0]
    return jnp.moveaxis(parts, 0, dim).reshape(shape)


def collect(array, axis, dim):
    return joined_along(from_everyone(array, axis), dim)


def split_up(array, dim, size):
    shape = array.shape
    parts = array.reshape(*shape[:dim], size, shape[dim] // size, *shape[dim + 1 :])
    return jnp.moveaxis(parts, dim, 0)


def sent_and_summed(array, axis, dim):
    parts = split_up(array, dim, lax.axis_size(axis))
    arrived = lax.all_to_all(parts, axis, split_axis=0, concat_axis=0, tiled=True)
    return arrived.astype(jnp.float32).sum(axis=0)


def causal_taps(rim, values, taps):
    width = taps.shape[0] - 1
    length = values.shape[0]
    padded = jnp.concatenate([rim, values], axis=0).astype(jnp.float32)
    total = jnp.broadcast_to(taps[width][None, :], (length, values.shape[1]))
    for index in range(width):
        total = total + taps[index][None, :] * padded[index : index + length]
    return jax.nn.silu(total).astype(jnp.bfloat16)


def fold_states(carried, items):
    decay_acc, state_acc = carried
    decay, state = items
    return ((decay_acc * decay, state_acc * decay[:, None, None] + state), (decay_acc, state_acc))


def combine_states(earlier, later):
    return (earlier[0] * later[0], earlier[1] * later[0][:, None, None] + later[1])


def mixer(current, weights):
    (
        prenorm,
        gate_weight,
        inner_weight,
        state_weight,
        step_weight,
        inner_taps,
        state_taps,
        step_bias,
        decay_rate,
        skip_scale,
        inner_gain,
        out_weight,
    ) = weights
    rows = current.shape[0]
    widened = current.astype(jnp.float32)
    normed_in = (
        widened * lax.rsqrt(jnp.mean(widened * widened, axis=1, keepdims=True) + EPS) * prenorm
    ).astype(jnp.bfloat16)
    gate_raw = jnp.dot(normed_in, gate_weight, preferred_element_type=jnp.float32).astype(
        jnp.bfloat16
    )
    inner_raw = jnp.dot(normed_in, inner_weight, preferred_element_type=jnp.float32).astype(
        jnp.bfloat16
    )
    state_raw = jnp.dot(normed_in, state_weight, preferred_element_type=jnp.float32).astype(
        jnp.bfloat16
    )
    step_raw = jnp.dot(normed_in, step_weight, preferred_element_type=jnp.float32)
    inner_width = inner_raw.shape[1]
    reach = inner_taps.shape[0] - 2
    rim = shifted(
        jnp.concatenate([inner_raw[rows - reach :], state_raw[rows - reach :]], axis=1), SEQ, 1
    )
    inner_conv = causal_taps(rim[:, :inner_width], inner_raw, inner_taps)
    state_conv = causal_taps(rim[:, inner_width:], state_raw, state_taps)
    heads = step_bias.shape[0]
    head_size = inner_width // heads
    state_size = state_raw.shape[1] // 2
    blocks = rows // BLOCK
    step_size = jax.nn.softplus(step_raw + step_bias)
    step_blocks = step_size.reshape(blocks, BLOCK, heads)
    cumulative = jnp.cumsum(-step_blocks * decay_rate, axis=1)
    inner_blocks = inner_conv.reshape(blocks, BLOCK, heads, head_size)
    input_blocks = state_conv[:, :state_size].reshape(blocks, BLOCK, state_size)
    output_blocks = state_conv[:, state_size:].reshape(blocks, BLOCK, state_size)
    weighting = jnp.exp(cumulative[:, -1:, :] - cumulative) * step_blocks
    weighted = (inner_blocks.astype(jnp.float32) * weighting[..., None]).astype(jnp.bfloat16)
    states = jnp.einsum(
        "bshp,bsn->bhpn", weighted, input_blocks, preferred_element_type=jnp.float32
    )
    decays = jnp.exp(cumulative[:, -1, :])
    start = (
        jnp.ones((heads,), jnp.float32),
        jnp.zeros((heads, head_size, state_size), jnp.float32),
    )
    (device_decay, device_state), (prior_decay, prior_state) = lax.scan(
        fold_states, start, (decays, states)
    )
    entry_decay, entry_state = entering_2(
        (device_decay, device_state),
        SEQ,
        combine_states,
        (jnp.ones_like(device_decay), jnp.zeros_like(device_state)),
    )
    scores = jnp.einsum(
        "bqn,bsn->bqs", output_blocks, input_blocks, preferred_element_type=jnp.float32
    )
    by_head = jnp.transpose(cumulative, (0, 2, 1))
    later = lax.broadcasted_iota(jnp.int32, (BLOCK, BLOCK), 0) >= lax.broadcasted_iota(
        jnp.int32, (BLOCK, BLOCK), 1
    )
    decay = jnp.exp(jnp.where(later, by_head[:, :, :, None] - by_head[:, :, None, :], -jnp.inf))
    mixing = (
        scores[:, None] * decay * jnp.transpose(step_blocks, (0, 2, 1))[:, :, None, :]
    ).astype(jnp.bfloat16)
    inside = jnp.einsum("bhqs,bshp->bqhp", mixing, inner_blocks, preferred_element_type=jnp.float32)
    entering = prior_state + prior_decay[:, :, None, None] * entry_state[None]
    across = jnp.exp(cumulative)[..., None] * jnp.einsum(
        "bqn,bhpn->bqhp", output_blocks.astype(jnp.float32), entering
    )
    mixed = inside + across + skip_scale[None, None, :, None] * inner_blocks.astype(jnp.float32)
    mixed = mixed.reshape(rows, inner_width)
    gated = mixed * jax.nn.silu(gate_raw.astype(jnp.float32))
    squares = of_everyone(jnp.sum(gated * gated, axis=1), "tensor")
    normed = (gated * lax.rsqrt(squares / INNER + EPS)[:, None] * inner_gain).astype(jnp.bfloat16)
    return jnp.dot(normed, out_weight, preferred_element_type=jnp.float32)


def shards(
    tokens,
    prenorm_gain,
    gate_weight,
    inner_weight,
    state_weight,
    step_weight,
    inner_taps,
    state_taps,
    step_bias,
    decay_rate,
    skip_scale,
    inner_gain,
    out_weight,
):
    weights = (
        prenorm_gain[0],
        gate_weight[0],
        inner_weight[0],
        state_weight[0],
        step_weight[0],
        inner_taps[0],
        state_taps[0],
        step_bias[0],
        decay_rate[0],
        skip_scale[0],
        inner_gain[0],
        out_weight[0],
    )
    sections = lax.axis_size("pipe")
    section = lax.axis_index("pipe")
    share = lax.axis_size("tensor")
    member = lax.axis_index("tensor")
    all_tokens = collect(tokens, "tensor", 2)
    micro_count, rows, width = all_tokens.shape
    narrow = width // share
    outputs = jnp.zeros((micro_count, rows, narrow), jnp.bfloat16)
    carried = None
    rounds = micro_count + sections - 1
    for turn in range(rounds):
        fresh = all_tokens[min(turn, micro_count - 1)]
        if turn == 0:
            current = fresh
        else:
            incoming = collect(carried, "tensor", 1)
            current = jnp.where(section == 0, fresh, incoming)
        term = mixer(current, weights)
        summed = sent_and_summed(term.astype(jnp.bfloat16), "tensor", 1)
        base = lax.dynamic_slice_in_dim(current, member * narrow, narrow, 1)
        own = (base.astype(jnp.float32) + summed).astype(jnp.bfloat16)
        micro = turn - section
        valid = jnp.logical_and(micro >= 0, micro < micro_count)
        position = jnp.clip(micro, 0, micro_count - 1)
        previous = lax.dynamic_index_in_dim(outputs, position, 0, keepdims=False)
        outputs = lax.dynamic_update_index_in_dim(
            outputs, jnp.where(valid, own, previous), position, 0
        )
        if turn + 1 < rounds:
            carried = shifted(own, "pipe", 1)
    return outputs[None]


def solution(mesh):
    torus = Mesh(
        mesh.devices.reshape(mesh.shape["pipe"], mesh.shape["tensor"], 8, 2),
        ("pipe", "tensor", "seq_0", "seq_1"),
    )
    return jax.shard_map(
        shards,
        mesh=torus,
        in_specs=(
            P(None, SEQ, "tensor"),
            P("pipe", None),
            P("pipe", None, "tensor"),
            P("pipe", None, "tensor"),
            P("pipe", None, None),
            P("pipe", None, "tensor"),
            P("pipe", None, "tensor"),
            P("pipe", None, None),
            P("pipe", "tensor"),
            P("pipe", "tensor"),
            P("pipe", "tensor"),
            P("pipe", "tensor"),
            P("pipe", "tensor", None),
        ),
        out_specs=P("pipe", None, SEQ, "tensor"),
        check_vma=False,
    )
```

profile of v0, /device:TPU:5, one launch (start us, length us, event | category | flops | bytes accessed | tf_op | source)
XLA Modules:
  0.0 445.6 jit_solution(13413323776747706453)
XLA Ops:
  8.9 5.3 %all-to-all-start = ((bf16[8,2,128,320]{2,3,1,0:T(8,128)(2,1)}), bf16[8,2,128,320]{2,3,1,0:T(8,128)(2,1)}, u32[]{:S(2)}, u32[]{:S(2)}) async-start(bf16[8,2,128,320]{2,3,1,0:T(8,128)(2,1)} %broadcast_in_dim.70), calls=%async_computation | async-start | bytes 2621440 | tf_op jit(solution)/shard_map/all_to_all | solution.py:50
  15.6 16.5 %all-to-all-done = bf16[8,2,128,320]{2,3,1,0:T(8,128)(2,1)} async-done(((bf16[8,2,128,320]{2,3,1,0:T(8,128)(2,1)}), bf16[8,2,128,320]{2,3,1,0:T(8,128)(2,1)}, u32[]{:S(2)}, u32[]{:S(2)}) %all-to-all-start) | async-done | bytes 1310752 | tf_op jit(solution)/shard_map/all_to_all | solution.py:50
  43.1 3.4 collective-permute-start
  62.3 4.8 %all-gather.1 = bf16[20,64,128]{2,1,0:T(8,128)(2,1)S(1)} all-gather(bf16[10,64,128]{2,1,0:T(8,128)(2,1)S(1)} %fusion.39), channel_id=3, replica_groups=mesh['pipe'=2,'tensor'=8,'seq_0'=8,'seq_1'=2] {'seq_1'}, dimensions={0}, use_global_device_ids=true | all-gather | bytes 491520 | tf_op jit(solution)/shard_map/all_gather | solution.py:33
  71.5 14.8 %all-gather.6 = bf16[8,1,10]{2,1,0:T(2,128)(2,1)S(1)} all-gather(bf16[1,1,10]{2,1,0:T(2,128)(2,1)S(1)} %multiply_convert_fusion.23), channel_id=1, replica_groups=mesh['pipe'=2,'tensor'=8,'seq_0'=8,'seq_1'=2] {'seq_0'}, dimensions={0}, use_global_device_ids=true | all-gather | bytes 180 | tf_op jit(solution)/shard_map/all_gather | solution.py:33
  90.1 16.8 %all-gather.13.cloned.1.call-done = bf16[8,10,64,128]{3,2,1,0:T(8,128)(2,1)} async-done(((bf16[1,10,64,128]{3,2,1,0:T(8,128)(2,1)}), bf16[8,10,64,128]{3,2,1,0:T(8,128)(2,1)}) %all-gather.13.cloned.1.call-update) | async-done | bytes 1310736 | tf_op jit(solution)/shard_map/all_gather | solution.py:33
  112.3 3.6 multiply_reduce_fusion.2
  116.5 9.2 %all-to-all-start.1 = ((f32[8,1,128]{2,1,0:T(1,128)}), f32[8,1,128]{2,1,0:T(1,128)S(1)}, u32[]{:S(2)}, u32[]{:S(2)}) async-start(f32[8,1,128]{2,1,0:T(1,128)} %broadcast_in_dim.77), calls=%async_computation.1 | async-start | bytes 8192 | tf_op jit(solution)/shard_map/all_to_all | solution.py:50
  125.7 4.5 %all-to-all-done.1 = f32[8,1,128]{2,1,0:T(1,128)S(1)} async-done(((f32[8,1,128]{2,1,0:T(1,128)}), f32[8,1,128]{2,1,0:T(1,128)S(1)}, u32[]{:S(2)}, u32[]{:S(2)}) %all-to-all-start.1) | async-done | bytes 4128 | tf_op jit(solution)/shard_map/all_to_all | solution.py:50
  135.0 4.8 %all-to-all-start.2 = ((bf16[8,128,320]{1,2,0:T(8,128)(2,1)}), bf16[8,128,320]{1,2,0:T(8,128)(2,1)}, u32[]{:S(2)}, u32[]{:S(2)}) async-start(bf16[8,128,320]{1,2,0:T(8,128)(2,1)} %bitcast.493), calls=%async_computation.2 | async-start | bytes 1310720 | tf_op jit(solution)/shard_map/all_to_all | solution.py:78
  142.2 8.5 %all-to-all-done.2 = bf16[8,128,320]{1,2,0:T(8,128)(2,1)} async-done(((bf16[8,128,320]{1,2,0:T(8,128)(2,1)}), bf16[8,128,320]{1,2,0:T(8,128)(2,1)}, u32[]{:S(2)}, u32[]{:S(2)}) %all-to-all-start.2) | async-done | bytes 655392 | tf_op jit(solution)/shard_map/all_to_all | solution.py:78
  154.1 5.4 %collective-permute-done.1 = bf16[128,320]{0,1:T(8,128)(2,1)S(1)} collective-permute-done((bf16[128,320]{0,1:T(8,128)(2,1)S(1)}, bf16[128,320]{0,1:T(8,128)(2,1)S(1)}, u32[]{:S(2)}, u32[]{:S(2)}) %collective-permute-start.1) | collective-permute-done | bytes 81952 | tf_op jit(solution)/shard_map/ppermute | solution.py:18
  160.4 6.2 %all-to-all-start.3 = ((bf16[8,128,320]{1,2,0:T(8,128)(2,1)}), bf16[8,128,320]{1,2,0:T(8,128)(2,1)}, u32[]{:S(2)}, u32[]{:S(2)}) async-start(bf16[8,128,320]{1,2,0:T(8,128)(2,1)} %broadcast_in_dim.79), calls=%async_computation.3 | async-start | bytes 1310720 | tf_op jit(solution)/shard_map/all_to_all | solution.py:50
  166.6 10.9 %all-to-all-done.3 = bf16[8,128,320]{1,2,0:T(8,128)(2,1)} async-done(((bf16[8,128,320]{1,2,0:T(8,128)(2,1)}), bf16[8,128,320]{1,2,0:T(8,128)(2,1)}, u32[]{:S(2)}, u32[]{:S(2)}) %all-to-all-start.3) | async-done | bytes 655392 | tf_op jit(solution)/shard_map/all_to_all | solution.py:50
  193.0 3.4 collective-permute-start.2
  212.9 4.8 %all-gather.3 = bf16[20,64,128]{2,1,0:T(8,128)(2,1)S(1)} all-gather(bf16[10,64,128]{2,1,0:T(8,128)(2,1)S(1)} %fusion.40), channel_id=5, replica_groups=mesh['pipe'=2,'tensor'=8,'seq_0'=8,'seq_1'=2] {'seq_1'}, dimensions={0}, use_global_device_ids=true | all-gather | bytes 491520 | tf_op jit(solution)/shard_map/all_gather | solution.py:33
  222.2 10.7 %all-gather.7 = bf16[8,1,10]{2,1,0:T(2,128)(2,1)S(1)} all-gather(bf16[1,1,10]{2,1,0:T(2,128)(2,1)S(1)} %multiply_convert_fusion.22), channel_id=1, replica_groups=mesh['pipe'=2,'tensor'=8,'seq_0'=8,'seq_1'=2] {'seq_0'}, dimensions={0}, use_global_device_ids=true | all-gather | bytes 180 | tf_op jit(solution)/shard_map/all_gather | solution.py:33
  239.1 14.4 %all-gather.15.cloned.1.call-done = bf16[8,10,64,128]{3,2,1,0:T(8,128)(2,1)} async-done(((bf16[1,10,64,128]{3,2,1,0:T(8,128)(2,1)}), bf16[8,10,64,128]{3,2,1,0:T(8,128)(2,1)}) %all-gather.15.cloned.1.call-update) | async-done | bytes 1310736 | tf_op jit(solution)/shard_map/all_gather | solution.py:33
  258.8 3.6 multiply_reduce_fusion.1
  262.5 14.4 %all_to_all.48 = f32[8,1,128]{2,1,0:T(1,128)S(1)} all-to-all(f32[8,1,128]{2,1,0:T(1,128)S(1)} %broadcast_in_dim.80), channel_id=1, replica_groups=mesh['pipe'=2,'tensor'=8,'seq_0'=8,'seq_1'=2] {'tensor'}, dimensions={0} | all-to-all | bytes 8192 | tf_op jit(solution)/shard_map/all_to_all | solution.py:50
  282.8 4.8 %all-to-all-start.5 = ((bf16[8,128,320]{1,2,0:T(8,128)(2,1)}), bf16[8,128,320]{1,2,0:T(8,128)(2,1)}, u32[]{:S(2)}, u32[]{:S(2)}) async-start(bf16[8,128,320]{1,2,0:T(8,128)(2,1)} %bitcast.495), calls=%async_computation.5 | async-start | bytes 1310720 | tf_op jit(solution)/shard_map/all_to_all | solution.py:78
  288.2 10.2 %all-to-all-done.5 = bf16[8,128,320]{1,2,0:T(8,128)(2,1)} async-done(((bf16[8,128,320]{1,2,0:T(8,128)(2,1)}), bf16[8,128,320]{1,2,0:T(8,128)(2,1)}, u32[]{:S(2)}, u32[]{:S(2)}) %all-to-all-start.5) | async-done | bytes 655392 | tf_op jit(solution)/shard_map/all_to_all | solution.py:78
  302.0 5.4 %collective-permute-done.3 = bf16[128,320]{0,1:T(8,128)(2,1)S(1)} collective-permute-done((bf16[128,320]{0,1:T(8,128)(2,1)S(1)}, bf16[128,320]{0,1:T(8,128)(2,1)S(1)}, u32[]{:S(2)}, u32[]{:S(2)}) %collective-permute-start.3) | collective-permute-done | bytes 81952 | tf_op jit(solution)/shard_map/ppermute | solution.py:18
  307.5 15.4 %all_to_all.49 = bf16[8,128,320]{1,2,0:T(8,128)(2,1)S(1)} all-to-all(bf16[8,128,320]{1,2,0:T(8,128)(2,1)S(1)} %broadcast_in_dim.83), channel_id=1, replica_groups=mesh['pipe'=2,'tensor'=8,'seq_0'=8,'seq_1'=2] {'tensor'}, dimensions={0} | all-to-all | bytes 1310720 | tf_op jit(solution)/shard_map/all_to_all | solution.py:50
  333.5 3.4 collective-permute-start.4
  352.7 4.8 %all-gather.5 = bf16[20,64,128]{2,1,0:T(8,128)(2,1)S(1)} all-gather(bf16[10,64,128]{2,1,0:T(8,128)(2,1)S(1)} %fusion.41), channel_id=7, replica_groups=mesh['pipe'=2,'tensor'=8,'seq_0'=8,'seq_1'=2] {'seq_1'}, dimensions={0}, use_global_device_ids=true | all-gather | bytes 491520 | tf_op jit(solution)/shard_map/all_gather | solution.py:33
  359.2 10.5 %all-gather.8 = bf16[8,1,10]{2,1,0:T(2,128)(2,1)S(1)} all-gather(bf16[1,1,10]{2,1,0:T(2,128)(2,1)S(1)} %multiply_convert_fusion.21), channel_id=1, replica_groups=mesh['pipe'=2,'tensor'=8,'seq_0'=8,'seq_1'=2] {'seq_0'}, dimensions={0}, use_global_device_ids=true | all-gather | bytes 180 | tf_op jit(solution)/shard_map/all_gather | solution.py:33
  375.3 17.2 %all-gather.17.cloned.1.call-done = bf16[8,10,64,128]{3,2,1,0:T(8,128)(2,1)} async-done(((bf16[1,10,64,128]{3,2,1,0:T(8,128)(2,1)}), bf16[8,10,64,128]{3,2,1,0:T(8,128)(2,1)}) %all-gather.17.cloned.1.call-update) | async-done | bytes 1310736 | tf_op jit(solution)/shard_map/all_gather | solution.py:33
  397.7 3.6 multiply_reduce_fusion
  401.4 14.5 %all_to_all.50 = f32[8,1,128]{2,1,0:T(1,128)S(1)} all-to-all(f32[8,1,128]{2,1,0:T(1,128)S(1)} %broadcast_in_dim.84), channel_id=1, replica_groups=mesh['pipe'=2,'tensor'=8,'seq_0'=8,'seq_1'=2] {'tensor'}, dimensions={0} | all-to-all | bytes 8192 | tf_op jit(solution)/shard_map/all_to_all | solution.py:50
  420.6 4.8 %all-to-all-start.8 = ((bf16[8,128,320]{1,2,0:T(8,128)(2,1)}), bf16[8,128,320]{1,2,0:T(8,128)(2,1)}, u32[]{:S(2)}, u32[]{:S(2)}) async-start(bf16[8,128,320]{1,2,0:T(8,128)(2,1)} %bitcast.494), calls=%async_computation.8 | async-start | bytes 1310720 | tf_op jit(solution)/shard_map/all_to_all | solution.py:78
  426.0 10.2 %all-to-all-done.8 = bf16[8,128,320]{1,2,0:T(8,128)(2,1)} async-done(((bf16[8,128,320]{1,2,0:T(8,128)(2,1)}), bf16[8,128,320]{1,2,0:T(8,128)(2,1)}, u32[]{:S(2)}, u32[]{:S(2)}) %all-to-all-start.8) | async-done | bytes 655392 | tf_op jit(solution)/shard_map/all_to_all | solution.py:78
  (293 shorter events, 161.0 us)
Async XLA Ops:
  6.5 123.7 %copy-start = (bf16[1,640,2560]{2,1,0:T(8,128)(2,1)S(1)}, bf16[1,640,2560]{2,1,0:T(8,128)(2,1)}, u32[]{:S(2)}) copy-start(bf16[1,640,2560]{2,1,0:T(8,128)(2,1)} %param.25) | copy-start | bytes 9830404
  8.9 5.5 %copy-start.37 = (f32[1,5,640]{2,0,1:T(1,128)S(1)}, f32[1,5,640]{2,0,1:T(1,128)}, u32[]{:S(2)}) copy-start(f32[1,5,640]{2,0,1:T(1,128)} %param.19) | copy-start | bytes 38404
  8.9 6.1 %copy-start.41 = (f32[1,5,256]{2,0,1:T(1,128)S(1)}, f32[1,5,256]{2,0,1:T(1,128)}, u32[]{:S(2)}) copy-start(f32[1,5,256]{2,0,1:T(1,128)} %param.20) | copy-start | bytes 15364
  8.9 23.2 %all-to-all-start = ((bf16[8,2,128,320]{2,3,1,0:T(8,128)(2,1)}), bf16[8,2,128,320]{2,3,1,0:T(8,128)(2,1)}, u32[]{:S(2)}, u32[]{:S(2)}) async-start(bf16[8,2,128,320]{2,3,1,0:T(8,128)(2,1)} %broadcast_in_dim.70), calls=%async_computation | async-start | bytes 2621440 | tf_op jit(solution)/shard_map/all_to_all | solution.py:50
  14.2 21.7 %copy-start.16 = (bf16[1,2560,10]{1,2,0:T(8,128)(2,1)S(1)}, bf16[1,2560,10]{1,2,0:T(8,128)(2,1)}, u32[]{:S(2)}) copy-start(bf16[1,2560,10]{1,2,0:T(8,128)(2,1)} %param.18) | copy-start | bytes 153604
  14.2 21.7 %copy-start.42 = (f32[1,10]{1,0:T(1,128)S(1)}, f32[1,10]{1,0:T(1,128)}, u32[]{:S(2)}) copy-start(f32[1,10]{1,0:T(1,128)} %param.21) | copy-start | bytes 124
  14.2 92.7 %all-gather.13.cloned.1.call-start = ((), (), s32[]{:S(2)}) async-start(), calls=%async_computation.9 | async-start | bytes 1474560 | tf_op jit(solution)/shard_map/all_gather | solution.py:33
  41.3 8.2 %copy-start.33 = (f32[1,128,10]{1,2,0:T(8,128)S(1)}, f32[1,128,10]{1,2,0:T(8,128)}, u32[]{:S(2)}) copy-start(f32[1,128,10]{1,2,0:T(8,128)} %copy.135) | copy-start | bytes 15364
  41.4 8.2 %copy-start.57 = (f32[10]{0:T(128)S(1)}, f32[10]{0:T(128)}, u32[]{:S(2)}) copy-start(f32[10]{0:T(128)} %get-tuple-element.89) | copy-start | bytes 124
  43.1 10.8 %collective-permute-start = (bf16[3,896]{1,0:T(4,128)(2,1)}, bf16[3,896]{1,0:T(4,128)(2,1)}, u32[]{:S(2)}, u32[]{:S(2)}) collective-permute-start(bf16[3,896]{1,0:T(4,128)(2,1)} %pad_maximum_fusion), channel_id=1, source_target_pairs={{0,1},{1,2},{2,3},{3,4},{4,5},{5,6},{6,7},{7,8},{8,9},{9,10},{10,1... | collective-permute-start | bytes 16136 | tf_op jit(solution)/shard_map/ppermute | solution.py:18
  58.2 9.6 %copy-start.51 = (f32[10]{0:T(128)S(1)}, f32[10]{0:T(128)}, u32[]{:S(2)}) copy-start(f32[10]{0:T(128)} %get-tuple-element.128) | copy-start | bytes 124
  58.2 9.6 %copy-start.58 = (f32[10]{0:T(128)S(1)}, f32[10]{0:T(128)}, u32[]{:S(2)}) copy-start(f32[10]{0:T(128)} %fusion.405) | copy-start | bytes 124
  112.3 13.4 %copy-start.48 = (f32[1,640]{1,0:T(1,128)S(1)}, f32[1,640]{1,0:T(1,128)}, u32[]{:S(2)}) copy-start(f32[1,640]{1,0:T(1,128)} %param.24) | copy-start | bytes 7684
  116.5 13.7 %all-to-all-start.1 = ((f32[8,1,128]{2,1,0:T(1,128)}), f32[8,1,128]{2,1,0:T(1,128)S(1)}, u32[]{:S(2)}, u32[]{:S(2)}) async-start(f32[8,1,128]{2,1,0:T(1,128)} %broadcast_in_dim.77), calls=%async_computation.1 | async-start | bytes 8192 | tf_op jit(solution)/shard_map/all_to_all | solution.py:50
  125.7 7.1 %copy-start.31 = (f32[640]{0:T(1024)}, f32[640]{0:T(1024)S(1)}, u32[]{:S(2)}) copy-start(f32[640]{0:T(1024)S(1)} %reduce.12) | copy-start | bytes 7684
  135.0 15.7 %all-to-all-start.2 = ((bf16[8,128,320]{1,2,0:T(8,128)(2,1)}), bf16[8,128,320]{1,2,0:T(8,128)(2,1)}, u32[]{:S(2)}, u32[]{:S(2)}) async-start(bf16[8,128,320]{1,2,0:T(8,128)(2,1)} %bitcast.493), calls=%async_computation.2 | async-start | bytes 1310720 | tf_op jit(solution)/shard_map/all_to_all | solution.py:78
  152.8 6.7 %collective-permute-start.1 = (bf16[128,320]{0,1:T(8,128)(2,1)S(1)}, bf16[128,320]{0,1:T(8,128)(2,1)S(1)}, u32[]{:S(2)}, u32[]{:S(2)}) collective-permute-start(bf16[128,320]{0,1:T(8,128)(2,1)S(1)} %get-tuple-element.71), channel_id=1, source_target_pairs={{0,128},{1,129},{2,130},{3,131},{4,132},{5,133},{6,134},{7,135},{8... | collective-permute-start | bytes 245768 | tf_op jit(solution)/shard_map/ppermute | solution.py:18
  160.4 17.1 %all-to-all-start.3 = ((bf16[8,128,320]{1,2,0:T(8,128)(2,1)}), bf16[8,128,320]{1,2,0:T(8,128)(2,1)}, u32[]{:S(2)}, u32[]{:S(2)}) async-start(bf16[8,128,320]{1,2,0:T(8,128)(2,1)} %broadcast_in_dim.79), calls=%async_computation.3 | async-start | bytes 1310720 | tf_op jit(solution)/shard_map/all_to_all | solution.py:50
  166.6 86.9 %all-gather.15.cloned.1.call-start = ((), (), s32[]{:S(2)}) async-start(), calls=%async_computation.10 | async-start | bytes 1474560 | tf_op jit(solution)/shard_map/all_gather | solution.py:33
  193.0 11.5 %collective-permute-start.2 = (bf16[3,896]{1,0:T(4,128)(2,1)}, bf16[3,896]{1,0:T(4,128)(2,1)}, u32[]{:S(2)}, u32[]{:S(2)}) collective-permute-start(bf16[3,896]{1,0:T(4,128)(2,1)} %pad_maximum_fusion.1), channel_id=1, source_target_pairs={{0,1},{1,2},{2,3},{3,4},{4,5},{5,6},{6,7},{7,8},{8,9},{9,10},{10,1... | collective-permute-start | bytes 16136 | tf_op jit(solution)/shard_map/ppermute | solution.py:18
  258.8 19.3 %copy-start.32 = (f32[640]{0:T(1024)S(1)}, f32[640]{0:T(1024)}, u32[]{:S(2)}) copy-start(f32[640]{0:T(1024)} %copy-done.31) | copy-start | bytes 7684
  282.8 15.7 %all-to-all-start.5 = ((bf16[8,128,320]{1,2,0:T(8,128)(2,1)}), bf16[8,128,320]{1,2,0:T(8,128)(2,1)}, u32[]{:S(2)}, u32[]{:S(2)}) async-start(bf16[8,128,320]{1,2,0:T(8,128)(2,1)} %bitcast.495), calls=%async_computation.5 | async-start | bytes 1310720 | tf_op jit(solution)/shard_map/all_to_all | solution.py:78
  287.6 104.9 %all-gather.17.cloned.1.call-start = ((), (), s32[]{:S(2)}) async-start(), calls=%async_computation.11 | async-start | bytes 1474560 | tf_op jit(solution)/shard_map/all_gather | solution.py:33
  300.7 6.7 %collective-permute-start.3 = (bf16[128,320]{0,1:T(8,128)(2,1)S(1)}, bf16[128,320]{0,1:T(8,128)(2,1)S(1)}, u32[]{:S(2)}, u32[]{:S(2)}) collective-permute-start(bf16[128,320]{0,1:T(8,128)(2,1)S(1)} %get-tuple-element.60), channel_id=1, source_target_pairs={{0,128},{1,129},{2,130},{3,131},{4,132},{5,133},{6,134},{7,135},{8... | collective-permute-start | bytes 245768 | tf_op jit(solution)/shard_map/ppermute | solution.py:18
  329.8 19.1 %copy-start.27 = (f32[640]{0:T(1024)S(1)}, f32[640]{0:T(1024)}, u32[]{:S(2)}) copy-start(f32[640]{0:T(1024)} %get-tuple-element.48) | copy-start | bytes 7684
  329.8 19.1 %copy-start.29 = (f32[640]{0:T(1024)S(1)}, f32[640]{0:T(1024)}, u32[]{:S(2)}) copy-start(f32[640]{0:T(1024)} %get-tuple-element.56) | copy-start | bytes 7684
  333.5 10.8 %collective-permute-start.4 = (bf16[3,896]{1,0:T(4,128)(2,1)}, bf16[3,896]{1,0:T(4,128)(2,1)}, u32[]{:S(2)}, u32[]{:S(2)}) collective-permute-start(bf16[3,896]{1,0:T(4,128)(2,1)} %pad_maximum_fusion.2), channel_id=1, source_target_pairs={{0,1},{1,2},{2,3},{3,4},{4,5},{5,6},{6,7},{7,8},{8,9},{9,10},{10,1... | collective-permute-start | bytes 16136 | tf_op jit(solution)/shard_map/ppermute | solution.py:18
  348.9 9.4 %copy-start.49 = (f32[10]{0:T(128)S(1)}, f32[10]{0:T(128)}, u32[]{:S(2)}) copy-start(f32[10]{0:T(128)} %get-tuple-element.124) | copy-start | bytes 124
  348.9 9.4 %copy-start.59 = (f32[10]{0:T(128)S(1)}, f32[10]{0:T(128)}, u32[]{:S(2)}) copy-start(f32[10]{0:T(128)} %fusion.407) | copy-start | bytes 124
  349.9 9.3 %copy-start.54 = (bf16[2,1,10]{2,1,0:T(2,128)(2,1)S(1)}, bf16[2,1,10]{2,1,0:T(2,128)(2,1)}, u32[]{:S(2)}) copy-start(bf16[2,1,10]{2,1,0:T(2,128)(2,1)} %copy-done.53) | copy-start | bytes 124
  351.6 40.9 %copy-start.50 = (f32[10]{0:T(128)S(1)}, f32[10]{0:T(128)}, u32[]{:S(2)}) copy-start(f32[10]{0:T(128)} %get-tuple-element.124) | copy-start | bytes 124
  420.6 15.7 %all-to-all-start.8 = ((bf16[8,128,320]{1,2,0:T(8,128)(2,1)}), bf16[8,128,320]{1,2,0:T(8,128)(2,1)}, u32[]{:S(2)}, u32[]{:S(2)}) async-start(bf16[8,128,320]{1,2,0:T(8,128)(2,1)} %bitcast.494), calls=%async_computation.8 | async-start | bytes 1310720 | tf_op jit(solution)/shard_map/all_to_all | solution.py:78
  (46 other events, 113.3 us)
Sparse Core Ops, SparseCore 0:
  68.8 38.0 all-gather.12
  220.1 33.2 all-gather.14
  359.3 33.1 all-gather.16
where the time goes:
time: 450 us; the launch traced here: 446 us
  waiting for transfers between devices  120 us (27%)
  blocking collectives  104 us (23%)
  local copies, waits for them, and re-layouts  62.3 us (14%)
  other arithmetic  53.4 us (12%)
  starting transfers between devices  47.8 us (11%)
  matrix products  44.3 us (10%)
  between operations  13.8 us (3%)
    all_gather x9, blocking collectives, entering_2(): lax.all_gather(part.astype(kind), axis)  59.7 us
    all_gather x3, waiting for transfers between devices, entering_2(): lax.all_gather(part.astype(kind), axis)  48.4 us
    all_to_all x3, blocking collectives, from_everyone(): lax.all_to_all(jnp.broadcast_to(array[None], (size, *array.shape)), axis,...  44.3 us
    all_to_all x3, waiting for transfers between devices, from_everyone(): lax.all_to_all(jnp.broadcast_to(array[None], (size, *array.shape)), axis,...  31.9 us
    all_to_all x3, waiting for transfers between devices, sent_and_summed(): lax.all_to_all(parts, axis, split_axis=0, concat_axis=0, tiled=True)  28.9 us
    all_to_all x3, starting transfers between devices, from_everyone(): lax.all_to_all(jnp.broadcast_to(array[None], (size, *array.shape)), axis,...  20.7 us
    all_to_all x3, starting transfers between devices, sent_and_summed(): lax.all_to_all(parts, axis, split_axis=0, concat_axis=0, tiled=True)  14.3 us
    ppermute x5, starting transfers between devices, shifted(): lax.ppermute(value, axis, [(source, source + steps) for source in range(f...  12.8 us
  transfers between devices with their start and end apart: 14, of which 11 were waited for; matrix products, arithmetic and copies ran while one was open for 9% of the time, Pallas kernels for 0%

commit v1 on v0

v1 whole, which is shorter than its diff:
```python
import jax
import jax.numpy as jnp
from jax import lax
from jax.sharding import Mesh
from jax.sharding import PartitionSpec as P

BLOCK = 128
INNER = 5120
EPS = 1e-05
SEQ = ("seq_0", "seq_1")
TENSOR = ("chip", "core")
SWAP = [(0, 1), (1, 0)]
F32 = jnp.float32
BF16 = jnp.bfloat16


def ring(size, steps):
    return [(source, (source + steps) % size) for source in range(size)]


def split_bf16(value, count):
    parts = []
    for _ in range(count):
        part = value.astype(BF16)
        parts.append(part)
        value = value - part.astype(F32)
    return parts


def causal_taps(rim, values, taps):
    width = taps.shape[0] - 1
    length = values.shape[1]
    padded = jnp.concatenate([rim, values], axis=1).astype(F32)
    total = taps[width]
    for index in range(width):
        total = total + taps[index] * padded[:, index : index + length]
    return jax.nn.silu(total).astype(BF16)


def gather_rows(piece):
    chip = lax.axis_index("chip")
    count = lax.axis_size("chip")
    pieces = jnp.stack(
        [piece] + [lax.ppermute(piece, "chip", ring(count, k)) for k in range(1, count)]
    )
    own = jnp.concatenate(
        [
            lax.dynamic_index_in_dim(pieces, lax.rem(chip - b + count, count), 0, keepdims=False)
            for b in range(count)
        ],
        axis=1,
    )
    other = lax.ppermute(own, "core", SWAP)
    return jnp.stack([own, other])


def exchange_states(states, decays):
    micros, rows, width = states.shape
    heads = decays.shape[1]
    head_rows = rows // heads
    members = lax.axis_size(SEQ)
    share = rows // members
    member = lax.axis_index(SEQ)
    first = [(s * share) // head_rows for s in range(members)]
    last = [(s * share + share - 1) // head_rows for s in range(members)]
    ends = jnp.stack(
        [
            jnp.stack([decays[:, h] for h in first]),
            jnp.stack([decays[:, h] for h in last]),
        ],
        axis=2,
    )
    ends = ends.reshape(members, micros * 2)
    high, low = split_bf16(ends, 2)
    extra = jnp.concatenate([high, low, high, low], axis=1)
    body = jnp.moveaxis(states.astype(BF16).reshape(micros, members, share, width), 0, 1)
    body = body.reshape(members, micros * share, width)
    sent = jnp.concatenate(
        [body, jnp.broadcast_to(extra[:, :, None], (*extra.shape, width))], axis=1
    )
    arrived = lax.all_to_all(sent, SEQ, 0, 0, tiled=True)
    ends = arrived[:, micros * share :].astype(F32)
    ends = ends[:, : 2 * micros] + ends[:, 2 * micros : 4 * micros]
    ends = ends.reshape(members, micros, 2, width)
    body = arrived[:, : micros * share].reshape(members, micros, share, width).astype(F32)
    row = member * share + lax.broadcasted_iota(jnp.int32, (share, width), 0)
    leading = row // head_rows == member * share // head_rows
    running = jnp.zeros((micros, share, width), F32)
    entering = []
    for s in range(members):
        entering.append(running.astype(BF16).reshape(micros * share, width))
        factor = jnp.where(leading, ends[s, :, 0:1], ends[s, :, 1:2])
        running = factor * running + body[s]
    back = lax.all_to_all(jnp.stack(entering), SEQ, 0, 0, tiled=True)
    back = jnp.moveaxis(back.reshape(members, micros, share, width), 1, 0)
    return back.reshape(micros, rows, width)


def layer(piece, weights):
    (
        prenorm,
        gate_weight,
        inner_weight,
        state_weight,
        step_weight,
        inner_taps,
        state_taps,
        step_bias,
        decay_rate,
        skip_scale,
        inner_gain,
        out_weight,
    ) = weights
    current = gather_rows(piece)
    micros, rows, _ = current.shape
    widened = current.astype(F32)
    normed_in = (
        widened * lax.rsqrt(jnp.mean(widened * widened, axis=2, keepdims=True) + EPS) * prenorm
    ).astype(BF16)
    inner_raw = jnp.dot(normed_in, inner_weight, preferred_element_type=F32).astype(BF16)
    state_raw = jnp.dot(normed_in, state_weight, preferred_element_type=F32).astype(BF16)
    reach = inner_taps.shape[0] - 2
    inner_width = inner_raw.shape[2]
    rim = lax.ppermute(
        jnp.concatenate([inner_raw[:, rows - reach :], state_raw[:, rows - reach :]], axis=2),
        SEQ,
        [(s, s + 1) for s in range(lax.axis_size(SEQ) - 1)],
    )
    step_raw = jnp.dot(normed_in, step_weight, preferred_element_type=F32)
    gate_raw = jnp.dot(normed_in, gate_weight, preferred_element_type=F32).astype(BF16)
    inner_conv = causal_taps(rim[:, :, :inner_width], inner_raw, inner_taps)
    state_conv = causal_taps(rim[:, :, inner_width:], state_raw, state_taps)
    heads = step_bias.shape[0]
    head_size = inner_width // heads
    state_size = state_raw.shape[2] // 2
    step_size = jax.nn.softplus(step_raw + step_bias)
    cumulative = jnp.cumsum(-step_size * decay_rate, axis=1)
    x = inner_conv.reshape(micros, rows, heads, head_size)
    b_map = state_conv[:, :, :state_size]
    c_map = state_conv[:, :, state_size:]
    weighting = jnp.exp(cumulative[:, -1:, :] - cumulative) * step_size
    weighted = (x.astype(F32) * weighting[..., None]).astype(BF16)
    states = jnp.einsum(
        "mrc,mrn->mcn", weighted.reshape(micros, rows, inner_width), b_map, preferred_element_type=F32
    )
    entering = exchange_states(states, jnp.exp(cumulative[:, -1, :]))
    scores = jnp.einsum("mqn,msn->mqs", c_map, b_map, preferred_element_type=F32)
    by_head = jnp.transpose(cumulative, (0, 2, 1))
    later = lax.broadcasted_iota(jnp.int32, (rows, rows), 0) >= lax.broadcasted_iota(
        jnp.int32, (rows, rows), 1
    )
    decay = jnp.exp(jnp.where(later, by_head[:, :, :, None] - by_head[:, :, None, :], -jnp.inf))
    mixing = (
        scores[:, None] * decay * jnp.transpose(step_size, (0, 2, 1))[:, :, None, :]
    ).astype(BF16)
    inside = jnp.einsum("mhqs,mshp->mqhp", mixing, x, preferred_element_type=F32)
    across = jnp.einsum("mqn,mcn->mqc", c_map, entering, preferred_element_type=F32)
    across = across.reshape(micros, rows, heads, head_size) * jnp.exp(cumulative)[..., None]
    mixed = inside + across + skip_scale[:, None] * x.astype(F32)
    gated = mixed.reshape(micros, rows, inner_width) * jax.nn.silu(gate_raw.astype(F32))
    squares = jnp.sum(gated * gated, axis=2)
    scaled = (gated * inner_gain).astype(BF16)
    term = jnp.dot(scaled, out_weight, preferred_element_type=F32).astype(BF16)
    return scatter_rows(piece, term, squares)


def with_squares(term, squares):
    rows, width = term.shape[-2:]
    row = jnp.concatenate(split_bf16(squares, 3))[None]
    row = jnp.pad(row, ((0, 7), (0, width - row.shape[1])))
    return jnp.concatenate([term, row], axis=0)


def from_squares(array, rows):
    row = array[rows].astype(F32)
    return array[:rows].astype(F32), row[:rows] + row[rows : 2 * rows] + row[2 * rows : 3 * rows]


def scatter_rows(piece, term, squares):
    chip = lax.axis_index("chip")
    count = lax.axis_size("chip")
    rows, width = piece.shape
    arrived = lax.ppermute(with_squares(term[1], squares[1]), "core", SWAP)
    other, other_squares = from_squares(arrived, rows)
    total = term[0].astype(F32) + other
    summed_squares = squares[0] + other_squares
    blocks = jnp.moveaxis(total.astype(BF16).reshape(rows, count, width), 1, 0)
    mine = lax.dynamic_index_in_dim(blocks, chip, 0, keepdims=False).astype(F32)
    all_squares = summed_squares
    for k in range(1, count):
        block = lax.dynamic_index_in_dim(blocks, lax.rem(chip + k, count), 0, keepdims=False)
        arrived = lax.ppermute(with_squares(block, summed_squares), "chip", ring(count, k))
        value, value_squares = from_squares(arrived, rows)
        mine = mine + value
        all_squares = all_squares + value_squares
    scale = lax.rsqrt(all_squares / INNER + EPS)
    return (piece.astype(F32) + scale[:, None] * mine).astype(BF16)


def shards(
    tokens,
    prenorm_gain,
    gate_weight,
    inner_weight,
    state_weight,
    step_weight,
    inner_taps,
    state_taps,
    step_bias,
    decay_rate,
    skip_scale,
    inner_gain,
    out_weight,
):
    weights = (
        prenorm_gain[0],
        gate_weight[0],
        inner_weight[0],
        state_weight[0],
        step_weight[0],
        inner_taps[0],
        state_taps[0],
        step_bias[0],
        decay_rate[0],
        skip_scale[0],
        inner_gain[0],
        out_weight[0],
    )
    sections = lax.axis_size("pipe")
    section = lax.axis_index("pipe")
    core = lax.axis_index("core")
    width = tokens.shape[2]
    mine = jnp.where(core == 0, tokens[0], tokens[1])
    given = lax.ppermute(jnp.where(core == 0, tokens[1], tokens[0]), "core", SWAP)
    piece = jnp.where(
        core == 0, jnp.concatenate([mine, given], 1), jnp.concatenate([given, mine], 1)
    )
    kept = None
    for turn in range(sections):
        own = layer(piece, weights)
        kept = own if turn == 0 else jnp.where(section == turn, own, kept)
        if turn + 1 < sections:
            piece = lax.ppermute(own, "pipe", [(s, s + 1) for s in range(sections - 1)])
    left, right = kept[:, :width], kept[:, width:]
    held = jnp.where(core == 0, left, right)
    given = lax.ppermute(jnp.where(core == 0, right, left), "core", SWAP)
    return jnp.where(core == 0, jnp.stack([held, given]), jnp.stack([given, held]))[None]


def solution(mesh):
    torus = Mesh(
        mesh.devices.reshape(mesh.shape["pipe"], mesh.shape["tensor"] // 2, 2, 8, 2),
        ("pipe", "chip", "core", "seq_0", "seq_1"),
    )
    return jax.shard_map(
        shards,
        mesh=torus,
        in_specs=(
            P(None, SEQ, TENSOR),
            P("pipe", None),
            P("pipe", None, TENSOR),
            P("pipe", None, TENSOR),
            P("pipe", None, None),
            P("pipe", None, TENSOR),
            P("pipe", None, TENSOR),
            P("pipe", None, None),
            P("pipe", TENSOR),
            P("pipe", TENSOR),
            P("pipe", TENSOR),
            P("pipe", TENSOR),
            P("pipe", TENSOR, None),
        ),
        out_specs=P("pipe", None, SEQ, TENSOR),
        check_vma=False,
    )
```

time: 450 us -> 274 us (0.61)
  blocking collectives: 104 us -> 0 us
  waiting for transfers between devices: 120 us -> 75.7 us
  matrix products: 44.3 us -> 26.4 us
  between operations: 13.8 us -> 1.23 us
  starting transfers between devices: 47.8 us -> 58.9 us
    all_gather x9 -> x0, blocking collectives: 59.7 us -> none  [entering_2(): lax.all_gather(part.astype(kind), axis)]
    all_gather x3 -> x0, waiting for transfers between devices: 48.4 us -> none  [entering_2(): lax.all_gather(part.astype(kind), axis)]
    all_to_all x3 -> x0, blocking collectives: 44.3 us -> none  [from_everyone(): lax.all_to_all(jnp.broadcast_to(array[None], (size, *array.shape)), axis,...]
    ppermute x5 -> x21, waiting for transfers between devices: 10.8 us -> 44 us  [the longest x6 17 us: scatter_rows(): lax.ppermute(with_squares(block, summed_squares), 'chip', ring(count, k))]
    all_to_all x6 -> x4, waiting for transfers between devices: 60.8 us -> 31.7 us  [the longest x2 25 us: exchange_states(): arrived = lax.all_to_all(sent, SEQ, 0, 0, tiled=True)]
    ppermute x5 -> x21, starting transfers between devices: 12.8 us -> 37.6 us  [the longest x6 8.76 us: gather_rows(): lax.ppermute(piece, 'chip', ring(count, k))]
    dot_general x27 -> x18, matrix products: 44.3 us -> 26.4 us  [the longest x2 7.65 us: layer(): jnp.dot(normed_in, gate_weight, preferred_element_type=F32).astype(BF16)]
    unnamed x2 -> x30, other arithmetic: 0.05 us -> 17.9 us
  transfers between devices with their start and end apart: 14 -> 25, of which waited for: 11 -> 21; matrix products, arithmetic and copies ran while one was open for 9% -> 11% of each run, Pallas kernels for 0% -> 0%
where the time goes in v1:
time: 274 us; the launch traced here: 272 us
  waiting for transfers between devices  75.7 us (28%)
  starting transfers between devices  58.9 us (21%)
  local copies, waits for them, and re-layouts  58.5 us (21%)
  other arithmetic  51.2 us (19%)
  matrix products  26.4 us (10%)
    all_to_all x2, waiting for transfers between devices, exchange_states(): arrived = lax.all_to_all(sent, SEQ, 0, 0, tiled=True)  25 us
    unnamed x30, other arithmetic  17.9 us
    ppermute x6, waiting for transfers between devices, scatter_rows(): lax.ppermute(with_squares(block, summed_squares), 'chip', ring(count, k))  17 us
    all_to_all x2, starting transfers between devices, exchange_states(): arrived = lax.all_to_all(sent, SEQ, 0, 0, tiled=True)  12.7 us
    ppermute x6, waiting for transfers between devices, gather_rows(): lax.ppermute(piece, 'chip', ring(count, k))  11.3 us
    ppermute x6, starting transfers between devices, gather_rows(): lax.ppermute(piece, 'chip', ring(count, k))  8.76 us
    all_to_all x2, starting transfers between devices, exchange_states(): back = lax.all_to_all(jnp.stack(entering), SEQ, 0, 0, tiled=True)  8.6 us
    ppermute x2, starting transfers between devices, scatter_rows(): arrived = lax.ppermute(with_squares(term[1], squares[1]), 'core', SWAP)  8.21 us
  transfers between devices with their start and end apart: 25, of which 21 were waited for; matrix products, arithmetic and copies ran while one was open for 11% of the time, Pallas kernels for 0%

profile of v1, /device:TPU:5, one launch (start us, length us, event | category | flops | bytes accessed | tf_op | source)
XLA Modules:
  0.0 271.9 jit_solution(10019839756853467746)
XLA Ops:
  6.1 2.6 collective-permute-start.2
  11.7 4.6 %collective-permute-done.2 = bf16[128,640]{1,0:T(8,128)(2,1)} collective-permute-done((bf16[128,640]{1,0:T(8,128)(2,1)S(1)}, bf16[128,640]{1,0:T(8,128)(2,1)}, u32[]{:S(2)}, u32[]{:S(2)}) %collective-permute-start.2) | collective-permute-done | bytes 163872 | tf_op jit(solution)/shard_map/ppermute | solution.py:44
  28.4 2.4 fusion.46
  31.4 2.4 fusion.28
  35.1 3.4 %collective-permute-start.5 = (bf16[2,3,896]{2,1,0:T(4,128)(2,1)}, bf16[2,3,896]{2,1,0:T(4,128)(2,1)}, u32[]{:S(2)}, u32[]{:S(2)}) collective-permute-start(bf16[2,3,896]{2,1,0:T(4,128)(2,1)} %pad_maximum_fusion.8), channel_id=1, source_target_pairs={{0,1},{1,2},{2,3},{3,4},{4,5},{5,6},{6,7},{7,8},{8,9},{9,10},{10,1... | collective-permute-start | bytes 32264 | tf_op jit(solution)/shard_map/ppermute | solution.py:124
  48.5 8.5 %all-to-all-start = ((bf16[16,96,128]{2,1,0:T(8,128)(2,1)}), bf16[16,96,128]{2,1,0:T(8,128)(2,1)}, u32[]{:S(2)}, u32[]{:S(2)}) async-start(bf16[16,96,128]{2,1,0:T(8,128)(2,1)} %pad_maximum_fusion.6), calls=%async_computation | async-start | bytes 786432 | tf_op jit(solution)/shard_map/all_to_all | solution.py:81
  57.8 12.2 %all-to-all-done = bf16[16,96,128]{2,1,0:T(8,128)(2,1)} async-done(((bf16[16,96,128]{2,1,0:T(8,128)(2,1)}), bf16[16,96,128]{2,1,0:T(8,128)(2,1)}, u32[]{:S(2)}, u32[]{:S(2)}) %all-to-all-start) | async-done | bytes 393248 | tf_op jit(solution)/shard_map/all_to_all | solution.py:81
  81.2 4.4 %all-to-all-start.1 = ((bf16[16,80,128]{2,1,0:T(8,128)(2,1)}), bf16[16,80,128]{2,1,0:T(8,128)(2,1)}, u32[]{:S(2)}, u32[]{:S(2)}) async-start(bf16[16,80,128]{2,1,0:T(8,128)(2,1)} %constant_dynamic-update-slice_fusion), calls=%async_computation.1 | async-start | bytes 655360 | tf_op jit(solution)/shard_map/all_to_all | solution.py:94
  93.2 2.6 all-to-all-done.1
  101.5 3.8 %multiply_reduce_fusion.1 = (f32[2,128]{1,0:T(2,128)S(1)}, f32[2,128,640]{2,1,0:T(8,128)S(1)}) fusion(f32[2,128,640]{2,1,0:T(8,128)} %copy.179, bf16[1,2560,640]{2,1,0:T(8,128)(2,1)} %param.15, f32[2560]{0:T(1024)S(1)} %copy-done.45, f32[2,128]{1,0:T(2,128)S(1)} %copy-done.56, bf16[1,128,2560]{2,1,0:T(8,128)(2,1)} %bitcast.11, ...), kind=kOutput, calls=%fused_computation.91 | convolution fusion | flops 843611904 | bytes 5910528 | tf_op jit(solution)/shard_map/dot_general | solution.py:130
  107.8 4.1 %collective-permute-start.6 = (bf16[136,2560]{1,0:T(8,128)(2,1)}, bf16[136,2560]{1,0:T(8,128)(2,1)}, u32[]{:S(2)}, u32[]{:S(2)}) collective-permute-start(bf16[136,2560]{1,0:T(8,128)(2,1)} %fusion.52), channel_id=1, source_target_pairs={{0,16},{16,0},{1,17},{17,1},{2,18},{18,2},{3,19},{19,3},{4,20},{20... | collective-permute-start | bytes 2088968 | tf_op jit(solution)/shard_map/ppermute | solution.py:183
  114.0 2.3 fusion.19
  116.3 2.4 reshape.6478
  118.7 3.3 %constant_dynamic-slice_fusion.4 = (bf16[128,1,640]{2,1,0:T(2,128)(2,1)S(1)}, bf16[128,1,640]{2,1,0:T(2,128)(2,1)S(1)}, bf16[128,1,640]{2,1,0:T(2,128)(2,1)S(1)}, bf16[128,1,640]{2,1,0:T(2,128)(2,1)S(1)}) fusion(bf16[128,4,640]{2,1,0:T(4,128)(2,1)} %reshape.6478, s32[]{:T(128)S(6)} %select_n.1405, s32[]{:T(128)S(6)} %select_n.1368, s32[]{:T(128)S(6)} %select_n.1369, ...), kind=kLoop, calls=%fused_computation.348 | loop fusion | bytes 1310736 | tf_op jit(solution)/shard_map/dynamic-slice.3
  123.0 2.4 collective-permute-start.8
  125.9 2.2 collective-permute-start.9
  130.2 4.4 %collective-permute-done.7 = bf16[136,640]{1,0:T(8,128)(2,1)S(1)} collective-permute-done((bf16[136,640]{1,0:T(8,128)(2,1)S(1)}, bf16[136,640]{1,0:T(8,128)(2,1)S(1)}, u32[]{:S(2)}, u32[]{:S(2)}) %collective-permute-start.7) | collective-permute-done | bytes 174112 | tf_op jit(solution)/shard_map/ppermute | solution.py:192
  136.1 7.3 %collective-permute-done.10 = bf16[128,640]{1,0:T(8,128)(2,1)S(1)} collective-permute-done((bf16[128,640]{1,0:T(8,128)(2,1)S(1)}, bf16[128,640]{1,0:T(8,128)(2,1)S(1)}, u32[]{:S(2)}, u32[]{:S(2)}) %collective-permute-start.10) | collective-permute-done | bytes 163872 | tf_op jit(solution)/shard_map/ppermute | solution.py:243
  148.9 3.0 %collective-permute-done.12 = bf16[128,640]{1,0:T(8,128)(2,1)S(1)} collective-permute-done((bf16[128,640]{1,0:T(8,128)(2,1)S(1)}, bf16[128,640]{1,0:T(8,128)(2,1)S(1)}, u32[]{:S(2)}, u32[]{:S(2)}) %collective-permute-start.12) | collective-permute-done | bytes 163872 | tf_op jit(solution)/shard_map/ppermute | solution.py:44
  153.4 2.6 collective-permute-start.14
  169.9 2.8 %collective-permute-start.15 = (bf16[2,3,896]{2,1,0:T(4,128)(2,1)}, bf16[2,3,896]{2,1,0:T(4,128)(2,1)}, u32[]{:S(2)}, u32[]{:S(2)}) collective-permute-start(bf16[2,3,896]{2,1,0:T(4,128)(2,1)} %pad_maximum_fusion.9), channel_id=1, source_target_pairs={{0,1},{1,2},{2,3},{3,4},{4,5},{5,6},{6,7},{7,8},{8,9},{9,10},{10,1... | collective-permute-start | bytes 32264 | tf_op jit(solution)/shard_map/ppermute | solution.py:124
  184.4 4.2 %all-to-all-start.2 = ((bf16[16,96,128]{2,1,0:T(8,128)(2,1)}), bf16[16,96,128]{2,1,0:T(8,128)(2,1)}, u32[]{:S(2)}, u32[]{:S(2)}) async-start(bf16[16,96,128]{2,1,0:T(8,128)(2,1)} %pad_maximum_fusion.7), calls=%async_computation.2 | async-start | bytes 786432 | tf_op jit(solution)/shard_map/all_to_all | solution.py:81
  189.2 12.8 %all-to-all-done.2 = bf16[16,96,128]{2,1,0:T(8,128)(2,1)} async-done(((bf16[16,96,128]{2,1,0:T(8,128)(2,1)}), bf16[16,96,128]{2,1,0:T(8,128)(2,1)}, u32[]{:S(2)}, u32[]{:S(2)}) %all-to-all-start.2) | async-done | bytes 393248 | tf_op jit(solution)/shard_map/all_to_all | solution.py:81
  213.3 4.2 %all-to-all-start.3 = ((bf16[16,80,128]{2,1,0:T(8,128)(2,1)}), bf16[16,80,128]{2,1,0:T(8,128)(2,1)}, u32[]{:S(2)}, u32[]{:S(2)}) async-start(bf16[16,80,128]{2,1,0:T(8,128)(2,1)} %constant_dynamic-update-slice_fusion.16), calls=%async_computation.3 | async-start | bytes 655360 | tf_op jit(solution)/shard_map/all_to_all | solution.py:94
  223.8 4.1 %all-to-all-done.3 = bf16[16,80,128]{2,1,0:T(8,128)(2,1)} async-done(((bf16[16,80,128]{2,1,0:T(8,128)(2,1)}), bf16[16,80,128]{2,1,0:T(8,128)(2,1)}, u32[]{:S(2)}, u32[]{:S(2)}) %all-to-all-start.3) | async-done | bytes 327712 | tf_op jit(solution)/shard_map/all_to_all | solution.py:94
  232.9 3.8 %multiply_reduce_fusion = (f32[2,128]{1,0:T(2,128)S(1)}, f32[2,128,640]{2,1,0:T(8,128)S(1)}) fusion(f32[2,128,640]{2,1,0:T(8,128)} %copy.229, bf16[1,2560,640]{2,1,0:T(8,128)(2,1)} %param.15, f32[2,128]{1,0:T(2,128)S(1)} %copy-done.58, f32[2560]{0:T(1024)S(1)} %copy-done.46, bf16[1,128,2560]{2,1,0:T(8,128)(2,1)} %bitcast.714, ...), kind=kOutput, calls=%fused_computation.82 | convolution fusion | flops 843611904 | bytes 5910528 | tf_op jit(solution)/shard_map/dot_general | solution.py:130
  238.1 4.1 %collective-permute-start.16 = (bf16[136,2560]{1,0:T(8,128)(2,1)S(1)}, bf16[136,2560]{1,0:T(8,128)(2,1)S(1)}, u32[]{:S(2)}, u32[]{:S(2)}) collective-permute-start(bf16[136,2560]{1,0:T(8,128)(2,1)S(1)} %fusion.53), channel_id=1, source_target_pairs={{0,16},{16,0},{1,17},{17,1},{2,18},{18,2},{3,19},{19,3},{4,20},{20... | collective-permute-start | bytes 2088968 | tf_op jit(solution)/shard_map/ppermute | solution.py:183
  245.9 2.4 reshape.6488
  248.2 4.0 %constant_dynamic-slice_fusion = (bf16[128,1,640]{2,1,0:T(2,128)(2,1)}, bf16[128,1,640]{2,1,0:T(2,128)(2,1)S(1)}, bf16[128,1,640]{2,1,0:T(2,128)(2,1)S(1)}, bf16[128,1,640]{2,1,0:T(2,128)(2,1)S(1)}) fusion(bf16[128,4,640]{2,1,0:T(4,128)(2,1)} %reshape.6488, s32[]{:T(128)S(6)} %select_n.1405, s32[]{:T(128)S(6)} %select_n.1368, s32[]{:T(128)S(6)} %select_n.1369, ...), kind=kLoop, calls=%fused_computation.344 | loop fusion | bytes 1310736 | tf_op jit(solution)/shard_map/dynamic-slice.7
  254.0 2.4 collective-permute-start.19
  257.0 3.8 %collective-permute-done.19 = bf16[136,640]{1,0:T(8,128)(2,1)} collective-permute-done((bf16[136,640]{1,0:T(8,128)(2,1)}, bf16[136,640]{1,0:T(8,128)(2,1)}, u32[]{:S(2)}, u32[]{:S(2)}) %collective-permute-start.19) | collective-permute-done | bytes 174112 | tf_op jit(solution)/shard_map/ppermute | solution.py:192
  263.5 4.7 %collective-permute-done.17 = bf16[136,640]{1,0:T(8,128)(2,1)S(1)} collective-permute-done((bf16[136,640]{1,0:T(8,128)(2,1)}, bf16[136,640]{1,0:T(8,128)(2,1)S(1)}, u32[]{:S(2)}, u32[]{:S(2)}) %collective-permute-start.17) | collective-permute-done | bytes 174112 | tf_op jit(solution)/shard_map/ppermute | solution.py:192
  (363 shorter events, 136.4 us)
Async XLA Ops:
  0.0 105.3 %copy-start = (bf16[1,640,2560]{2,1,0:T(8,128)(2,1)S(1)}, bf16[1,640,2560]{2,1,0:T(8,128)(2,1)}, u32[]{:S(2)}) copy-start(bf16[1,640,2560]{2,1,0:T(8,128)(2,1)} %param.25) | copy-start | bytes 9830404
  2.9 1.7 collective-permute-start
  4.7 12.8 %copy-start.13 = (bf16[128,640]{1,0:T(8,128)(2,1)}, bf16[128,640]{1,0:T(8,128)(2,1)S(1)}, u32[]{:S(2)}) copy-start(bf16[128,640]{1,0:T(8,128)(2,1)S(1)} %maximum_select_fusion.1) | copy-start | bytes 491524
  4.8 6.9 %collective-permute-start.1 = (bf16[128,640]{1,0:T(8,128)(2,1)S(1)}, bf16[128,640]{1,0:T(8,128)(2,1)}, u32[]{:S(2)}, u32[]{:S(2)}) collective-permute-start(bf16[128,640]{1,0:T(8,128)(2,1)S(1)} %maximum_select_fusion.1), channel_id=1, source_target_pairs={{0,32},{32,64},{64,96},{96,0},{1,33},{33,65},{65,97},{97,1},{2,34}... | collective-permute-start | bytes 491528 | tf_op jit(solution)/shard_map/ppermute | solution.py:44
  6.1 10.2 %collective-permute-start.2 = (bf16[128,640]{1,0:T(8,128)(2,1)S(1)}, bf16[128,640]{1,0:T(8,128)(2,1)}, u32[]{:S(2)}, u32[]{:S(2)}) collective-permute-start(bf16[128,640]{1,0:T(8,128)(2,1)S(1)} %maximum_select_fusion.1), channel_id=1, source_target_pairs={{0,64},{32,96},{64,0},{96,32},{1,65},{33,97},{65,1},{97,33},{2,66}... | collective-permute-start | bytes 491528 | tf_op jit(solution)/shard_map/ppermute | solution.py:44
  8.8 7.6 %collective-permute-start.3 = (bf16[128,640]{1,0:T(8,128)(2,1)S(1)}, bf16[128,640]{1,0:T(8,128)(2,1)}, u32[]{:S(2)}, u32[]{:S(2)}) collective-permute-start(bf16[128,640]{1,0:T(8,128)(2,1)S(1)} %maximum_select_fusion.1), channel_id=1, source_target_pairs={{0,96},{32,0},{64,32},{96,64},{1,97},{33,1},{65,33},{97,65},{2,98}... | collective-permute-start | bytes 491528 | tf_op jit(solution)/shard_map/ppermute | solution.py:44
  18.8 3.3 %collective-permute-start.4 = (bf16[128,2560]{1,0:T(8,128)(2,1)}, bf16[128,2560]{1,0:T(8,128)(2,1)}, u32[]{:S(2)}, u32[]{:S(2)}) collective-permute-start(bf16[128,2560]{1,0:T(8,128)(2,1)} %get-tuple-element.61), channel_id=1, source_target_pairs={{0,16},{16,0},{1,17},{17,1},{2,18},{18,2},{3,19},{19,3},{4,20},{20... | collective-permute-start | bytes 1966088 | tf_op jit(solution)/shard_map/ppermute | solution.py:53
  35.1 7.3 %collective-permute-start.5 = (bf16[2,3,896]{2,1,0:T(4,128)(2,1)}, bf16[2,3,896]{2,1,0:T(4,128)(2,1)}, u32[]{:S(2)}, u32[]{:S(2)}) collective-permute-start(bf16[2,3,896]{2,1,0:T(4,128)(2,1)} %pad_maximum_fusion.8), channel_id=1, source_target_pairs={{0,1},{1,2},{2,3},{3,4},{4,5},{5,6},{6,7},{7,8},{8,9},{9,10},{10,1... | collective-permute-start | bytes 32264 | tf_op jit(solution)/shard_map/ppermute | solution.py:124
  48.5 21.5 %all-to-all-start = ((bf16[16,96,128]{2,1,0:T(8,128)(2,1)}), bf16[16,96,128]{2,1,0:T(8,128)(2,1)}, u32[]{:S(2)}, u32[]{:S(2)}) async-start(bf16[16,96,128]{2,1,0:T(8,128)(2,1)} %pad_maximum_fusion.6), calls=%async_computation | async-start | bytes 786432 | tf_op jit(solution)/shard_map/all_to_all | solution.py:81
  81.2 14.6 %all-to-all-start.1 = ((bf16[16,80,128]{2,1,0:T(8,128)(2,1)}), bf16[16,80,128]{2,1,0:T(8,128)(2,1)}, u32[]{:S(2)}, u32[]{:S(2)}) async-start(bf16[16,80,128]{2,1,0:T(8,128)(2,1)} %constant_dynamic-update-slice_fusion), calls=%async_computation.1 | async-start | bytes 655360 | tf_op jit(solution)/shard_map/all_to_all | solution.py:94
  107.8 6.2 %collective-permute-start.6 = (bf16[136,2560]{1,0:T(8,128)(2,1)}, bf16[136,2560]{1,0:T(8,128)(2,1)}, u32[]{:S(2)}, u32[]{:S(2)}) collective-permute-start(bf16[136,2560]{1,0:T(8,128)(2,1)} %fusion.52), channel_id=1, source_target_pairs={{0,16},{16,0},{1,17},{17,1},{2,18},{18,2},{3,19},{19,3},{4,20},{20... | collective-permute-start | bytes 2088968 | tf_op jit(solution)/shard_map/ppermute | solution.py:183
  122.0 12.7 %copy-start.14 = (bf16[128,640]{1,0:T(8,128)(2,1)S(1)}, bf16[128,640]{1,0:T(8,128)(2,1)}, u32[]{:S(2)}) copy-start(bf16[128,640]{1,0:T(8,128)(2,1)} %copy-done.13) | copy-start | bytes 491524
  123.0 7.2 %collective-permute-start.8 = (bf16[136,640]{1,0:T(8,128)(2,1)S(1)}, bf16[136,640]{1,0:T(8,128)(2,1)S(1)}, u32[]{:S(2)}, u32[]{:S(2)}) collective-permute-start(bf16[136,640]{1,0:T(8,128)(2,1)S(1)} %get-tuple-element.171), channel_id=1, source_target_pairs={{0,64},{32,96},{64,0},{96,32},{1,65},{33,97},{65,1},{97,33},{2,66}... | collective-permute-start | bytes 522248 | tf_op jit(solution)/shard_map/ppermute | solution.py:192
  125.4 9.2 %collective-permute-start.7 = (bf16[136,640]{1,0:T(8,128)(2,1)S(1)}, bf16[136,640]{1,0:T(8,128)(2,1)S(1)}, u32[]{:S(2)}, u32[]{:S(2)}) collective-permute-start(bf16[136,640]{1,0:T(8,128)(2,1)S(1)} %get-tuple-element.170), channel_id=1, source_target_pairs={{0,32},{32,64},{64,96},{96,0},{1,33},{33,65},{65,97},{97,1},{2,34}... | collective-permute-start | bytes 522248 | tf_op jit(solution)/shard_map/ppermute | solution.py:192
  125.9 8.8 %collective-permute-start.9 = (bf16[136,640]{1,0:T(8,128)(2,1)S(1)}, bf16[136,640]{1,0:T(8,128)(2,1)S(1)}, u32[]{:S(2)}, u32[]{:S(2)}) collective-permute-start(bf16[136,640]{1,0:T(8,128)(2,1)S(1)} %get-tuple-element.172), channel_id=1, source_target_pairs={{0,96},{32,0},{64,32},{96,64},{1,97},{33,1},{65,33},{97,65},{2,98}... | collective-permute-start | bytes 522248 | tf_op jit(solution)/shard_map/ppermute | solution.py:192
  134.8 18.3 %copy-start.12 = (bf16[128,640]{1,0:T(8,128)(2,1)}, bf16[128,640]{1,0:T(8,128)(2,1)S(1)}, u32[]{:S(2)}) copy-start(bf16[128,640]{1,0:T(8,128)(2,1)S(1)} %fusion.89) | copy-start | bytes 491524
  134.8 8.6 %collective-permute-start.10 = (bf16[128,640]{1,0:T(8,128)(2,1)S(1)}, bf16[128,640]{1,0:T(8,128)(2,1)S(1)}, u32[]{:S(2)}, u32[]{:S(2)}) collective-permute-start(bf16[128,640]{1,0:T(8,128)(2,1)S(1)} %fusion.89), channel_id=1, source_target_pairs={{0,128},{1,129},{2,130},{3,131},{4,132},{5,133},{6,134},{7,135},{8... | collective-permute-start | bytes 491528 | tf_op jit(solution)/shard_map/ppermute | solution.py:243
  143.5 9.8 %copy-start.9 = (bf16[128,640]{1,0:T(8,128)(2,1)}, bf16[128,640]{1,0:T(8,128)(2,1)S(1)}, u32[]{:S(2)}) copy-start(bf16[128,640]{1,0:T(8,128)(2,1)S(1)} %collective-permute-done.10) | copy-start | bytes 491524
  143.5 5.4 %collective-permute-start.11 = (bf16[128,640]{1,0:T(8,128)(2,1)S(1)}, bf16[128,640]{1,0:T(8,128)(2,1)S(1)}, u32[]{:S(2)}, u32[]{:S(2)}) collective-permute-start(bf16[128,640]{1,0:T(8,128)(2,1)S(1)} %collective-permute-done.10), channel_id=1, source_target_pairs={{0,32},{32,64},{64,96},{96,0},{1,33},{33,65},{65,97},{97,1},{2,34}... | collective-permute-start | bytes 491528 | tf_op jit(solution)/shard_map/ppermute | solution.py:44
  144.8 7.1 %collective-permute-start.12 = (bf16[128,640]{1,0:T(8,128)(2,1)S(1)}, bf16[128,640]{1,0:T(8,128)(2,1)S(1)}, u32[]{:S(2)}, u32[]{:S(2)}) collective-permute-start(bf16[128,640]{1,0:T(8,128)(2,1)S(1)} %collective-permute-done.10), channel_id=1, source_target_pairs={{0,64},{32,96},{64,0},{96,32},{1,65},{33,97},{65,1},{97,33},{2,66}... | collective-permute-start | bytes 491528 | tf_op jit(solution)/shard_map/ppermute | solution.py:44
  146.1 7.0 %collective-permute-start.13 = (bf16[128,640]{1,0:T(8,128)(2,1)S(1)}, bf16[128,640]{1,0:T(8,128)(2,1)S(1)}, u32[]{:S(2)}, u32[]{:S(2)}) collective-permute-start(bf16[128,640]{1,0:T(8,128)(2,1)S(1)} %collective-permute-done.10), channel_id=1, source_target_pairs={{0,96},{32,0},{64,32},{96,64},{1,97},{33,1},{65,33},{97,65},{2,98}... | collective-permute-start | bytes 491528 | tf_op jit(solution)/shard_map/ppermute | solution.py:44
  153.4 4.3 %collective-permute-start.14 = (bf16[128,2560]{1,0:T(8,128)(2,1)S(1)}, bf16[128,2560]{1,0:T(8,128)(2,1)S(1)}, u32[]{:S(2)}, u32[]{:S(2)}) collective-permute-start(bf16[128,2560]{1,0:T(8,128)(2,1)S(1)} %get-tuple-element.51), channel_id=1, source_target_pairs={{0,16},{16,0},{1,17},{17,1},{2,18},{18,2},{3,19},{19,3},{4,20},{20... | collective-permute-start | bytes 1966088 | tf_op jit(solution)/shard_map/ppermute | solution.py:53
  163.5 16.4 %copy-start.21 = (bf16[2,128,256]{2,1,0:T(8,128)(2,1)S(1)}, bf16[2,128,256]{2,1,0:T(8,128)(2,1)}, u32[]{:S(2)}) copy-start(bf16[2,128,256]{2,1,0:T(8,128)(2,1)} %fusion.49) | copy-start | bytes 393220
  169.9 9.3 %collective-permute-start.15 = (bf16[2,3,896]{2,1,0:T(4,128)(2,1)}, bf16[2,3,896]{2,1,0:T(4,128)(2,1)}, u32[]{:S(2)}, u32[]{:S(2)}) collective-permute-start(bf16[2,3,896]{2,1,0:T(4,128)(2,1)} %pad_maximum_fusion.9), channel_id=1, source_target_pairs={{0,1},{1,2},{2,3},{3,4},{4,5},{5,6},{6,7},{7,8},{8,9},{9,10},{10,1... | collective-permute-start | bytes 32264 | tf_op jit(solution)/shard_map/ppermute | solution.py:124
  184.4 17.7 %all-to-all-start.2 = ((bf16[16,96,128]{2,1,0:T(8,128)(2,1)}), bf16[16,96,128]{2,1,0:T(8,128)(2,1)}, u32[]{:S(2)}, u32[]{:S(2)}) async-start(bf16[16,96,128]{2,1,0:T(8,128)(2,1)} %pad_maximum_fusion.7), calls=%async_computation.2 | async-start | bytes 786432 | tf_op jit(solution)/shard_map/all_to_all | solution.py:81
  213.3 14.6 %all-to-all-start.3 = ((bf16[16,80,128]{2,1,0:T(8,128)(2,1)}), bf16[16,80,128]{2,1,0:T(8,128)(2,1)}, u32[]{:S(2)}, u32[]{:S(2)}) async-start(bf16[16,80,128]{2,1,0:T(8,128)(2,1)} %constant_dynamic-update-slice_fusion.16), calls=%async_computation.3 | async-start | bytes 655360 | tf_op jit(solution)/shard_map/all_to_all | solution.py:94
  238.1 5.9 %collective-permute-start.16 = (bf16[136,2560]{1,0:T(8,128)(2,1)S(1)}, bf16[136,2560]{1,0:T(8,128)(2,1)S(1)}, u32[]{:S(2)}, u32[]{:S(2)}) collective-permute-start(bf16[136,2560]{1,0:T(8,128)(2,1)S(1)} %fusion.53), channel_id=1, source_target_pairs={{0,16},{16,0},{1,17},{17,1},{2,18},{18,2},{3,19},{19,3},{4,20},{20... | collective-permute-start | bytes 2088968 | tf_op jit(solution)/shard_map/ppermute | solution.py:183
  252.2 15.9 %copy-start.10 = (bf16[128,640]{1,0:T(8,128)(2,1)S(1)}, bf16[128,640]{1,0:T(8,128)(2,1)}, u32[]{:S(2)}) copy-start(bf16[128,640]{1,0:T(8,128)(2,1)} %copy-done.9) | copy-start | bytes 491524
  254.0 6.8 %collective-permute-start.19 = (bf16[136,640]{1,0:T(8,128)(2,1)}, bf16[136,640]{1,0:T(8,128)(2,1)}, u32[]{:S(2)}, u32[]{:S(2)}) collective-permute-start(bf16[136,640]{1,0:T(8,128)(2,1)} %get-tuple-element.169), channel_id=1, source_target_pairs={{0,96},{32,0},{64,32},{96,64},{1,97},{33,1},{65,33},{97,65},{2,98}... | collective-permute-start | bytes 522248 | tf_op jit(solution)/shard_map/ppermute | solution.py:192
  256.4 7.1 %collective-permute-start.18 = (bf16[136,640]{1,0:T(8,128)(2,1)}, bf16[136,640]{1,0:T(8,128)(2,1)S(1)}, u32[]{:S(2)}, u32[]{:S(2)}) collective-permute-start(bf16[136,640]{1,0:T(8,128)(2,1)} %get-tuple-element.168), channel_id=1, source_target_pairs={{0,64},{32,96},{64,0},{96,32},{1,65},{33,97},{65,1},{97,33},{2,66}... | collective-permute-start | bytes 522248 | tf_op jit(solution)/shard_map/ppermute | solution.py:192
  256.8 11.4 %collective-permute-start.17 = (bf16[136,640]{1,0:T(8,128)(2,1)}, bf16[136,640]{1,0:T(8,128)(2,1)S(1)}, u32[]{:S(2)}, u32[]{:S(2)}) collective-permute-start(bf16[136,640]{1,0:T(8,128)(2,1)} %get-tuple-element.167), channel_id=1, source_target_pairs={{0,32},{32,64},{64,96},{96,0},{1,33},{33,65},{65,97},{97,1},{2,34}... | collective-permute-start | bytes 522248 | tf_op jit(solution)/shard_map/ppermute | solution.py:192
  269.5 1.5 collective-permute-start.20
  (62 other events, 170.1 us)

commit v2 on v1

v2 whole, which is shorter than its diff:
```python
import jax
import jax.numpy as jnp
from jax import lax
from jax.experimental import pallas as pl
from jax.experimental.pallas import tpu as pltpu
from jax.sharding import Mesh
from jax.sharding import PartitionSpec as P

BLOCK = 128
INNER = 5120
EPS = 1e-05
EDGE = 8
SEQ = ("seq_0", "seq_1")
TENSOR = ("chip", "core")
SWAP = [(0, 1), (1, 0)]
F32 = jnp.float32
BF16 = jnp.bfloat16
VMEM = pl.BlockSpec(memory_space=pltpu.VMEM)
SMEM = pl.BlockSpec(memory_space=pltpu.SMEM)
HBM = pl.BlockSpec(memory_space=pltpu.MemorySpace.HBM)


def ring(size, steps):
    return [(source, (source + steps) % size) for source in range(size)]


def split_bf16(value, count):
    parts = []
    for _ in range(count):
        part = value.astype(BF16)
        parts.append(part)
        value = value - part.astype(F32)
    return parts


def local(body, args, outs, scalars=0, weights=0, scratch=(), mib=16, flops=1 << 28):
    first = len(args) - weights
    args = [
        pltpu.with_memory_space_constraint(arg, pltpu.MemorySpace.HBM) if index >= first else arg
        for index, arg in enumerate(args)
    ]
    return pl.pallas_call(
        body,
        out_shape=[jax.ShapeDtypeStruct(shape, kind) for shape, kind in outs],
        in_specs=[SMEM] * scalars + [VMEM] * (len(args) - scalars - weights) + [HBM] * weights,
        out_specs=[VMEM] * len(outs),
        cost_estimate=pl.CostEstimate(flops=flops, transcendentals=0, bytes_accessed=1 << 22),
        name=body.__name__,
        scratch_shapes=list(scratch),
        compiler_params=pltpu.CompilerParams(vmem_limit_bytes=mib << 20),
    )(*args)


def fetch(source, target, semaphores):
    parts = semaphores.shape[0]
    size = source.shape[0] // parts
    copies = [
        pltpu.make_async_copy(
            source.at[pl.ds(part * size, size)],
            target.at[pl.ds(part * size, size)],
            semaphores.at[part],
        )
        for part in range(parts)
    ]
    for copy in copies:
        copy.start()
    return copies


def room(weight, parts):
    return [pltpu.VMEM(weight.shape, weight.dtype), pltpu.SemaphoreType.DMA((parts,))]


def dot(a, b, dims=((1,), (0,))):
    return lax.dot_general(a, b, (dims, ((), ())), preferred_element_type=F32)


def sigmoid(value):
    return 1.0 / (1.0 + jnp.exp(-value))


def iota(shape, dim):
    return lax.broadcasted_iota(jnp.int32, shape, dim)


def spread(heads, width):
    size = width // heads
    lane, head = iota((heads, width), 1), iota((heads, width), 0)
    return jnp.where((lane >= head * size) & (lane < (head + 1) * size), 1.0, 0.0).astype(BF16)


def over_channels(value, picks):
    return sum(dot(part, picks) for part in split_bf16(value, 3))


def convolve(rim, values, taps):
    width = taps.shape[0] - 1
    length = values.shape[0]
    padded = jnp.concatenate([rim, values], axis=0).astype(F32)
    lead = rim.shape[0] - width + 1
    total = taps[width]
    for index in range(width):
        total = total + taps[index] * padded[lead + index : lead + index + length]
    return (total * sigmoid(total)).astype(BF16)


def enter(chip_ref, *refs):
    count = (len(refs) - 19) // 2
    sides = refs[:count], refs[count : 2 * count]
    gain, step_w, inner_taps, state_taps, bias, rate, state_hbm, inner_hbm = refs[2 * count :][:8]
    normed, x, maps, steps, sums, sent, tails = refs[2 * count + 8 :][:7]
    state_w, state_sems, inner_w, inner_sems = refs[2 * count + 15 :]
    state_copies = fetch(state_hbm, state_w, state_sems)
    inner_copies = fetch(inner_hbm, inner_w, inner_sems)
    chip = chip_ref[0]
    rows, width = x.shape[1:]
    block = gain.shape[2]
    edge = sides[0][0].shape[0] - rows
    heads = bias.shape[1]
    n = maps.shape[2] // 2
    for side, pieces in enumerate(sides):
        squares = jnp.zeros((rows + edge, 128), F32)
        for piece in pieces:
            value = piece[...].astype(F32)
            value = value * value
            for tile in range(block // 128):
                squares = squares + value[:, tile * 128 : (tile + 1) * 128]
        scale = lax.rsqrt(jnp.sum(squares, axis=1, keepdims=True) / (count * block) + EPS)
        for k, piece in enumerate(pieces):
            b = lax.rem(chip - k + count, count)
            value = piece[...].astype(F32) * scale * gain[b]
            normed[b, side * rows : (side + 1) * rows, :] = value[edge:].astype(BF16)
            tails[b, side * edge : (side + 1) * edge, :] = value[:edge]

    def times(weight, copies):
        main, tail = 0.0, 0.0
        for b in range(count):
            copies[b].wait()
            part = weight[b * block : (b + 1) * block, :]
            main = main + dot(normed[b], part)
            tail = tail + dot(tails[b].astype(BF16), part)
        return main, tail

    raw = jnp.zeros((2 * rows, heads), F32)
    for b in range(count):
        raw = raw + dot(normed[b], step_w[:, b * block : (b + 1) * block], ((1,), (1,)))
    raw = raw + bias[...]
    step_all = jnp.maximum(raw, 0.0) + jnp.log1p(jnp.exp(-jnp.abs(raw)))
    state, state_tail = times(state_w, state_copies)
    inner, inner_tail = times(inner_w, inner_copies)
    lower = (iota((rows, rows), 0) >= iota((rows, rows), 1)).astype(BF16)
    picks = spread(heads, width)
    for m in range(2):
        span = slice(m * rows, (m + 1) * rows)
        ends = slice(m * edge, (m + 1) * edge)
        xm = convolve(
            inner_tail[ends].astype(BF16).astype(F32),
            inner[span].astype(BF16).astype(F32),
            inner_taps,
        )
        sm = convolve(
            state_tail[ends].astype(BF16).astype(F32),
            state[span].astype(BF16).astype(F32),
            state_taps,
        )
        x[m] = xm
        maps[m] = sm
        step = step_all[span]
        total = -sum(dot(lower, part) for part in split_bf16(step * rate[...], 3))
        last = total[rows - 1 :]
        steps[m] = step
        sums[m] = total
        weighting = over_channels(jnp.exp(last - total) * step, picks)
        weighted = (xm.astype(F32) * weighting).astype(BF16)
        sent[span, :width] = dot(sm[:, :n], weighted, ((0,), (0,))).astype(BF16)
        high, low = split_bf16(jnp.exp(last), 2)
        row = iota((rows, heads), 0) % 16
        ends = jnp.where(row == 0, high.astype(F32), low.astype(F32))
        ends = jnp.concatenate([ends, jnp.zeros((rows, sent.shape[1] - width - heads), F32)], 1)
        sent[span, width:] = ends.astype(BF16)


def gate_project(normed, gate_hbm, gate, gate_w, gate_sems):
    count, _, width = normed.shape
    copies = fetch(gate_hbm, gate_w, gate_sems)
    total = jnp.zeros(gate.shape, F32)
    for block in range(count):
        copies[block].wait()
        total = total + dot(normed[block], gate_w[block * width : (block + 1) * width, :])
    gate[...] = (total.astype(BF16).astype(F32) * sigmoid(total.astype(BF16).astype(F32))).astype(
        gate.dtype
    )


def local_mixing(x, maps, steps, sums, gate, skip, base, ahead):
    micros, rows, width = x.shape
    heads = skip.shape[1]
    size = width // heads
    pair = 128 // size
    n = maps.shape[2] // 2
    picks = spread(heads, width)
    skips = over_channels(jnp.broadcast_to(skip[...], (8, heads)), picks)[:1]
    later = iota((rows, rows), 0) >= iota((rows, rows), 1)
    lane = iota((rows, pair * size), 1)
    for m in range(micros):
        maps_m, sums_m, steps_m = maps[m], sums[m], steps[m]
        scores = dot(maps_m[:, n:], maps_m[:, :n], ((1,), (1,)))
        fill = jnp.zeros((rows, 128 - heads), F32)
        sums_t = jnp.transpose(jnp.concatenate([sums_m, fill], 1))
        steps_t = jnp.transpose(jnp.concatenate([steps_m, fill], 1))
        for g in range(heads // pair):
            span = slice(g * pair * size, (g + 1) * pair * size)
            xg = x[m, :, span]
            left, right = [], []
            for j in range(pair):
                h = g * pair + j
                gap = sums_m[:, h : h + 1] - sums_t[h : h + 1, :]
                decay = jnp.exp(jnp.where(later, gap, -jnp.inf))
                left.append((scores * decay * steps_t[h : h + 1, :]).astype(BF16))
                right.append(
                    jnp.where((lane >= j * size) & (lane < (j + 1) * size), xg, jnp.zeros_like(xg))
                )
            inside = dot(jnp.concatenate(left, 1), jnp.concatenate(right, 0))
            silu = gate[m * rows : (m + 1) * rows, span]
            base[m, :, span] = (inside + skips[:, span] * xg.astype(F32)) * silu
        ahead[m] = over_channels(jnp.exp(sums_m), picks) * gate[m * rows : (m + 1) * rows]


def scan_states(arrived, back, heads=10):
    members, rows, width = back.shape
    picks = spread(128, 128 * (width // heads))[:, :width]
    ends = arrived[:, :, width:].reshape(members * rows, arrived.shape[2] - width)
    factors = dot(ends, picks)
    running = jnp.zeros((rows, width), F32)
    for s in range(members):
        back[s] = running.astype(BF16)
        factor = factors[s * rows : s * rows + 1] + factors[s * rows + 1 : s * rows + 2]
        running = running * factor + arrived[s, :, :width].astype(F32)


def squares_rows(squares):
    rows = squares.shape[0]
    lane = iota((rows, 128), 1)
    block = jnp.zeros((rows, 128), F32)
    for index, part in enumerate(split_bf16(squares, 3)):
        block = jnp.where(lane == index, part.astype(F32), block)
    return jnp.transpose(block)[:8]


def output_term(m, base, ahead, maps, entering, gain, out_hbm, term, out_w, out_sems):
    n = maps.shape[2] // 2
    count, tall, width = term.shape
    (copy,) = fetch(out_hbm, out_w, out_sems)
    rows = base.shape[1]
    across = dot(maps[m, :, n:], entering[m])
    gated = base[m] + across * ahead[m]
    squares = jnp.sum(gated * gated, axis=1, keepdims=True)
    scaled = (gated * gain[...]).astype(BF16)
    block = squares_rows(squares)
    block = jnp.concatenate([block, jnp.zeros((8, width - 128), F32)], 1).astype(term.dtype)
    copy.wait()
    for b in range(count):
        value = dot(scaled, out_w[:, b * width : (b + 1) * width])
        term[b, :rows] = value.astype(term.dtype)
        term[b, rows:] = block


def other_term(*refs):
    output_term(1, *refs)


def own_term(*refs):
    output_term(0, *refs)


def merge_cores(chip_ref, mine, arrived, kept, *sent):
    count, tall, width = mine.shape
    rows = tall - 8
    chip = chip_ref[0]
    kept[:rows] = mine[chip, :rows] + arrived[chip, :rows].astype(F32)
    both = jnp.sum(mine[0, rows:] + arrived[0, rows:].astype(F32), axis=0, keepdims=True)
    row = iota((8, width), 0)
    kept[rows:] = jnp.where(row == 0, both, 0.0)
    block = jnp.zeros((8, width), F32)
    for index, part in enumerate(split_bf16(both, 3)):
        block = jnp.where(row == index, part.astype(F32), block)
    for k in range(1, count):
        b = lax.rem(chip + k, count)
        sent[k - 1][:rows] = (mine[b, :rows] + arrived[b, :rows].astype(F32)).astype(BF16)
        sent[k - 1][rows:] = block.astype(BF16)


def finish(piece, kept, *refs):
    arrived, result = refs[:-1], refs[-1]
    rows = piece.shape[0]
    total = kept[:rows]
    squares = kept[rows:, :128]
    for part in arrived:
        total = total + part[:rows].astype(F32)
        squares = squares + part[rows:, :128].astype(F32)
    squares = jnp.broadcast_to(jnp.sum(squares, axis=0, keepdims=True), (rows, 128))
    scale = lax.rsqrt(jnp.transpose(squares) / INNER + EPS)
    for tile in range(piece.shape[1] // 128):
        span = slice(tile * 128, (tile + 1) * 128)
        result[:, span] = (piece[:, span].astype(F32) + scale * total[:, span]).astype(BF16)


def layer(piece, edge, weights):
    (
        prenorm,
        gate_weight,
        inner_weight,
        state_weight,
        step_weight,
        inner_taps,
        state_taps,
        step_bias,
        decay_rate,
        skip_scale,
        inner_gain,
        out_weight,
    ) = weights
    chip = lax.axis_index("chip").reshape(1)
    count = lax.axis_size("chip")
    members = lax.axis_size(SEQ)
    rows, block = piece.shape
    tall = 2 * rows
    width = inner_weight.shape[1]
    maps_width = state_weight.shape[1]
    heads = step_weight.shape[1]
    spread_rows = jnp.concatenate([edge, piece], axis=0)
    own = [spread_rows] + [
        lax.ppermute(spread_rows, "chip", ring(count, k)) for k in range(1, count)
    ]
    other = [lax.ppermute(part, "core", SWAP) for part in own]
    normed, x, maps, steps, sums, sent = local(
        enter,
        [
            chip,
            *own,
            *other,
            prenorm.reshape(count, 1, block),
            step_weight.T,
            inner_taps[:, None],
            state_taps[:, None],
            step_bias[None],
            decay_rate[None],
            state_weight,
            inner_weight,
        ],
        [
            ((count, tall, block), BF16),
            ((2, rows, width), BF16),
            ((2, rows, maps_width), BF16),
            ((2, rows, heads), F32),
            ((2, rows, heads), F32),
            ((tall, width + 128), BF16),
        ],
        scalars=1,
        weights=2,
        scratch=[
            pltpu.VMEM((count, 2 * edge.shape[0], block), F32),
            *room(state_weight, count),
            *room(inner_weight, count),
        ],
    )
    with jax.named_scope("forth"):
        arrived = lax.all_to_all(
            sent.reshape(members, tall // members, -1), SEQ, 0, 0, tiled=True
        )
    (gate,) = local(
        gate_project,
        [normed, gate_weight],
        [((tall, width), F32)],
        weights=1,
        scratch=room(gate_weight, count),
    )
    base, ahead = local(
        local_mixing,
        [x, maps, steps, sums, gate, skip_scale[None]],
        [((2, rows, width), F32), ((2, rows, width), F32)],
    )
    (back,) = local(scan_states, [arrived], [((members, tall // members, width), BF16)])
    back = lax.all_to_all(back, SEQ, 0, 0, tiled=True)
    entering = back.reshape(2, rows, width)
    common = [base, ahead, maps, entering, inner_gain[None], out_weight]
    (given,) = local(
        other_term, common, [((count, rows + 8, block), BF16)], weights=1, scratch=room(out_weight, 1)
    )
    taken = lax.ppermute(given, "core", SWAP)
    (mine,) = local(
        own_term, common, [((count, rows + 8, block), F32)], weights=1, scratch=room(out_weight, 1)
    )
    kept, *leaving = local(
        merge_cores,
        [chip, mine, taken],
        [((rows + 8, block), F32)] + [((rows + 8, block), BF16)] * (count - 1),
        scalars=1,
    )
    parts = [lax.ppermute(part, "chip", ring(count, k + 1)) for k, part in enumerate(leaving)]
    return local(finish, [piece, kept, *parts], [((rows, block), BF16)])[0]


def shards(
    tokens,
    prenorm_gain,
    gate_weight,
    inner_weight,
    state_weight,
    step_weight,
    inner_taps,
    state_taps,
    step_bias,
    decay_rate,
    skip_scale,
    inner_gain,
    out_weight,
):
    weights = (
        prenorm_gain[0],
        gate_weight[0],
        inner_weight[0],
        state_weight[0],
        step_weight[0],
        inner_taps[0],
        state_taps[0],
        step_bias[0],
        decay_rate[0],
        skip_scale[0],
        inner_gain[0],
        out_weight[0],
    )
    sections = lax.axis_size("pipe")
    section = lax.axis_index("pipe")
    core = lax.axis_index("core")
    width = tokens.shape[2]
    members = lax.axis_size(SEQ)
    mine = jnp.where(core == 0, tokens[0], tokens[1])
    theirs = jnp.where(core == 0, tokens[1], tokens[0])
    given = lax.ppermute(theirs, "core", SWAP)
    mine_edge = lax.ppermute(mine[-EDGE:], SEQ, [(s, s + 1) for s in range(members - 1)])
    given_edge = lax.ppermute(
        theirs[-EDGE:],
        ("core", *SEQ),
        [
            (c * members + s, (1 - c) * members + s + 1)
            for c in range(2)
            for s in range(members - 1)
        ],
    )

    def joined(left, right):
        return jnp.where(
            core == 0, jnp.concatenate([left, right], 1), jnp.concatenate([right, left], 1)
        )

    piece, edge = joined(mine, given), joined(mine_edge, given_edge)
    kept = None
    for turn in range(sections):
        own = layer(piece, edge, weights)
        kept = own if turn == 0 else jnp.where(section == turn, own, kept)
        if turn + 1 < sections:
            piece = lax.ppermute(own, "pipe", [(s, s + 1) for s in range(sections - 1)])
            edge = lax.ppermute(
                own[-EDGE:],
                ("pipe", *SEQ),
                [
                    (p * members + s, (p + 1) * members + s + 1)
                    for p in range(sections - 1)
                    for s in range(members - 1)
                ],
            )
    left, right = kept[:, :width], kept[:, width:]
    held = jnp.where(core == 0, left, right)
    given = lax.ppermute(jnp.where(core == 0, right, left), "core", SWAP)
    return jnp.where(core == 0, jnp.stack([held, given]), jnp.stack([given, held]))[None]


def solution(mesh):
    torus = Mesh(
        mesh.devices.reshape(mesh.shape["pipe"], mesh.shape["tensor"] // 2, 2, 8, 2),
        ("pipe", "chip", "core", "seq_0", "seq_1"),
    )
    return jax.shard_map(
        shards,
        mesh=torus,
        in_specs=(
            P(None, SEQ, TENSOR),
            P("pipe", None),
            P("pipe", None, TENSOR),
            P("pipe", None, TENSOR),
            P("pipe", None, None),
            P("pipe", None, TENSOR),
            P("pipe", None, TENSOR),
            P("pipe", None, None),
            P("pipe", TENSOR),
            P("pipe", TENSOR),
            P("pipe", TENSOR),
            P("pipe", TENSOR),
            P("pipe", TENSOR, None),
        ),
        out_specs=P("pipe", None, SEQ, TENSOR),
        check_vma=False,
    )
```

time: 274 us -> 183 us (0.67)
  local copies, waits for them, and re-layouts: 58.5 us -> 3.77 us
  other arithmetic: 51.2 us -> 0.43 us
  blocking collectives: 0 us -> 39.7 us
  Pallas kernels: 0 us -> 36.1 us
  matrix products: 26.4 us -> 0 us
  waiting for transfers between devices: 75.7 us -> 53.7 us
  starting transfers between devices: 58.9 us -> 48.2 us
    all_to_all x0 -> x2, blocking collectives: none -> 39.7 us  [layer(): lax.all_to_all(sent.reshape(members, tall // members, -1), SEQ, 0, 0, til...]
    pallas_call x0 -> x16, Pallas kernels: none -> 36.1 us  [local(): pl.pallas_call(body, out_shape=[jax.ShapeDtypeStruct(shape, kind) for sha...]
    dot_general x18 -> x0, matrix products: 26.4 us -> none  [the longest x2 7.65 us: layer(): jnp.dot(normed_in, gate_weight, preferred_element_type=F32).astype(BF16)]
    unnamed x30 -> x0, other arithmetic: 17.9 us -> none
    all_to_all x4 -> x2, waiting for transfers between devices: 31.7 us -> 14.1 us  [layer(): back = lax.all_to_all(back, SEQ, 0, 0, tiled=True)]
    convert_element_type x31 -> x0, other arithmetic: 13.3 us -> none  [the longest x2 3.28 us: scatter_rows(): blocks = jnp.moveaxis(total.astype(BF16).reshape(rows, count, width), 1, 0)]
    another operation x12 -> x0, local copies, waits for them, and re-layouts: 13.2 us -> none
    all_to_all x4 -> x2, starting transfers between devices: 21.3 us -> 8.25 us  [layer(): back = lax.all_to_all(back, SEQ, 0, 0, tiled=True)]
  transfers between devices with their start and end apart: 25 -> 30, of which waited for: 21 -> 16; matrix products, arithmetic and copies ran while one was open for 11% -> 0% of each run, Pallas kernels for 0% -> 8%
where the time goes in v2:
time: 183 us; the launch traced here: 182 us
  waiting for transfers between devices  53.7 us (29%)
  starting transfers between devices  48.2 us (26%)
  blocking collectives  39.7 us (22%)
  Pallas kernels  36.1 us (20%)
  local copies, waits for them, and re-layouts  3.77 us (2%)
    all_to_all x2, blocking collectives, layer(): lax.all_to_all(sent.reshape(members, tall // members, -1), SEQ, 0, 0, til...  39.7 us
    pallas_call x16, Pallas kernels, local(): pl.pallas_call(body, out_shape=[jax.ShapeDtypeStruct(shape, kind) for sha...  36.1 us
    ppermute x6, waiting for transfers between devices, layer(): lax.ppermute(part, 'chip', ring(count, k + 1))  17.1 us
    all_to_all x2, waiting for transfers between devices, layer(): back = lax.all_to_all(back, SEQ, 0, 0, tiled=True)  14.1 us
    ppermute x6, waiting for transfers between devices, layer(): lax.ppermute(spread_rows, 'chip', ring(count, k))  12.3 us
    ppermute x8, starting transfers between devices, layer(): other = [lax.ppermute(part, 'core', SWAP) for part in own]  10.1 us
    all_to_all x2, starting transfers between devices, layer(): back = lax.all_to_all(back, SEQ, 0, 0, tiled=True)  8.25 us
    ppermute x6, starting transfers between devices, layer(): lax.ppermute(spread_rows, 'chip', ring(count, k))  7.4 us
  transfers between devices with their start and end apart: 30, of which 16 were waited for; matrix products, arithmetic and copies ran while one was open for 0% of the time, Pallas kernels for 8%

profile of v2, /device:TPU:5, one launch (start us, length us, event | category | flops | bytes accessed | tf_op | source)
XLA Modules:
  0.0 182.4 jit_solution(12537978782755324135)
XLA Ops:
  1.4 3.4 %collective-permute-start.2 = (bf16[8,320]{1,0:T(8,128)(2,1)S(1)}, bf16[8,320]{1,0:T(8,128)(2,1)S(1)}, u32[]{:S(2)}, u32[]{:S(2)}) collective-permute-start(bf16[8,320]{1,0:T(8,128)(2,1)S(1)} %slice_bitcast_fusion), channel_id=1, source_target_pairs={{0,17},{1,18},{2,19},{3,20},{4,21},{5,22},{6,23},{7,24},{8,25},{9,... | collective-permute-start | bytes 15368 | tf_op jit(solution)/shard_map/ppermute | solution.py:442
  4.8 3.8 %collective-permute-start.1 = (bf16[8,320]{1,0:T(8,128)(2,1)S(1)}, bf16[8,320]{1,0:T(8,128)(2,1)S(1)}, u32[]{:S(2)}, u32[]{:S(2)}) collective-permute-start(bf16[8,320]{1,0:T(8,128)(2,1)S(1)} %slice_bitcast_fusion.1), channel_id=1, source_target_pairs={{0,1},{1,2},{2,3},{3,4},{4,5},{5,6},{6,7},{7,8},{8,9},{9,10},{10,1... | collective-permute-start | bytes 15368 | tf_op jit(solution)/shard_map/ppermute | solution.py:441
  10.1 2.8 %collective-permute-start.5 = (bf16[136,640]{1,0:T(8,128)(2,1)S(1)}, bf16[136,640]{1,0:T(8,128)(2,1)S(1)}, u32[]{:S(2)}, u32[]{:S(2)}) collective-permute-start(bf16[136,640]{1,0:T(8,128)(2,1)S(1)} %pad_maximum_fusion.refs_0_), channel_id=1, source_target_pairs={{0,96},{32,0},{64,32},{96,64},{1,97},{33,1},{65,33},{97,65},{2,98}... | collective-permute-start | bytes 522248 | tf_op jit(solution)/shard_map/ppermute | solution.py:333
  15.0 5.2 %collective-permute-done.5.refs_3_ = bf16[136,640]{1,0:T(8,128)(2,1)S(1)} collective-permute-done((bf16[136,640]{1,0:T(8,128)(2,1)S(1)}, bf16[136,640]{1,0:T(8,128)(2,1)S(1)}, u32[]{:S(2)}, u32[]{:S(2)}) %collective-permute-start.5) | collective-permute-done | bytes 174112 | tf_op jit(solution)/shard_map/ppermute | solution.py:333
  22.2 2.3 %collective-permute-done.3.refs_1_ = bf16[136,640]{1,0:T(8,128)(2,1)S(1)} collective-permute-done((bf16[136,640]{1,0:T(8,128)(2,1)S(1)}, bf16[136,640]{1,0:T(8,128)(2,1)S(1)}, u32[]{:S(2)}, u32[]{:S(2)}) %collective-permute-start.3) | collective-permute-done | bytes 174112 | tf_op jit(solution)/shard_map/ppermute | solution.py:333
  27.7 6.8 %enter.2 = (bf16[4,256,640]{2,1,0:T(8,128)(2,1)S(1)}, bf16[2,128,640]{2,1,0:T(8,128)(2,1)S(1)}, bf16[2,128,256]{2,1,0:T(8,128)(2,1)S(1)}, f32[2,128,10]{2,1,0:T(...) custom-call(s32[1]{0:T(128)} %bitcast.2.chip_ref, bf16[136,640]{1,0:T(8,128)(2,1)S(1)} %pad_maximum_fusion.refs_0_, ...), custom_call_target="tpu_custom_call" | custom-call | flops 268435456 | bytes 4194304 | tf_op jit(solution)/shard_map/enter/pallas_call | solution.py:42
  34.5 23.0 %all_to_all.20.arrived = bf16[16,16,768]{2,1,0:T(8,128)(2,1)S(1)} all-to-all(bf16[16,16,768]{2,1,0:T(8,128)(2,1)S(1)} %bitcast.28), channel_id=1, replica_groups=mesh['pipe'=2,'chip'=4,'core'=2,'seq_0'=8,'seq_1'=2] {'seq_0','seq_1'}, dimensions={0} | all-to-all | bytes 786432 | tf_op jit(solution)/shard_map/forth/all_to_all | solution.py:368
  58.5 4.1 %all-to-all-start.1 = ((bf16[16,16,640]{2,1,0:T(8,128)(2,1)}), bf16[16,16,640]{2,1,0:T(8,128)(2,1)S(1)}, u32[]{:S(2)}, u32[]{:S(2)}) async-start(bf16[16,16,640]{2,1,0:T(8,128)(2,1)} %scan_states.2), calls=%async_computation.1 | async-start | bytes 655360 | tf_op jit(solution)/shard_map/all_to_all | solution.py:384
  62.6 3.2 %gate_project.2.gate = f32[256,640]{1,0:T(8,128)S(1)} custom-call(bf16[4,256,640]{2,1,0:T(8,128)(2,1)S(1)} %get-tuple-element.33.normed, bf16[2560,640]{1,0:T(8,128)(2,1)} %bitcast.42), custom_call_target="tpu_custom_call" | custom-call | flops 268435456 | bytes 4194304 | tf_op jit(solution)/shard_map/gate_project/pallas_call | solution.py:42
  66.8 7.0 %all-to-all-done.1 = bf16[16,16,640]{2,1,0:T(8,128)(2,1)S(1)} async-done(((bf16[16,16,640]{2,1,0:T(8,128)(2,1)}), bf16[16,16,640]{2,1,0:T(8,128)(2,1)S(1)}, u32[]{:S(2)}, u32[]{:S(2)}) %all-to-all-start.1) | async-done | bytes 327712 | tf_op jit(solution)/shard_map/all_to_all | solution.py:384
  73.8 2.9 %other_term.2 = bf16[4,136,640]{2,1,0:T(8,128)(2,1)S(1)} custom-call(f32[2,128,640]{2,1,0:T(8,128)S(1)} %get-tuple-element.34.refs_0_, f32[2,128,640]{2,1,0:T(8,128)S(1)} %get-tuple-element.35.refs_1_, bf16[2,128,256]{2,1,0:T(8,128)(2,1)S(1)} %get-tuple-element.30.maps.refs_2_, bf16[2,128,640]{2,1,0:T(8,128)(2,1)S(1)} %bitcast.24, f32[1,640]{1,0:T(1,128)S(1)} %copy-done.9, ...), custom_call_target="tpu_custom_call" | custom-call | flops 268435456 | bytes 4194304 | tf_op jit(solution)/shard_map/other_term/pallas_call | solution.py:42
  76.7 3.2 %collective-permute-start.10 = (bf16[4,136,640]{2,1,0:T(8,128)(2,1)S(1)}, bf16[4,136,640]{2,1,0:T(8,128)(2,1)S(1)}, u32[]{:S(2)}, u32[]{:S(2)}) collective-permute-start(bf16[4,136,640]{2,1,0:T(8,128)(2,1)S(1)} %other_term.2), channel_id=1, source_target_pairs={{0,16},{16,0},{1,17},{17,1},{2,18},{18,2},{3,19},{19,3},{4,20},{20... | collective-permute-start | bytes 2088968 | tf_op jit(solution)/shard_map/ppermute | solution.py:390
  80.0 2.9 %own_term.2.mine = f32[4,136,640]{2,1,0:T(8,128)S(1)} custom-call(f32[2,128,640]{2,1,0:T(8,128)S(1)} %get-tuple-element.34.refs_0_, f32[2,128,640]{2,1,0:T(8,128)S(1)} %get-tuple-element.35.refs_1_, bf16[2,128,256]{2,1,0:T(8,128)(2,1)S(1)} %get-tuple-element.30.maps.refs_2_, bf16[2,128,640]{2,1,0:T(8,128)(2,1)S(1)} %bitcast.25, f32[1,640]{1,0:T(1,128)S(1)} %copy-done.9, ...), custom_call_target="tpu_custom_call" | custom-call | flops 268435456 | bytes 4194304 | tf_op jit(solution)/shard_map/own_term/pallas_call | solution.py:42
  83.2 1.5 collective-permute-start.12
  85.9 8.2 %collective-permute-done.11.refs_0_ = bf16[136,640]{1,0:T(8,128)(2,1)S(1)} collective-permute-done((bf16[136,640]{1,0:T(8,128)(2,1)S(1)}, bf16[136,640]{1,0:T(8,128)(2,1)S(1)}, u32[]{:S(2)}, u32[]{:S(2)}) %collective-permute-start.11) | collective-permute-done | bytes 174112 | tf_op jit(solution)/shard_map/ppermute | solution.py:400
  94.6 1.3 collective-permute-start.14
  96.6 6.0 %collective-permute-done.14.piece = bf16[128,640]{1,0:T(8,128)(2,1)S(1)} collective-permute-done((bf16[128,640]{1,0:T(8,128)(2,1)S(1)}, bf16[128,640]{1,0:T(8,128)(2,1)S(1)}, u32[]{:S(2)}, u32[]{:S(2)}) %collective-permute-start.14) | collective-permute-done | bytes 163872 | tf_op jit(solution)/shard_map/ppermute | solution.py:463
  102.6 2.9 %collective-permute-start.18 = (bf16[136,640]{1,0:T(8,128)(2,1)S(1)}, bf16[136,640]{1,0:T(8,128)(2,1)S(1)}, u32[]{:S(2)}, u32[]{:S(2)}) collective-permute-start(bf16[136,640]{1,0:T(8,128)(2,1)S(1)} %constant_dynamic-update-slice_fusion.refs_0_), channel_id=1, source_target_pairs={{0,96},{32,0},{64,32},{96,64},{1,97},{33,1},{65,33},{97,65},{2,98}... | collective-permute-start | bytes 522248 | tf_op jit(solution)/shard_map/ppermute | solution.py:333
  106.2 2.2 %collective-permute-start.19 = (bf16[136,640]{1,0:T(8,128)(2,1)S(1)}, bf16[136,640]{1,0:T(8,128)(2,1)S(1)}, u32[]{:S(2)}, u32[]{:S(2)}) collective-permute-start(bf16[136,640]{1,0:T(8,128)(2,1)S(1)} %constant_dynamic-update-slice_fusion.refs_0_), channel_id=1, source_target_pairs={{0,16},{16,0},{1,17},{17,1},{2,18},{18,2},{3,19},{19,3},{4,20},{20... | collective-permute-start | bytes 522248 | tf_op jit(solution)/shard_map/ppermute | solution.py:335
  108.4 3.9 %collective-permute-done.18.refs_3_ = bf16[136,640]{1,0:T(8,128)(2,1)S(1)} collective-permute-done((bf16[136,640]{1,0:T(8,128)(2,1)S(1)}, bf16[136,640]{1,0:T(8,128)(2,1)S(1)}, u32[]{:S(2)}, u32[]{:S(2)}) %collective-permute-start.18) | collective-permute-done | bytes 174112 | tf_op jit(solution)/shard_map/ppermute | solution.py:333
  112.3 1.6 collective-permute-start.22
  113.8 1.9 %collective-permute-start.21 = (bf16[136,640]{1,0:T(8,128)(2,1)S(1)}, bf16[136,640]{1,0:T(8,128)(2,1)S(1)}, u32[]{:S(2)}, u32[]{:S(2)}) collective-permute-start(bf16[136,640]{1,0:T(8,128)(2,1)S(1)} %collective-permute-done.17.refs_2_), channel_id=1, source_target_pairs={{0,16},{16,0},{1,17},{17,1},{2,18},{18,2},{3,19},{19,3},{4,20},{20... | collective-permute-start | bytes 522248 | tf_op jit(solution)/shard_map/ppermute | solution.py:335
  118.6 6.8 %enter.3 = (bf16[4,256,640]{2,1,0:T(8,128)(2,1)S(1)}, bf16[2,128,640]{2,1,0:T(8,128)(2,1)S(1)}, bf16[2,128,256]{2,1,0:T(8,128)(2,1)S(1)}, f32[2,128,10]{2,1,0:T(...) custom-call(s32[1]{0:T(128)} %bitcast.2.chip_ref, ...), custom_call_target="tpu_custom_call" | custom-call | flops 268435456 | bytes 4194304 | tf_op jit(solution)/shard_map/enter/pallas_call | solution.py:42
  125.4 16.8 %all_to_all.21.arrived = bf16[16,16,768]{2,1,0:T(8,128)(2,1)S(1)} all-to-all(bf16[16,16,768]{2,1,0:T(8,128)(2,1)S(1)} %bitcast.29), channel_id=1, replica_groups=mesh['pipe'=2,'chip'=4,'core'=2,'seq_0'=8,'seq_1'=2] {'seq_0','seq_1'}, dimensions={0} | all-to-all | bytes 786432 | tf_op jit(solution)/shard_map/forth/all_to_all | solution.py:368
  143.2 4.1 %all-to-all-start.3 = ((bf16[16,16,640]{2,1,0:T(8,128)(2,1)}), bf16[16,16,640]{2,1,0:T(8,128)(2,1)S(1)}, u32[]{:S(2)}, u32[]{:S(2)}) async-start(bf16[16,16,640]{2,1,0:T(8,128)(2,1)} %scan_states.3), calls=%async_computation.3 | async-start | bytes 655360 | tf_op jit(solution)/shard_map/all_to_all | solution.py:384
  147.3 3.2 %gate_project.3.gate = f32[256,640]{1,0:T(8,128)S(1)} custom-call(bf16[4,256,640]{2,1,0:T(8,128)(2,1)S(1)} %get-tuple-element.45.normed, bf16[2560,640]{1,0:T(8,128)(2,1)} %bitcast.43), custom_call_target="tpu_custom_call" | custom-call | flops 268435456 | bytes 4194304 | tf_op jit(solution)/shard_map/gate_project/pallas_call | solution.py:42
  151.4 7.1 %all-to-all-done.3 = bf16[16,16,640]{2,1,0:T(8,128)(2,1)S(1)} async-done(((bf16[16,16,640]{2,1,0:T(8,128)(2,1)}), bf16[16,16,640]{2,1,0:T(8,128)(2,1)S(1)}, u32[]{:S(2)}, u32[]{:S(2)}) %all-to-all-start.3) | async-done | bytes 327712 | tf_op jit(solution)/shard_map/all_to_all | solution.py:384
  158.5 2.9 %other_term.3 = bf16[4,136,640]{2,1,0:T(8,128)(2,1)S(1)} custom-call(f32[2,128,640]{2,1,0:T(8,128)S(1)} %get-tuple-element.46.refs_0_, f32[2,128,640]{2,1,0:T(8,128)S(1)} %get-tuple-element.47.refs_1_, bf16[2,128,256]{2,1,0:T(8,128)(2,1)S(1)} %get-tuple-element.42.maps.refs_2_, bf16[2,128,640]{2,1,0:T(8,128)(2,1)S(1)} %bitcast.26, f32[1,640]{1,0:T(1,128)S(1)} %copy-done.9, ...), custom_call_target="tpu_custom_call" | custom-call | flops 268435456 | bytes 4194304 | tf_op jit(solution)/shard_map/other_term/pallas_call | solution.py:42
  161.4 3.2 %collective-permute-start.23 = (bf16[4,136,640]{2,1,0:T(8,128)(2,1)S(1)}, bf16[4,136,640]{2,1,0:T(8,128)(2,1)S(1)}, u32[]{:S(2)}, u32[]{:S(2)}) collective-permute-start(bf16[4,136,640]{2,1,0:T(8,128)(2,1)S(1)} %other_term.3), channel_id=1, source_target_pairs={{0,16},{16,0},{1,17},{17,1},{2,18},{18,2},{3,19},{19,3},{4,20},{20... | collective-permute-start | bytes 2088968 | tf_op jit(solution)/shard_map/ppermute | solution.py:390
  164.6 2.9 %own_term.3.mine = f32[4,136,640]{2,1,0:T(8,128)S(1)} custom-call(f32[2,128,640]{2,1,0:T(8,128)S(1)} %get-tuple-element.46.refs_0_, f32[2,128,640]{2,1,0:T(8,128)S(1)} %get-tuple-element.47.refs_1_, bf16[2,128,256]{2,1,0:T(8,128)(2,1)S(1)} %get-tuple-element.42.maps.refs_2_, bf16[2,128,640]{2,1,0:T(8,128)(2,1)S(1)} %bitcast.27, f32[1,640]{1,0:T(1,128)S(1)} %copy-done.9, ...), custom_call_target="tpu_custom_call" | custom-call | flops 268435456 | bytes 4194304 | tf_op jit(solution)/shard_map/own_term/pallas_call | solution.py:42
  167.8 1.9 %collective-permute-start.25 = (bf16[136,640]{1,0:T(8,128)(2,1)S(1)}, bf16[136,640]{1,0:T(8,128)(2,1)S(1)}, u32[]{:S(2)}, u32[]{:S(2)}) collective-permute-start(bf16[136,640]{1,0:T(8,128)(2,1)S(1)} %get-tuple-element.51), channel_id=1, source_target_pairs={{0,64},{32,96},{64,0},{96,32},{1,65},{33,97},{65,1},{97,33},{2,66}... | collective-permute-start | bytes 522248 | tf_op jit(solution)/shard_map/ppermute | solution.py:400
  170.5 8.2 %collective-permute-done.24.refs_0_ = bf16[136,640]{1,0:T(8,128)(2,1)S(1)} collective-permute-done((bf16[136,640]{1,0:T(8,128)(2,1)S(1)}, bf16[136,640]{1,0:T(8,128)(2,1)S(1)}, u32[]{:S(2)}, u32[]{:S(2)}) %collective-permute-start.24) | collective-permute-done | bytes 174112 | tf_op jit(solution)/shard_map/ppermute | solution.py:400
  (94 shorter events, 24.7 us)
Async XLA Ops:
  1.4 7.4 %collective-permute-start.2 = (bf16[8,320]{1,0:T(8,128)(2,1)S(1)}, bf16[8,320]{1,0:T(8,128)(2,1)S(1)}, u32[]{:S(2)}, u32[]{:S(2)}) collective-permute-start(bf16[8,320]{1,0:T(8,128)(2,1)S(1)} %slice_bitcast_fusion), channel_id=1, source_target_pairs={{0,17},{1,18},{2,19},{3,20},{4,21},{5,22},{6,23},{7,24},{8,25},{9,... | collective-permute-start | bytes 15368 | tf_op jit(solution)/shard_map/ppermute | solution.py:442
  4.8 4.6 %collective-permute-start.1 = (bf16[8,320]{1,0:T(8,128)(2,1)S(1)}, bf16[8,320]{1,0:T(8,128)(2,1)S(1)}, u32[]{:S(2)}, u32[]{:S(2)}) collective-permute-start(bf16[8,320]{1,0:T(8,128)(2,1)S(1)} %slice_bitcast_fusion.1), channel_id=1, source_target_pairs={{0,1},{1,2},{2,3},{3,4},{4,5},{5,6},{6,7},{7,8},{8,9},{9,10},{10,1... | collective-permute-start | bytes 15368 | tf_op jit(solution)/shard_map/ppermute | solution.py:441
  8.6 1.4 collective-permute-start
  10.1 10.0 %collective-permute-start.5 = (bf16[136,640]{1,0:T(8,128)(2,1)S(1)}, bf16[136,640]{1,0:T(8,128)(2,1)S(1)}, u32[]{:S(2)}, u32[]{:S(2)}) collective-permute-start(bf16[136,640]{1,0:T(8,128)(2,1)S(1)} %pad_maximum_fusion.refs_0_), channel_id=1, source_target_pairs={{0,96},{32,0},{64,32},{96,64},{1,97},{33,1},{65,33},{97,65},{2,98}... | collective-permute-start | bytes 522248 | tf_op jit(solution)/shard_map/ppermute | solution.py:333
  12.9 8.4 %collective-permute-start.4 = (bf16[136,640]{1,0:T(8,128)(2,1)S(1)}, bf16[136,640]{1,0:T(8,128)(2,1)S(1)}, u32[]{:S(2)}, u32[]{:S(2)}) collective-permute-start(bf16[136,640]{1,0:T(8,128)(2,1)S(1)} %pad_maximum_fusion.refs_0_), channel_id=1, source_target_pairs={{0,64},{32,96},{64,0},{96,32},{1,65},{33,97},{65,1},{97,33},{2,66}... | collective-permute-start | bytes 522248 | tf_op jit(solution)/shard_map/ppermute | solution.py:333
  13.3 11.2 %collective-permute-start.3 = (bf16[136,640]{1,0:T(8,128)(2,1)S(1)}, bf16[136,640]{1,0:T(8,128)(2,1)S(1)}, u32[]{:S(2)}, u32[]{:S(2)}) collective-permute-start(bf16[136,640]{1,0:T(8,128)(2,1)S(1)} %pad_maximum_fusion.refs_0_), channel_id=1, source_target_pairs={{0,32},{32,64},{64,96},{96,0},{1,33},{33,65},{65,97},{97,1},{2,34}... | collective-permute-start | bytes 522248 | tf_op jit(solution)/shard_map/ppermute | solution.py:333
  14.0 11.0 %collective-permute-start.6 = (bf16[136,640]{1,0:T(8,128)(2,1)S(1)}, bf16[136,640]{1,0:T(8,128)(2,1)S(1)}, u32[]{:S(2)}, u32[]{:S(2)}) collective-permute-start(bf16[136,640]{1,0:T(8,128)(2,1)S(1)} %pad_maximum_fusion.refs_0_), channel_id=1, source_target_pairs={{0,16},{16,0},{1,17},{17,1},{2,18},{18,2},{3,19},{19,3},{4,20},{20... | collective-permute-start | bytes 522248 | tf_op jit(solution)/shard_map/ppermute | solution.py:335
  20.2 4.9 %collective-permute-start.9 = (bf16[136,640]{1,0:T(8,128)(2,1)S(1)}, bf16[136,640]{1,0:T(8,128)(2,1)S(1)}, u32[]{:S(2)}, u32[]{:S(2)}) collective-permute-start(bf16[136,640]{1,0:T(8,128)(2,1)S(1)} %collective-permute-done.5.refs_3_), channel_id=1, source_target_pairs={{0,16},{16,0},{1,17},{17,1},{2,18},{18,2},{3,19},{19,3},{4,20},{20... | collective-permute-start | bytes 522248 | tf_op jit(solution)/shard_map/ppermute | solution.py:335
  21.3 3.7 %collective-permute-start.8 = (bf16[136,640]{1,0:T(8,128)(2,1)S(1)}, bf16[136,640]{1,0:T(8,128)(2,1)S(1)}, u32[]{:S(2)}, u32[]{:S(2)}) collective-permute-start(bf16[136,640]{1,0:T(8,128)(2,1)S(1)} %collective-permute-done.4.refs_2_), channel_id=1, source_target_pairs={{0,16},{16,0},{1,17},{17,1},{2,18},{18,2},{3,19},{19,3},{4,20},{20... | collective-permute-start | bytes 522248 | tf_op jit(solution)/shard_map/ppermute | solution.py:335
  24.5 1.5 collective-permute-start.7
  58.5 15.3 %all-to-all-start.1 = ((bf16[16,16,640]{2,1,0:T(8,128)(2,1)}), bf16[16,16,640]{2,1,0:T(8,128)(2,1)S(1)}, u32[]{:S(2)}, u32[]{:S(2)}) async-start(bf16[16,16,640]{2,1,0:T(8,128)(2,1)} %scan_states.2), calls=%async_computation.1 | async-start | bytes 655360 | tf_op jit(solution)/shard_map/all_to_all | solution.py:384
  76.7 6.2 %collective-permute-start.10 = (bf16[4,136,640]{2,1,0:T(8,128)(2,1)S(1)}, bf16[4,136,640]{2,1,0:T(8,128)(2,1)S(1)}, u32[]{:S(2)}, u32[]{:S(2)}) collective-permute-start(bf16[4,136,640]{2,1,0:T(8,128)(2,1)S(1)} %other_term.2), channel_id=1, source_target_pairs={{0,16},{16,0},{1,17},{17,1},{2,18},{18,2},{3,19},{19,3},{4,20},{20... | collective-permute-start | bytes 2088968 | tf_op jit(solution)/shard_map/ppermute | solution.py:390
  82.9 35.7 %copy-start.6 = (f32[1,5,640]{2,0,1:T(1,128)S(1)}, f32[1,5,640]{2,0,1:T(1,128)}, u32[]{:S(2)}) copy-start(f32[1,5,640]{2,0,1:T(1,128)} %param.19) | copy-start | bytes 38404
  82.9 35.7 %copy-start.8 = (f32[1,2560]{1,0:T(1,128)S(1)}, f32[1,2560]{1,0:T(1,128)}, u32[]{:S(2)}) copy-start(f32[1,2560]{1,0:T(1,128)} %param.14) | copy-start | bytes 30724
  83.1 11.0 %collective-permute-start.11 = (bf16[136,640]{1,0:T(8,128)(2,1)S(1)}, bf16[136,640]{1,0:T(8,128)(2,1)S(1)}, u32[]{:S(2)}, u32[]{:S(2)}) collective-permute-start(bf16[136,640]{1,0:T(8,128)(2,1)S(1)} %get-tuple-element.38), channel_id=1, source_target_pairs={{0,32},{32,64},{64,96},{96,0},{1,33},{33,65},{65,97},{97,1},{2,34}... | collective-permute-start | bytes 522248 | tf_op jit(solution)/shard_map/ppermute | solution.py:400
  83.2 10.9 %collective-permute-start.12 = (bf16[136,640]{1,0:T(8,128)(2,1)S(1)}, bf16[136,640]{1,0:T(8,128)(2,1)S(1)}, u32[]{:S(2)}, u32[]{:S(2)}) collective-permute-start(bf16[136,640]{1,0:T(8,128)(2,1)S(1)} %get-tuple-element.39), channel_id=1, source_target_pairs={{0,64},{32,96},{64,0},{96,32},{1,65},{33,97},{65,1},{97,33},{2,66}... | collective-permute-start | bytes 522248 | tf_op jit(solution)/shard_map/ppermute | solution.py:400
  84.7 9.7 %collective-permute-start.13 = (bf16[136,640]{1,0:T(8,128)(2,1)S(1)}, bf16[136,640]{1,0:T(8,128)(2,1)S(1)}, u32[]{:S(2)}, u32[]{:S(2)}) collective-permute-start(bf16[136,640]{1,0:T(8,128)(2,1)S(1)} %get-tuple-element.40), channel_id=1, source_target_pairs={{0,96},{32,0},{64,32},{96,64},{1,97},{33,1},{65,33},{97,65},{2,98}... | collective-permute-start | bytes 522248 | tf_op jit(solution)/shard_map/ppermute | solution.py:400
  94.6 8.0 %collective-permute-start.14 = (bf16[128,640]{1,0:T(8,128)(2,1)S(1)}, bf16[128,640]{1,0:T(8,128)(2,1)S(1)}, u32[]{:S(2)}, u32[]{:S(2)}) collective-permute-start(bf16[128,640]{1,0:T(8,128)(2,1)S(1)} %finish.2), channel_id=1, source_target_pairs={{0,128},{1,129},{2,130},{3,131},{4,132},{5,133},{6,134},{7,135},{8... | collective-permute-start | bytes 491528 | tf_op jit(solution)/shard_map/ppermute | solution.py:463
  95.9 0.7 collective-permute-start.15
  102.6 9.7 %collective-permute-start.18 = (bf16[136,640]{1,0:T(8,128)(2,1)S(1)}, bf16[136,640]{1,0:T(8,128)(2,1)S(1)}, u32[]{:S(2)}, u32[]{:S(2)}) collective-permute-start(bf16[136,640]{1,0:T(8,128)(2,1)S(1)} %constant_dynamic-update-slice_fusion.refs_0_), channel_id=1, source_target_pairs={{0,96},{32,0},{64,32},{96,64},{1,97},{33,1},{65,33},{97,65},{2,98}... | collective-permute-start | bytes 522248 | tf_op jit(solution)/shard_map/ppermute | solution.py:333
  105.5 8.4 %collective-permute-start.17 = (bf16[136,640]{1,0:T(8,128)(2,1)S(1)}, bf16[136,640]{1,0:T(8,128)(2,1)S(1)}, u32[]{:S(2)}, u32[]{:S(2)}) collective-permute-start(bf16[136,640]{1,0:T(8,128)(2,1)S(1)} %constant_dynamic-update-slice_fusion.refs_0_), channel_id=1, source_target_pairs={{0,64},{32,96},{64,0},{96,32},{1,65},{33,97},{65,1},{97,33},{2,66}... | collective-permute-start | bytes 522248 | tf_op jit(solution)/shard_map/ppermute | solution.py:333
  105.7 10.9 %collective-permute-start.16 = (bf16[136,640]{1,0:T(8,128)(2,1)S(1)}, bf16[136,640]{1,0:T(8,128)(2,1)S(1)}, u32[]{:S(2)}, u32[]{:S(2)}) collective-permute-start(bf16[136,640]{1,0:T(8,128)(2,1)S(1)} %constant_dynamic-update-slice_fusion.refs_0_), channel_id=1, source_target_pairs={{0,32},{32,64},{64,96},{96,0},{1,33},{33,65},{65,97},{97,1},{2,34}... | collective-permute-start | bytes 522248 | tf_op jit(solution)/shard_map/ppermute | solution.py:333
  106.2 11.4 %collective-permute-start.19 = (bf16[136,640]{1,0:T(8,128)(2,1)S(1)}, bf16[136,640]{1,0:T(8,128)(2,1)S(1)}, u32[]{:S(2)}, u32[]{:S(2)}) collective-permute-start(bf16[136,640]{1,0:T(8,128)(2,1)S(1)} %constant_dynamic-update-slice_fusion.refs_0_), channel_id=1, source_target_pairs={{0,16},{16,0},{1,17},{17,1},{2,18},{18,2},{3,19},{19,3},{4,20},{20... | collective-permute-start | bytes 522248 | tf_op jit(solution)/shard_map/ppermute | solution.py:335
  112.3 5.2 %collective-permute-start.22 = (bf16[136,640]{1,0:T(8,128)(2,1)S(1)}, bf16[136,640]{1,0:T(8,128)(2,1)S(1)}, u32[]{:S(2)}, u32[]{:S(2)}) collective-permute-start(bf16[136,640]{1,0:T(8,128)(2,1)S(1)} %collective-permute-done.18.refs_3_), channel_id=1, source_target_pairs={{0,16},{16,0},{1,17},{17,1},{2,18},{18,2},{3,19},{19,3},{4,20},{20... | collective-permute-start | bytes 522248 | tf_op jit(solution)/shard_map/ppermute | solution.py:335
  113.8 3.7 %collective-permute-start.21 = (bf16[136,640]{1,0:T(8,128)(2,1)S(1)}, bf16[136,640]{1,0:T(8,128)(2,1)S(1)}, u32[]{:S(2)}, u32[]{:S(2)}) collective-permute-start(bf16[136,640]{1,0:T(8,128)(2,1)S(1)} %collective-permute-done.17.refs_2_), channel_id=1, source_target_pairs={{0,16},{16,0},{1,17},{17,1},{2,18},{18,2},{3,19},{19,3},{4,20},{20... | collective-permute-start | bytes 522248 | tf_op jit(solution)/shard_map/ppermute | solution.py:335
  116.6 1.9 %collective-permute-start.20 = (bf16[136,640]{1,0:T(8,128)(2,1)S(1)}, bf16[136,640]{1,0:T(8,128)(2,1)S(1)}, u32[]{:S(2)}, u32[]{:S(2)}) collective-permute-start(bf16[136,640]{1,0:T(8,128)(2,1)S(1)} %collective-permute-done.16.refs_1_), channel_id=1, source_target_pairs={{0,16},{16,0},{1,17},{17,1},{2,18},{18,2},{3,19},{19,3},{4,20},{20... | collective-permute-start | bytes 522248 | tf_op jit(solution)/shard_map/ppermute | solution.py:335
  143.2 15.4 %all-to-all-start.3 = ((bf16[16,16,640]{2,1,0:T(8,128)(2,1)}), bf16[16,16,640]{2,1,0:T(8,128)(2,1)S(1)}, u32[]{:S(2)}, u32[]{:S(2)}) async-start(bf16[16,16,640]{2,1,0:T(8,128)(2,1)} %scan_states.3), calls=%async_computation.3 | async-start | bytes 655360 | tf_op jit(solution)/shard_map/all_to_all | solution.py:384
  161.4 6.1 %collective-permute-start.23 = (bf16[4,136,640]{2,1,0:T(8,128)(2,1)S(1)}, bf16[4,136,640]{2,1,0:T(8,128)(2,1)S(1)}, u32[]{:S(2)}, u32[]{:S(2)}) collective-permute-start(bf16[4,136,640]{2,1,0:T(8,128)(2,1)S(1)} %other_term.3), channel_id=1, source_target_pairs={{0,16},{16,0},{1,17},{17,1},{2,18},{18,2},{3,19},{19,3},{4,20},{20... | collective-permute-start | bytes 2088968 | tf_op jit(solution)/shard_map/ppermute | solution.py:390
  167.7 11.0 %collective-permute-start.24 = (bf16[136,640]{1,0:T(8,128)(2,1)S(1)}, bf16[136,640]{1,0:T(8,128)(2,1)S(1)}, u32[]{:S(2)}, u32[]{:S(2)}) collective-permute-start(bf16[136,640]{1,0:T(8,128)(2,1)S(1)} %get-tuple-element.50), channel_id=1, source_target_pairs={{0,32},{32,64},{64,96},{96,0},{1,33},{33,65},{65,97},{97,1},{2,34}... | collective-permute-start | bytes 522248 | tf_op jit(solution)/shard_map/ppermute | solution.py:400
  167.8 10.9 %collective-permute-start.25 = (bf16[136,640]{1,0:T(8,128)(2,1)S(1)}, bf16[136,640]{1,0:T(8,128)(2,1)S(1)}, u32[]{:S(2)}, u32[]{:S(2)}) collective-permute-start(bf16[136,640]{1,0:T(8,128)(2,1)S(1)} %get-tuple-element.51), channel_id=1, source_target_pairs={{0,64},{32,96},{64,0},{96,32},{1,65},{33,97},{65,1},{97,33},{2,66}... | collective-permute-start | bytes 522248 | tf_op jit(solution)/shard_map/ppermute | solution.py:400
  169.7 9.3 %collective-permute-start.26 = (bf16[136,640]{1,0:T(8,128)(2,1)S(1)}, bf16[136,640]{1,0:T(8,128)(2,1)S(1)}, u32[]{:S(2)}, u32[]{:S(2)}) collective-permute-start(bf16[136,640]{1,0:T(8,128)(2,1)S(1)} %get-tuple-element.52), channel_id=1, source_target_pairs={{0,96},{32,0},{64,32},{96,64},{1,97},{33,1},{65,33},{97,65},{2,98}... | collective-permute-start | bytes 522248 | tf_op jit(solution)/shard_map/ppermute | solution.py:400
  179.3 2.2 %collective-permute-start.27 = (bf16[128,320]{1,0:T(8,128)(2,1)S(1)}, bf16[128,320]{1,0:T(8,128)(2,1)S(1)}, u32[]{:S(2)}, u32[]{:S(2)}) collective-permute-start(bf16[128,320]{1,0:T(8,128)(2,1)S(1)} %get-tuple-element.56), channel_id=1, source_target_pairs={{0,16},{16,0},{1,17},{17,1},{2,18},{18,2},{3,19},{19,3},{4,20},{20... | collective-permute-start | bytes 245768 | tf_op jit(solution)/shard_map/ppermute | solution.py:475
  (14 other events, 271.7 us)

commit v3 on v2

--- a/solution.py
+++ b/solution.py
@@ -6,10 +6,11 @@
 from jax.sharding import Mesh
 from jax.sharding import PartitionSpec as P
 
-BLOCK = 128
 INNER = 5120
 EPS = 1e-05
 EDGE = 8
+NEAR = (0,)
+FAR = (2, 1, 3)
 SEQ = ("seq_0", "seq_1")
 TENSOR = ("chip", "core")
 SWAP = [(0, 1), (1, 0)]
@@ -45,18 +46,17 @@
         in_specs=[SMEM] * scalars + [VMEM] * (len(args) - scalars - weights) + [HBM] * weights,
         out_specs=[VMEM] * len(outs),
         cost_estimate=pl.CostEstimate(flops=flops, transcendentals=0, bytes_accessed=1 << 22),
-        name=body.__name__,
         scratch_shapes=list(scratch),
         compiler_params=pltpu.CompilerParams(vmem_limit_bytes=mib << 20),
     )(*args)
 
 
-def fetch(source, target, semaphores):
+def fetch(source, target, semaphores, blocks=None):
     parts = semaphores.shape[0]
-    size = source.shape[0] // parts
+    size = target.shape[0] // parts
     copies = [
         pltpu.make_async_copy(
-            source.at[pl.ds(part * size, size)],
+            source.at[pl.ds((part if blocks is None else blocks[part]) * size, size)],
             target.at[pl.ds(part * size, size)],
             semaphores.at[part],
         )
@@ -67,8 +67,30 @@
     return copies
 
 
-def room(weight, parts):
-    return [pltpu.VMEM(weight.shape, weight.dtype), pltpu.SemaphoreType.DMA((parts,))]
+def blocks_of(steps):
+    chip, count = lax.axis_index("chip"), 4
+    return [lax.rem(chip - step + count, count) for step in steps]
+
+
+def fetch_columns(source, target, semaphores):
+    parts = semaphores.shape[0]
+    size = target.shape[1] // parts
+    copies = [
+        pltpu.make_async_copy(
+            source.at[:, pl.ds(part * size, size)],
+            target.at[:, pl.ds(part * size, size)],
+            semaphores.at[part],
+        )
+        for part in range(parts)
+    ]
+    for copy in copies:
+        copy.start()
+    return copies
+
+
+def room(weight, parts, rows=None):
+    shape = (rows or weight.shape[0], weight.shape[1])
+    return [pltpu.VMEM(shape, weight.dtype), pltpu.SemaphoreType.DMA((parts,))]
 
 
 def dot(a, b, dims=((1,), (0,))):
@@ -83,14 +105,15 @@
     return lax.broadcasted_iota(jnp.int32, shape, dim)
 
 
-def spread(heads, width):
+def spread(heads, width, copies=1):
     size = width // heads
-    lane, head = iota((heads, width), 1), iota((heads, width), 0)
+    lane, head = iota((heads * copies, width), 1), iota((heads * copies, width), 0) % heads
     return jnp.where((lane >= head * size) & (lane < (head + 1) * size), 1.0, 0.0).astype(BF16)
 
 
-def over_channels(value, picks):
-    return sum(dot(part, picks) for part in split_bf16(value, 3))
+def over_channels(value, width):
+    parts = [part.astype(F32) for part in split_bf16(value, 3)]
+    return dot(jnp.concatenate(parts, 1).astype(BF16), spread(value.shape[1], width, 3))
 
 
 def convolve(rim, values, taps):
@@ -104,65 +127,107 @@
     return (total * sigmoid(total)).astype(BF16)
 
 
-def enter(chip_ref, *refs):
-    count = (len(refs) - 19) // 2
+def place(piece, gain, scaled, side, edge):
+    rows = piece.shape[0] - edge
+    value = piece[...].astype(F32)
+    square = value * value
+    squares = 0.0
+    for tile in range(piece.shape[1] // 128):
+        squares = squares + square[:, tile * 128 : (tile + 1) * 128]
+    value = value * gain
+    scaled[side * rows : (side + 1) * rows, :] = value[edge:].astype(BF16)
+    return squares, value[:edge]
+
+
+def columns(array, b, width):
+    return array[:, pl.ds(pl.multiple_of(b * width, width), width)]
+
+
+def multiply(scaled, part, step_w, state_w, inner_w, copies):
+    block = scaled.shape[1]
+    span = slice(part * block, (part + 1) * block)
+    value = scaled[...]
+    step = dot(value, step_w, ((1,), (1,)))
+    copies[0][part].wait()
+    state = dot(value, state_w[span, :])
+    copies[1][part].wait()
+    return step, state, dot(value, inner_w[span, :])
+
+
+def enter_near(*refs):
+    count = len(NEAR)
     sides = refs[:count], refs[count : 2 * count]
-    gain, step_w, inner_taps, state_taps, bias, rate, state_hbm, inner_hbm = refs[2 * count :][:8]
-    normed, x, maps, steps, sums, sent, tails = refs[2 * count + 8 :][:7]
-    state_w, state_sems, inner_w, inner_sems = refs[2 * count + 15 :]
-    state_copies = fetch(state_hbm, state_w, state_sems)
-    inner_copies = fetch(inner_hbm, inner_w, inner_sems)
-    chip = chip_ref[0]
+    gain, step_w, state_hbm, inner_hbm = refs[2 * count :][:4]
+    scaled, squares, step, state, inner = refs[2 * count + 4 :][:5]
+    state_w, state_sems, inner_w, inner_sems = refs[2 * count + 9 :]
+    blocks = blocks_of(NEAR)
+    copies = fetch(state_hbm, state_w, state_sems, blocks), fetch(
+        inner_hbm, inner_w, inner_sems, blocks
+    )
+    edge = EDGE
+    rows = sides[0][0].shape[0] - edge
+    width = sides[0][0].shape[1]
+    sums = [0.0, 0.0]
+    totals = [0.0, 0.0, 0.0]
+    for k, b in enumerate(blocks):
+        tails = []
+        for side in range(2):
+            part, tail = place(sides[side][k], gain[b], scaled.at[k], side, edge)
+            sums[side] = sums[side] + part
+            tails.append(tail)
+        scaled[k, 2 * rows :, :] = jnp.concatenate(tails).astype(BF16)
+        parts = multiply(scaled.at[k], k, columns(step_w, b, width), state_w, inner_w, copies)
+        totals = [total + part for total, part in zip(totals, parts)]
+    for side in range(2):
+        squares[side * rows : (side + 1) * rows, :] = sums[side][edge:]
+        squares[2 * rows + side * edge : 2 * rows + (side + 1) * edge, :] = sums[side][:edge]
+    step[...], state[...], inner[...] = totals
+
+
+def enter_far(*refs):
+    count = len(FAR)
+    sides = refs[:count], refs[count : 2 * count]
+    squares_in, step_in, state_in, inner_in = refs[2 * count :][:4]
+    refs = refs[2 * count + 4 :]
+    gain, step_w, inner_taps, state_taps, bias, rate, state_hbm, inner_hbm = refs[:8]
+    scaled, scales, x, maps, steps, sums, sent = refs[8:15]
+    state_w, state_sems, inner_w, inner_sems = refs[15:]
+    blocks = blocks_of(FAR)
+    copies = fetch(state_hbm, state_w, state_sems, blocks), fetch(
+        inner_hbm, inner_w, inner_sems, blocks
+    )
+    edge = EDGE
     rows, width = x.shape[1:]
-    block = gain.shape[2]
-    edge = sides[0][0].shape[0] - rows
+    block = sides[0][0].shape[1]
     heads = bias.shape[1]
     n = maps.shape[2] // 2
-    for side, pieces in enumerate(sides):
-        squares = jnp.zeros((rows + edge, 128), F32)
-        for piece in pieces:
-            value = piece[...].astype(F32)
-            value = value * value
-            for tile in range(block // 128):
-                squares = squares + value[:, tile * 128 : (tile + 1) * 128]
-        scale = lax.rsqrt(jnp.sum(squares, axis=1, keepdims=True) / (count * block) + EPS)
-        for k, piece in enumerate(pieces):
-            b = lax.rem(chip - k + count, count)
-            value = piece[...].astype(F32) * scale * gain[b]
-            normed[b, side * rows : (side + 1) * rows, :] = value[edge:].astype(BF16)
-            tails[b, side * edge : (side + 1) * edge, :] = value[:edge]
-
-    def times(weight, copies):
-        main, tail = 0.0, 0.0
-        for b in range(count):
-            copies[b].wait()
-            part = weight[b * block : (b + 1) * block, :]
-            main = main + dot(normed[b], part)
-            tail = tail + dot(tails[b].astype(BF16), part)
-        return main, tail
-
-    raw = jnp.zeros((2 * rows, heads), F32)
-    for b in range(count):
-        raw = raw + dot(normed[b], step_w[:, b * block : (b + 1) * block], ((1,), (1,)))
-    raw = raw + bias[...]
+    found = [0.0, 0.0]
+    for k, b in enumerate(blocks):
+        tails = []
+        for side in range(2):
+            part, tail = place(sides[side][k], gain[b], scaled.at[k], side, edge)
+            found[side] = found[side] + part
+            tails.append(tail)
+        scaled[k, 2 * rows :, :] = jnp.concatenate(tails).astype(BF16)
+    found = jnp.concatenate([found[0][edge:], found[1][edge:], found[0][:edge], found[1][:edge]])
+    squares = jnp.sum(squares_in[...] + found, axis=1, keepdims=True)
+    scale = lax.rsqrt(squares / (len(NEAR + FAR) * block) + EPS)
+    scales[...] = jnp.broadcast_to(scale[: 2 * rows], scales.shape)
+    totals = [step_in[...], state_in[...], inner_in[...]]
+    for k, b in enumerate(blocks):
+        parts = multiply(scaled.at[k], k, columns(step_w, b, block), state_w, inner_w, copies)
+        totals = [total + part for total, part in zip(totals, parts)]
+    step, state, inner = totals
+    raw = (step * scale)[: 2 * rows] + bias[...]
     step_all = jnp.maximum(raw, 0.0) + jnp.log1p(jnp.exp(-jnp.abs(raw)))
-    state, state_tail = times(state_w, state_copies)
-    inner, inner_tail = times(inner_w, inner_copies)
+    state = (state * scale).astype(BF16).astype(F32)
+    inner = (inner * scale).astype(BF16).astype(F32)
     lower = (iota((rows, rows), 0) >= iota((rows, rows), 1)).astype(BF16)
-    picks = spread(heads, width)
     for m in range(2):
         span = slice(m * rows, (m + 1) * rows)
-        ends = slice(m * edge, (m + 1) * edge)
-        xm = convolve(
-            inner_tail[ends].astype(BF16).astype(F32),
-            inner[span].astype(BF16).astype(F32),
-            inner_taps,
-        )
-        sm = convolve(
-            state_tail[ends].astype(BF16).astype(F32),
-            state[span].astype(BF16).astype(F32),
-            state_taps,
-        )
+        ends = slice(2 * rows + m * edge, 2 * rows + (m + 1) * edge)
+        sm = convolve(state[ends], state[span], state_taps)
+        xm = convolve(inner[ends], inner[span], inner_taps)
         x[m] = xm
         maps[m] = sm
         step = step_all[span]
@@ -170,7 +235,7 @@
         last = total[rows - 1 :]
         steps[m] = step
         sums[m] = total
-        weighting = over_channels(jnp.exp(last - total) * step, picks)
+        weighting = over_channels(jnp.exp(last - total) * step, width)
         weighted = (xm.astype(F32) * weighting).astype(BF16)
         sent[span, :width] = dot(sm[:, :n], weighted, ((0,), (0,))).astype(BF16)
         high, low = split_bf16(jnp.exp(last), 2)
@@ -180,16 +245,19 @@
         sent[span, width:] = ends.astype(BF16)
 
 
-def gate_project(normed, gate_hbm, gate, gate_w, gate_sems):
-    count, _, width = normed.shape
-    copies = fetch(gate_hbm, gate_w, gate_sems)
-    total = jnp.zeros(gate.shape, F32)
-    for block in range(count):
-        copies[block].wait()
-        total = total + dot(normed[block], gate_w[block * width : (block + 1) * width, :])
-    gate[...] = (total.astype(BF16).astype(F32) * sigmoid(total.astype(BF16).astype(F32))).astype(
-        gate.dtype
-    )
+def gate_project(near, far, scales, gate_hbm, gate, gate_w, gate_sems):
+    copies = fetch(gate_hbm, gate_w, gate_sems, blocks_of(NEAR + FAR))
+    rows, width = gate.shape
+    block = far.shape[2]
+    total = 0.0
+    for part in range(len(NEAR + FAR)):
+        scaled = near[part, :rows] if part < len(NEAR) else far[part - len(NEAR), :rows]
+        copies[part].wait()
+        total = total + dot(scaled, gate_w[part * block : (part + 1) * block, :])
+    for tile in range(width // 128):
+        span = slice(tile * 128, (tile + 1) * 128)
+        value = (total[:, span] * scales[...]).astype(BF16).astype(F32)
+        gate[:, span] = value * sigmoid(value)
 
 
 def local_mixing(x, maps, steps, sums, gate, skip, base, ahead):
@@ -198,8 +266,7 @@
     size = width // heads
     pair = 128 // size
     n = maps.shape[2] // 2
-    picks = spread(heads, width)
-    skips = over_channels(jnp.broadcast_to(skip[...], (8, heads)), picks)[:1]
+    skips = over_channels(jnp.broadcast_to(skip[...], (8, heads)), width)[:1]
     later = iota((rows, rows), 0) >= iota((rows, rows), 1)
     lane = iota((rows, pair * size), 1)
     for m in range(micros):
@@ -223,7 +290,7 @@
             inside = dot(jnp.concatenate(left, 1), jnp.concatenate(right, 0))
             silu = gate[m * rows : (m + 1) * rows, span]
             base[m, :, span] = (inside + skips[:, span] * xg.astype(F32)) * silu
-        ahead[m] = over_channels(jnp.exp(sums_m), picks) * gate[m * rows : (m + 1) * rows]
+        ahead[m] = over_channels(jnp.exp(sums_m), width) * gate[m * rows : (m + 1) * rows]
 
 
 def scan_states(arrived, back, heads=10):
@@ -247,38 +314,35 @@
     return jnp.transpose(block)[:8]
 
 
-def output_term(m, base, ahead, maps, entering, gain, out_hbm, term, out_w, out_sems):
+def output_terms(base, ahead, maps, entering, gain, out_hbm, mine, given, out_w, out_sems):
     n = maps.shape[2] // 2
-    count, tall, width = term.shape
-    (copy,) = fetch(out_hbm, out_w, out_sems)
+    count, _, width = mine.shape
+    copies = fetch_columns(out_hbm, out_w, out_sems)
     rows = base.shape[1]
-    across = dot(maps[m, :, n:], entering[m])
-    gated = base[m] + across * ahead[m]
-    squares = jnp.sum(gated * gated, axis=1, keepdims=True)
-    scaled = (gated * gain[...]).astype(BF16)
-    block = squares_rows(squares)
-    block = jnp.concatenate([block, jnp.zeros((8, width - 128), F32)], 1).astype(term.dtype)
-    copy.wait()
+    scaled = []
+    for m, term in enumerate((mine, given)):
+        across = dot(maps[m, :, n:], entering[m])
+        gated = base[m] + across * ahead[m]
+        squares = jnp.sum(gated * gated, axis=1, keepdims=True)
+        scaled.append((gated * gain[...]).astype(BF16))
+        block = squares_rows(squares)
+        block = jnp.concatenate([block, jnp.zeros((8, width - 128), F32)], 1).astype(term.dtype)
+        for b in range(count):
+            term[b, rows:] = block
+    scaled = jnp.concatenate(scaled)
     for b in range(count):
+        copies[b].wait()
         value = dot(scaled, out_w[:, b * width : (b + 1) * width])
-        term[b, :rows] = value.astype(term.dtype)
-        term[b, rows:] = block
-
-
-def other_term(*refs):
-    output_term(1, *refs)
-
-
-def own_term(*refs):
-    output_term(0, *refs)
+        mine[b, :rows] = value[:rows].astype(mine.dtype)
+        given[b, :rows] = value[rows:].astype(given.dtype)
 
 
 def merge_cores(chip_ref, mine, arrived, kept, *sent):
     count, tall, width = mine.shape
     rows = tall - 8
     chip = chip_ref[0]
-    kept[:rows] = mine[chip, :rows] + arrived[chip, :rows].astype(F32)
-    both = jnp.sum(mine[0, rows:] + arrived[0, rows:].astype(F32), axis=0, keepdims=True)
+    kept[:rows] = mine[chip, :rows].astype(F32) + arrived[chip, :rows].astype(F32)
+    both = jnp.sum(mine[0, rows:].astype(F32) + arrived[0, rows:].astype(F32), axis=0, keepdims=True)
     row = iota((8, width), 0)
     kept[rows:] = jnp.where(row == 0, both, 0.0)
     block = jnp.zeros((8, width), F32)
@@ -286,7 +350,7 @@
         block = jnp.where(row == index, part.astype(F32), block)
     for k in range(1, count):
         b = lax.rem(chip + k, count)
-        sent[k - 1][:rows] = (mine[b, :rows] + arrived[b, :rows].astype(F32)).astype(BF16)
+        sent[k - 1][:rows] = (mine[b, :rows].astype(F32) + arrived[b, :rows].astype(F32)).astype(BF16)
         sent[k - 1][rows:] = block.astype(BF16)
 
 
@@ -329,18 +393,44 @@
     maps_width = state_weight.shape[1]
     heads = step_weight.shape[1]
     spread_rows = jnp.concatenate([edge, piece], axis=0)
-    own = [spread_rows] + [
-        lax.ppermute(spread_rows, "chip", ring(count, k)) for k in range(1, count)
-    ]
-    other = [lax.ppermute(part, "core", SWAP) for part in own]
-    normed, x, maps, steps, sums, sent = local(
-        enter,
+    gain = prenorm.reshape(count, 1, block)
+    steps_weight = step_weight.T
+
+    def moved(step):
+        return lax.ppermute(spread_rows, "chip", ring(count, step))
+
+    far = moved(2)
+    before = moved(1)
+    after = moved(3)
+    own = {0: spread_rows, 1: before, 2: far, 3: after}
+    other = {k: lax.ppermute(part, "core", SWAP) for k, part in own.items()}
+    near = [own[k] for k in NEAR] + [other[k] for k in NEAR]
+    far = [own[k] for k in FAR] + [other[k] for k in FAR]
+    high = 2 * spread_rows.shape[0]
+    scaled, squares, *partial = local(
+        enter_near,
+        [*near, gain, steps_weight, state_weight, inner_weight],
         [
-            chip,
-            *own,
-            *other,
-            prenorm.reshape(count, 1, block),
-            step_weight.T,
+            ((len(NEAR), high, block), BF16),
+            ((high, 128), F32),
+            ((high, heads), F32),
+            ((high, maps_width), F32),
+            ((high, width), F32),
+        ],
+        weights=2,
+        scratch=[
+            *room(state_weight, len(NEAR), len(NEAR) * block),
+            *room(inner_weight, len(NEAR), len(NEAR) * block),
+        ],
+    )
+    scaled_far, scales, x, maps, steps, sums, sent = local(
+        enter_far,
+        [
+            *far,
+            squares,
+            *partial,
+            gain,
+            steps_weight,
             inner_taps[:, None],
             state_taps[:, None],
             step_bias[None],
@@ -349,28 +439,26 @@
             inner_weight,
         ],
         [
-            ((count, tall, block), BF16),
+            ((len(FAR), high, block), BF16),
+            ((tall, 128), F32),
             ((2, rows, width), BF16),
             ((2, rows, maps_width), BF16),
             ((2, rows, heads), F32),
             ((2, rows, heads), F32),
             ((tall, width + 128), BF16),
         ],
-        scalars=1,
         weights=2,
         scratch=[
-            pltpu.VMEM((count, 2 * edge.shape[0], block), F32),
-            *room(state_weight, count),
-            *room(inner_weight, count),
+            *room(state_weight, len(FAR), len(FAR) * block),
+            *room(inner_weight, len(FAR), len(FAR) * block),
         ],
     )
-    with jax.named_scope("forth"):
-        arrived = lax.all_to_all(
-            sent.reshape(members, tall // members, -1), SEQ, 0, 0, tiled=True
-        )
+    arrived = lax.all_to_all(
+        sent.reshape(members, tall // members, -1), SEQ, 0, 0, tiled=True
+    )
     (gate,) = local(
         gate_project,
-        [normed, gate_weight],
+        [scaled, scaled_far, scales, gate_weight],
         [((tall, width), F32)],
         weights=1,
         scratch=room(gate_weight, count),
@@ -383,14 +471,14 @@
     (back,) = local(scan_states, [arrived], [((members, tall // members, width), BF16)])
     back = lax.all_to_all(back, SEQ, 0, 0, tiled=True)
     entering = back.reshape(2, rows, width)
-    common = [base, ahead, maps, entering, inner_gain[None], out_weight]
-    (given,) = local(
-        other_term, common, [((count, rows + 8, block), BF16)], weights=1, scratch=room(out_weight, 1)
+    mine, given = local(
+        output_terms,
+        [base, ahead, maps, entering, inner_gain[None], out_weight],
+        [((count, rows + 8, block), BF16)] * 2,
+        weights=1,
+        scratch=room(out_weight, count),
     )
     taken = lax.ppermute(given, "core", SWAP)
-    (mine,) = local(
-        own_term, common, [((count, rows + 8, block), F32)], weights=1, scratch=room(out_weight, 1)
-    )
     kept, *leaving = local(
         merge_cores,
         [chip, mine, taken],
@@ -435,26 +523,18 @@
     core = lax.axis_index("core")
     width = tokens.shape[2]
     members = lax.axis_size(SEQ)
-    mine = jnp.where(core == 0, tokens[0], tokens[1])
-    theirs = jnp.where(core == 0, tokens[1], tokens[0])
-    given = lax.ppermute(theirs, "core", SWAP)
-    mine_edge = lax.ppermute(mine[-EDGE:], SEQ, [(s, s + 1) for s in range(members - 1)])
-    given_edge = lax.ppermute(
-        theirs[-EDGE:],
-        ("core", *SEQ),
-        [
-            (c * members + s, (1 - c) * members + s + 1)
-            for c in range(2)
-            for s in range(members - 1)
-        ],
-    )
+    edges = lax.ppermute(tokens[:, -EDGE:], SEQ, [(s, s + 1) for s in range(members - 1)])
+    rows = jnp.concatenate([edges, tokens], axis=1)
+    mine = jnp.where(core == 0, rows[0], rows[1])
+    given = lax.ppermute(jnp.where(core == 0, rows[1], rows[0]), "core", SWAP)
 
     def joined(left, right):
         return jnp.where(
             core == 0, jnp.concatenate([left, right], 1), jnp.concatenate([right, left], 1)
         )
 
-    piece, edge = joined(mine, given), joined(mine_edge, given_edge)
+    joint = joined(mine, given)
+    piece, edge = joint[EDGE:], joint[:EDGE]
     kept = None
     for turn in range(sections):
         own = layer(piece, edge, weights)

time: 183 us -> 181 us (0.989)
  waiting for transfers between devices: 53.7 us -> 45.7 us
  starting transfers between devices: 48.2 us -> 54.8 us
  Pallas kernels: 36.1 us -> 33.6 us
  blocking collectives: 39.7 us -> 42 us
    ppermute x17 -> x16, waiting for transfers between devices: 15.5 us -> 3.8 us  [the longest x6 2.02 us: moved(): return lax.ppermute(spread_rows, 'chip', ring(count, step))]
    ppermute x17 -> x16, starting transfers between devices: 24.9 us -> 32.4 us  [the longest x8 18.6 us: layer(): other = {k: lax.ppermute(part, 'core', SWAP) for k, part in own.items()}]
    ppermute x2, waiting for transfers between devices: 0.01 us -> 3.78 us  [layer(): taken = lax.ppermute(given, 'core', SWAP)]
    pallas_call x16, Pallas kernels: 36.1 us -> 33.6 us  [local(): pl.pallas_call(body, out_shape=[jax.ShapeDtypeStruct(shape, kind) for sha...]
    all_to_all x2, blocking collectives: 39.7 us -> 42 us  [layer(): lax.all_to_all(sent.reshape(members, tall // members, -1), SEQ, 0, 0, til...]
  transfers between devices with their start and end apart: 30 -> 29, of which waited for: 16 -> 16; matrix products, arithmetic and copies ran while one was open for 0% -> 0% of each run, Pallas kernels for 8% -> 7%
where the time goes in v3:
time: 181 us
  starting transfers between devices  54.8 us (30%)
  waiting for transfers between devices  45.7 us (25%)
  blocking collectives  42 us (23%)
  Pallas kernels  33.6 us (19%)
  local copies, waits for them, and re-layouts  3.63 us (2%)
    all_to_all x2, blocking collectives, layer(): lax.all_to_all(sent.reshape(members, tall // members, -1), SEQ, 0, 0, til...  42 us
    pallas_call x16, Pallas kernels, local(): pl.pallas_call(body, out_shape=[jax.ShapeDtypeStruct(shape, kind) for sha...  33.6 us
    ppermute x8, starting transfers between devices, layer(): other = {k: lax.ppermute(part, 'core', SWAP) for k, part in own.items()}  18.6 us
    ppermute x6, waiting for transfers between devices, layer(): lax.ppermute(part, 'chip', ring(count, k + 1))  16.5 us
    all_to_all x2, waiting for transfers between devices, layer(): back = lax.all_to_all(back, SEQ, 0, 0, tiled=True)  15.2 us
    ppermute x6, starting transfers between devices, moved(): return lax.ppermute(spread_rows, 'chip', ring(count, step))  9.36 us
    all_to_all x2, starting transfers between devices, layer(): back = lax.all_to_all(back, SEQ, 0, 0, tiled=True)  8.34 us
    ppermute x1, waiting for transfers between devices, shards(): piece = lax.ppermute(own, 'pipe', [(s, s + 1) for s in range(sections - 1)])  5.56 us
  transfers between devices with their start and end apart: 29, of which 16 were waited for; matrix products, arithmetic and copies ran while one was open for 0% of the time, Pallas kernels for 7%

profile of v3, /device:TPU:5, one launch (start us, length us, event | category | flops | bytes accessed | tf_op | source)
XLA Modules:
  0.0 180.6 jit_solution(2059563654175068771)
XLA Ops:
  1.2 2.8 %collective-permute-start = (bf16[2,8,320]{2,1,0:T(8,128)(2,1)S(1)}, bf16[2,8,320]{2,1,0:T(8,128)(2,1)S(1)}, u32[]{:S(2)}, u32[]{:S(2)}) collective-permute-start(bf16[2,8,320]{2,1,0:T(8,128)(2,1)S(1)} %slice.32), channel_id=1, source_target_pairs={{0,1},{1,2},{2,3},{3,4},{4,5},{5,6},{6,7},{7,8},{8,9},{9,10},{10,1... | collective-permute-start | bytes 30728 | tf_op jit(solution)/shard_map/ppermute | solution.py:526
  7.6 2.8 %collective-permute-start.4 = (bf16[136,640]{1,0:T(8,128)(2,1)S(1)}, bf16[136,640]{1,0:T(8,128)(2,1)S(1)}, u32[]{:S(2)}, u32[]{:S(2)}) collective-permute-start(bf16[136,640]{1,0:T(8,128)(2,1)S(1)} %maximum_select_fusion.1.refs_0_), channel_id=1, source_target_pairs={{0,96},{32,0},{64,32},{96,64},{1,97},{33,1},{65,33},{97,65},{2,98}... | collective-permute-start | bytes 522248 | tf_op jit(solution)/shard_map/ppermute | solution.py:400
  13.8 5.0 %collective-permute-start.7 = (bf16[136,640]{1,0:T(8,128)(2,1)S(1)}, bf16[136,640]{1,0:T(8,128)(2,1)S(1)}, u32[]{:S(2)}, u32[]{:S(2)}) collective-permute-start(bf16[136,640]{1,0:T(8,128)(2,1)S(1)} %collective-permute-done.4.refs_2_), channel_id=1, source_target_pairs={{0,16},{16,0},{1,17},{17,1},{2,18},{18,2},{3,19},{19,3},{4,20},{20... | collective-permute-start | bytes 522248 | tf_op jit(solution)/shard_map/ppermute | solution.py:406
  18.8 3.4 %collective-permute-start.6 = (bf16[136,640]{1,0:T(8,128)(2,1)S(1)}, bf16[136,640]{1,0:T(8,128)(2,1)S(1)}, u32[]{:S(2)}, u32[]{:S(2)}) collective-permute-start(bf16[136,640]{1,0:T(8,128)(2,1)S(1)} %collective-permute-done.3.refs_1_), channel_id=1, source_target_pairs={{0,16},{16,0},{1,17},{17,1},{2,18},{18,2},{3,19},{19,3},{4,20},{20... | collective-permute-start | bytes 522248 | tf_op jit(solution)/shard_map/ppermute | solution.py:406
  23.8 2.0 %shard_map.127 = (bf16[1,272,640]{2,1,0:T(8,128)(2,1)S(1)}, f32[272,128]{1,0:T(8,128)S(1)}, f32[272,10]{1,0:T(8,128)S(1)}, f32[272,256]{1,0:T(8,128)S(1)}, f32[272,640]{1,0:T(8,128)S(1)}) custom-call(bf16[136,640]{1,0:T(8,128)(2,1)S(1)} %maximum_select_fusion.1.refs_0_, bf16[136,640]{1,0:T(8,128)(2,1)S(1)} %collective-permute-done.8.refs_1_, ...), custom_call_target="tpu_custom_call" | custom-call | flops 268435456 | bytes 4194304 | tf_op jit(solution)/shard_map/pallas_call | solution.py:43
  25.9 5.7 %shard_map.128 = (bf16[3,272,640]{2,1,0:T(8,128)(2,1)S(1)}, f32[256,128]{1,0:T(8,128)S(1)}, bf16[2,128,640]{2,1,0:T(8,128)(2,1)S(1)}, bf16[2,128,256]{2,1,0:T(8,...) custom-call(bf16[136,640]{1,0:T(8,128)(2,1)S(1)} %collective-permute-done.2.refs_0, ...), custom_call_target="tpu_custom_call" | custom-call | flops 268435456 | bytes 4194304 | tf_op jit(solution)/shard_map/pallas_call | solution.py:43
  31.6 24.8 %all_to_all.20.arrived = bf16[16,16,768]{2,1,0:T(8,128)(2,1)S(1)} all-to-all(bf16[16,16,768]{2,1,0:T(8,128)(2,1)S(1)} %bitcast.28), channel_id=1, replica_groups=mesh['pipe'=2,'chip'=4,'core'=2,'seq_0'=8,'seq_1'=2] {'seq_0','seq_1'}, dimensions={0} | all-to-all | bytes 786432 | tf_op jit(solution)/shard_map/all_to_all | solution.py:456
  57.4 4.2 %all-to-all-start.1 = ((bf16[16,16,640]{2,1,0:T(8,128)(2,1)}), bf16[16,16,640]{2,1,0:T(8,128)(2,1)S(1)}, u32[]{:S(2)}, u32[]{:S(2)}) async-start(bf16[16,16,640]{2,1,0:T(8,128)(2,1)} %shard_map.131), calls=%async_computation.1 | async-start | bytes 655360 | tf_op jit(solution)/shard_map/all_to_all | solution.py:472
  61.7 3.2 %shard_map.129.gate = f32[256,640]{1,0:T(8,128)S(1)} custom-call(bf16[1,272,640]{2,1,0:T(8,128)(2,1)S(1)} %get-tuple-element.53.near, bf16[3,272,640]{2,1,0:T(8,128)(2,1)S(1)} %get-tuple-element.54.far, f32[256,128]{1,0:T(8,128)S(1)} %get-tuple-element.55.scales, bf16[2560,640]{1,0:T(8,128)(2,1)} %bitcast.48), custom_call_target="tpu_custom_call" | custom-call | flops 268435456 | bytes 4194304 | tf_op jit(solution)/shard_map/pallas_call | solution.py:43
  65.8 7.6 %all-to-all-done.1 = bf16[16,16,640]{2,1,0:T(8,128)(2,1)S(1)} async-done(((bf16[16,16,640]{2,1,0:T(8,128)(2,1)}), bf16[16,16,640]{2,1,0:T(8,128)(2,1)S(1)}, u32[]{:S(2)}, u32[]{:S(2)}) %all-to-all-start.1) | async-done | bytes 327712 | tf_op jit(solution)/shard_map/all_to_all | solution.py:472
  73.4 4.0 %shard_map.132 = (bf16[4,136,640]{2,1,0:T(8,128)(2,1)S(1)}, bf16[4,136,640]{2,1,0:T(8,128)(2,1)}) custom-call(f32[2,128,640]{2,1,0:T(8,128)S(1)} %get-tuple-element.56.base, f32[2,128,640]{2,1,0:T(8,128)S(1)} %get-tuple-element.57.ahead, bf16[2,128,256]{2,1,0:T(8,128)(2,1)S(1)} %get-tuple-element.50.maps, bf16[2,128,640]{2,1,0:T(8,128)(2,1)S(1)} %bitcast.22, ...), custom_call_target="tpu_custom_call" | custom-call | flops 268435456 | bytes 4194304 | tf_op jit(solution)/shard_map/pallas_call | solution.py:43
  77.4 2.5 %collective-permute-start.9 = (bf16[4,136,640]{2,1,0:T(8,128)(2,1)}, bf16[4,136,640]{2,1,0:T(8,128)(2,1)S(1)}, u32[]{:S(2)}, u32[]{:S(2)}) collective-permute-start(bf16[4,136,640]{2,1,0:T(8,128)(2,1)} %get-tuple-element.60), channel_id=1, source_target_pairs={{0,16},{16,0},{1,17},{17,1},{2,18},{18,2},{3,19},{19,3},{4,20},{20... | collective-permute-start | bytes 2088968 | tf_op jit(solution)/shard_map/ppermute | solution.py:481
  79.9 2.0 %collective-permute-done.9.arrived = bf16[4,136,640]{2,1,0:T(8,128)(2,1)S(1)} collective-permute-done((bf16[4,136,640]{2,1,0:T(8,128)(2,1)}, bf16[4,136,640]{2,1,0:T(8,128)(2,1)S(1)}, u32[]{:S(2)}, u32[]{:S(2)}) %collective-permute-start.9) | collective-permute-done | bytes 696352 | tf_op jit(solution)/shard_map/ppermute | solution.py:481
  82.2 1.9 %collective-permute-start.11 = (bf16[136,640]{1,0:T(8,128)(2,1)S(1)}, bf16[136,640]{1,0:T(8,128)(2,1)S(1)}, u32[]{:S(2)}, u32[]{:S(2)}) collective-permute-start(bf16[136,640]{1,0:T(8,128)(2,1)S(1)} %get-tuple-element.63), channel_id=1, source_target_pairs={{0,64},{32,96},{64,0},{96,32},{1,65},{33,97},{65,1},{97,33},{2,66}... | collective-permute-start | bytes 522248 | tf_op jit(solution)/shard_map/ppermute | solution.py:488
  84.9 4.9 %collective-permute-done.10.refs_0_ = bf16[136,640]{1,0:T(8,128)(2,1)S(1)} collective-permute-done((bf16[136,640]{1,0:T(8,128)(2,1)S(1)}, bf16[136,640]{1,0:T(8,128)(2,1)S(1)}, u32[]{:S(2)}, u32[]{:S(2)}) %collective-permute-start.10) | collective-permute-done | bytes 174112 | tf_op jit(solution)/shard_map/ppermute | solution.py:488
  89.8 2.2 %collective-permute-done.11.refs_1_ = bf16[136,640]{1,0:T(8,128)(2,1)S(1)} collective-permute-done((bf16[136,640]{1,0:T(8,128)(2,1)S(1)}, bf16[136,640]{1,0:T(8,128)(2,1)S(1)}, u32[]{:S(2)}, u32[]{:S(2)}) %collective-permute-start.11) | collective-permute-done | bytes 174112 | tf_op jit(solution)/shard_map/ppermute | solution.py:488
  95.3 5.6 %collective-permute-done.13.piece = bf16[128,640]{1,0:T(8,128)(2,1)S(1)} collective-permute-done((bf16[128,640]{1,0:T(8,128)(2,1)S(1)}, bf16[128,640]{1,0:T(8,128)(2,1)S(1)}, u32[]{:S(2)}, u32[]{:S(2)}) %collective-permute-start.13) | collective-permute-done | bytes 163872 | tf_op jit(solution)/shard_map/ppermute | solution.py:543
  100.9 3.6 %collective-permute-start.17 = (bf16[136,640]{1,0:T(8,128)(2,1)S(1)}, bf16[136,640]{1,0:T(8,128)(2,1)S(1)}, u32[]{:S(2)}, u32[]{:S(2)}) collective-permute-start(bf16[136,640]{1,0:T(8,128)(2,1)S(1)} %constant_dynamic-update-slice_fusion.refs_0_), channel_id=1, source_target_pairs={{0,96},{32,0},{64,32},{96,64},{1,97},{33,1},{65,33},{97,65},{2,98}... | collective-permute-start | bytes 522248 | tf_op jit(solution)/shard_map/ppermute | solution.py:400
  105.8 2.2 %collective-permute-start.21 = (bf16[136,640]{1,0:T(8,128)(2,1)S(1)}, bf16[136,640]{1,0:T(8,128)(2,1)S(1)}, u32[]{:S(2)}, u32[]{:S(2)}) collective-permute-start(bf16[136,640]{1,0:T(8,128)(2,1)S(1)} %constant_dynamic-update-slice_fusion.refs_0_), channel_id=1, source_target_pairs={{0,16},{16,0},{1,17},{17,1},{2,18},{18,2},{3,19},{19,3},{4,20},{20... | collective-permute-start | bytes 522248 | tf_op jit(solution)/shard_map/ppermute | solution.py:406
  108.0 5.2 %collective-permute-start.20 = (bf16[136,640]{1,0:T(8,128)(2,1)S(1)}, bf16[136,640]{1,0:T(8,128)(2,1)S(1)}, u32[]{:S(2)}, u32[]{:S(2)}) collective-permute-start(bf16[136,640]{1,0:T(8,128)(2,1)S(1)} %collective-permute-done.17.refs_2_), channel_id=1, source_target_pairs={{0,16},{16,0},{1,17},{17,1},{2,18},{18,2},{3,19},{19,3},{4,20},{20... | collective-permute-start | bytes 522248 | tf_op jit(solution)/shard_map/ppermute | solution.py:406
  116.3 2.0 %shard_map.135 = (bf16[1,272,640]{2,1,0:T(8,128)(2,1)S(1)}, f32[272,128]{1,0:T(8,128)S(1)}, f32[272,10]{1,0:T(8,128)S(1)}, f32[272,256]{1,0:T(8,128)S(1)}, f32[272,640]{1,0:T(8,128)S(1)}) custom-call(bf16[136,640]{1,0:T(8,128)(2,1)S(1)} %constant_dynamic-update-slice_fusion.refs_0_, bf16[136,640]{1,0:T(8,128)(2,1)S(1)} %collective-permute-done.21.refs_1_, ...), custom_call_target="tpu_custom_call" | custom-call | flops 268435456 | bytes 4194304 | tf_op jit(solution)/shard_map/pallas_call | solution.py:43
  118.3 5.7 %shard_map.136 = (bf16[3,272,640]{2,1,0:T(8,128)(2,1)S(1)}, f32[256,128]{1,0:T(8,128)S(1)}, bf16[2,128,640]{2,1,0:T(8,128)(2,1)S(1)}, bf16[2,128,256]{2,1,0:T(8,...) custom-call(bf16[136,640]{1,0:T(8,128)(2,1)S(1)} %collective-permute-done.15.refs_, ...), custom_call_target="tpu_custom_call" | custom-call | flops 268435456 | bytes 4194304 | tf_op jit(solution)/shard_map/pallas_call | solution.py:43
  124.0 17.2 %all_to_all.21.arrived = bf16[16,16,768]{2,1,0:T(8,128)(2,1)S(1)} all-to-all(bf16[16,16,768]{2,1,0:T(8,128)(2,1)S(1)} %bitcast.29), channel_id=1, replica_groups=mesh['pipe'=2,'chip'=4,'core'=2,'seq_0'=8,'seq_1'=2] {'seq_0','seq_1'}, dimensions={0} | all-to-all | bytes 786432 | tf_op jit(solution)/shard_map/all_to_all | solution.py:456
  142.3 4.1 %all-to-all-start.3 = ((bf16[16,16,640]{2,1,0:T(8,128)(2,1)}), bf16[16,16,640]{2,1,0:T(8,128)(2,1)S(1)}, u32[]{:S(2)}, u32[]{:S(2)}) async-start(bf16[16,16,640]{2,1,0:T(8,128)(2,1)} %shard_map.139), calls=%async_computation.3 | async-start | bytes 655360 | tf_op jit(solution)/shard_map/all_to_all | solution.py:472
  146.4 3.2 %shard_map.137.gate = f32[256,640]{1,0:T(8,128)S(1)} custom-call(bf16[1,272,640]{2,1,0:T(8,128)(2,1)S(1)} %get-tuple-element.73.near, bf16[3,272,640]{2,1,0:T(8,128)(2,1)S(1)} %get-tuple-element.74.far, f32[256,128]{1,0:T(8,128)S(1)} %get-tuple-element.75.scales, bf16[2560,640]{1,0:T(8,128)(2,1)} %bitcast.49), custom_call_target="tpu_custom_call" | custom-call | flops 268435456 | bytes 4194304 | tf_op jit(solution)/shard_map/pallas_call | solution.py:43
  150.5 7.6 %all-to-all-done.3 = bf16[16,16,640]{2,1,0:T(8,128)(2,1)S(1)} async-done(((bf16[16,16,640]{2,1,0:T(8,128)(2,1)}), bf16[16,16,640]{2,1,0:T(8,128)(2,1)S(1)}, u32[]{:S(2)}, u32[]{:S(2)}) %all-to-all-start.3) | async-done | bytes 327712 | tf_op jit(solution)/shard_map/all_to_all | solution.py:472
  158.1 3.3 %shard_map.140 = (bf16[4,136,640]{2,1,0:T(8,128)(2,1)S(1)}, bf16[4,136,640]{2,1,0:T(8,128)(2,1)S(1)}) custom-call(f32[2,128,640]{2,1,0:T(8,128)S(1)} %get-tuple-element.76.base, f32[2,128,640]{2,1,0:T(8,128)S(1)} %get-tuple-element.77.ahead, bf16[2,128,256]{2,1,0:T(8,128)(2,1)S(1)} %get-tuple-element.70.maps, bf16[2,128,640]{2,1,0:T(8,128)(2,1)S(1)} %bitcast.23, ...), custom_call_target="tpu_custom_call" | custom-call | flops 268435456 | bytes 4194304 | tf_op jit(solution)/shard_map/pallas_call | solution.py:43
  161.4 2.5 %collective-permute-start.22 = (bf16[4,136,640]{2,1,0:T(8,128)(2,1)S(1)}, bf16[4,136,640]{2,1,0:T(8,128)(2,1)S(1)}, u32[]{:S(2)}, u32[]{:S(2)}) collective-permute-start(bf16[4,136,640]{2,1,0:T(8,128)(2,1)S(1)} %get-tuple-element.80), channel_id=1, source_target_pairs={{0,16},{16,0},{1,17},{17,1},{2,18},{18,2},{3,19},{19,3},{4,20},{20... | collective-permute-start | bytes 2088968 | tf_op jit(solution)/shard_map/ppermute | solution.py:481
  164.0 1.8 collective-permute-done.22.arrived
  166.0 1.9 %collective-permute-start.24 = (bf16[136,640]{1,0:T(8,128)(2,1)S(1)}, bf16[136,640]{1,0:T(8,128)(2,1)S(1)}, u32[]{:S(2)}, u32[]{:S(2)}) collective-permute-start(bf16[136,640]{1,0:T(8,128)(2,1)S(1)} %get-tuple-element.83), channel_id=1, source_target_pairs={{0,64},{32,96},{64,0},{96,32},{1,65},{33,97},{65,1},{97,33},{2,66}... | collective-permute-start | bytes 522248 | tf_op jit(solution)/shard_map/ppermute | solution.py:488
  168.7 4.9 %collective-permute-done.23.refs_0_ = bf16[136,640]{1,0:T(8,128)(2,1)S(1)} collective-permute-done((bf16[136,640]{1,0:T(8,128)(2,1)S(1)}, bf16[136,640]{1,0:T(8,128)(2,1)S(1)}, u32[]{:S(2)}, u32[]{:S(2)}) %collective-permute-start.23) | collective-permute-done | bytes 174112 | tf_op jit(solution)/shard_map/ppermute | solution.py:488
  173.6 2.2 %collective-permute-done.24.refs_1_ = bf16[136,640]{1,0:T(8,128)(2,1)S(1)} collective-permute-done((bf16[136,640]{1,0:T(8,128)(2,1)S(1)}, bf16[136,640]{1,0:T(8,128)(2,1)S(1)}, u32[]{:S(2)}, u32[]{:S(2)}) %collective-permute-start.24) | collective-permute-done | bytes 174112 | tf_op jit(solution)/shard_map/ppermute | solution.py:488
  (76 shorter events, 28.0 us)
Async XLA Ops:
  0.0 25.8 %copy-start.8 = (f32[1,10]{1,0:T(1,128)S(1)}, f32[1,10]{1,0:T(1,128)}, u32[]{:S(2)}) copy-start(f32[1,10]{1,0:T(1,128)} %refs_14_.3) | copy-start | bytes 124
  0.0 25.8 %copy-start.5 = (f32[1,5,256]{2,0,1:T(1,128)S(1)}, f32[1,5,256]{2,0,1:T(1,128)}, u32[]{:S(2)}) copy-start(f32[1,5,256]{2,0,1:T(1,128)} %param.20) | copy-start | bytes 15364
  0.0 25.8 %copy-start.4 = (f32[1,5,640]{2,0,1:T(1,128)S(1)}, f32[1,5,640]{2,0,1:T(1,128)}, u32[]{:S(2)}) copy-start(f32[1,5,640]{2,0,1:T(1,128)} %param.19) | copy-start | bytes 38404
  1.2 3.6 %collective-permute-start = (bf16[2,8,320]{2,1,0:T(8,128)(2,1)S(1)}, bf16[2,8,320]{2,1,0:T(8,128)(2,1)S(1)}, u32[]{:S(2)}, u32[]{:S(2)}) collective-permute-start(bf16[2,8,320]{2,1,0:T(8,128)(2,1)S(1)} %slice.32), channel_id=1, source_target_pairs={{0,1},{1,2},{2,3},{3,4},{4,5},{5,6},{6,7},{7,8},{8,9},{9,10},{10,1... | collective-permute-start | bytes 30728 | tf_op jit(solution)/shard_map/ppermute | solution.py:526
  4.9 2.6 %collective-permute-start.1 = (bf16[136,320]{1,0:T(8,128)(2,1)S(1)}, bf16[136,320]{1,0:T(8,128)(2,1)S(1)}, u32[]{:S(2)}, u32[]{:S(2)}) collective-permute-start(bf16[136,320]{1,0:T(8,128)(2,1)S(1)} %get-tuple-element.86), channel_id=1, source_target_pairs={{0,16},{16,0},{1,17},{17,1},{2,18},{18,2},{3,19},{19,3},{4,20},{20... | collective-permute-start | bytes 261128 | tf_op jit(solution)/shard_map/ppermute | solution.py:529
  7.6 6.2 %collective-permute-start.4 = (bf16[136,640]{1,0:T(8,128)(2,1)S(1)}, bf16[136,640]{1,0:T(8,128)(2,1)S(1)}, u32[]{:S(2)}, u32[]{:S(2)}) collective-permute-start(bf16[136,640]{1,0:T(8,128)(2,1)S(1)} %maximum_select_fusion.1.refs_0_), channel_id=1, source_target_pairs={{0,96},{32,0},{64,32},{96,64},{1,97},{33,1},{65,33},{97,65},{2,98}... | collective-permute-start | bytes 522248 | tf_op jit(solution)/shard_map/ppermute | solution.py:400
  10.4 8.4 %collective-permute-start.3 = (bf16[136,640]{1,0:T(8,128)(2,1)S(1)}, bf16[136,640]{1,0:T(8,128)(2,1)S(1)}, u32[]{:S(2)}, u32[]{:S(2)}) collective-permute-start(bf16[136,640]{1,0:T(8,128)(2,1)S(1)} %maximum_select_fusion.1.refs_0_), channel_id=1, source_target_pairs={{0,32},{32,64},{64,96},{96,0},{1,33},{33,65},{65,97},{97,1},{2,34}... | collective-permute-start | bytes 522248 | tf_op jit(solution)/shard_map/ppermute | solution.py:400
  10.4 11.8 %collective-permute-start.2 = (bf16[136,640]{1,0:T(8,128)(2,1)S(1)}, bf16[136,640]{1,0:T(8,128)(2,1)S(1)}, u32[]{:S(2)}, u32[]{:S(2)}) collective-permute-start(bf16[136,640]{1,0:T(8,128)(2,1)S(1)} %maximum_select_fusion.1.refs_0_), channel_id=1, source_target_pairs={{0,64},{32,96},{64,0},{96,32},{1,65},{33,97},{65,1},{97,33},{2,66}... | collective-permute-start | bytes 522248 | tf_op jit(solution)/shard_map/ppermute | solution.py:400
  12.1 10.1 %collective-permute-start.8 = (bf16[136,640]{1,0:T(8,128)(2,1)S(1)}, bf16[136,640]{1,0:T(8,128)(2,1)S(1)}, u32[]{:S(2)}, u32[]{:S(2)}) collective-permute-start(bf16[136,640]{1,0:T(8,128)(2,1)S(1)} %maximum_select_fusion.1.refs_0_), channel_id=1, source_target_pairs={{0,16},{16,0},{1,17},{17,1},{2,18},{18,2},{3,19},{19,3},{4,20},{20... | collective-permute-start | bytes 522248 | tf_op jit(solution)/shard_map/ppermute | solution.py:406
  13.8 12.0 %collective-permute-start.7 = (bf16[136,640]{1,0:T(8,128)(2,1)S(1)}, bf16[136,640]{1,0:T(8,128)(2,1)S(1)}, u32[]{:S(2)}, u32[]{:S(2)}) collective-permute-start(bf16[136,640]{1,0:T(8,128)(2,1)S(1)} %collective-permute-done.4.refs_2_), channel_id=1, source_target_pairs={{0,16},{16,0},{1,17},{17,1},{2,18},{18,2},{3,19},{19,3},{4,20},{20... | collective-permute-start | bytes 522248 | tf_op jit(solution)/shard_map/ppermute | solution.py:406
  18.8 7.0 %collective-permute-start.6 = (bf16[136,640]{1,0:T(8,128)(2,1)S(1)}, bf16[136,640]{1,0:T(8,128)(2,1)S(1)}, u32[]{:S(2)}, u32[]{:S(2)}) collective-permute-start(bf16[136,640]{1,0:T(8,128)(2,1)S(1)} %collective-permute-done.3.refs_1_), channel_id=1, source_target_pairs={{0,16},{16,0},{1,17},{17,1},{2,18},{18,2},{3,19},{19,3},{4,20},{20... | collective-permute-start | bytes 522248 | tf_op jit(solution)/shard_map/ppermute | solution.py:406
  22.2 3.6 %collective-permute-start.5 = (bf16[136,640]{1,0:T(8,128)(2,1)S(1)}, bf16[136,640]{1,0:T(8,128)(2,1)S(1)}, u32[]{:S(2)}, u32[]{:S(2)}) collective-permute-start(bf16[136,640]{1,0:T(8,128)(2,1)S(1)} %collective-permute-done.2.refs_0_), channel_id=1, source_target_pairs={{0,16},{16,0},{1,17},{17,1},{2,18},{18,2},{3,19},{19,3},{4,20},{20... | collective-permute-start | bytes 522248 | tf_op jit(solution)/shard_map/ppermute | solution.py:406
  57.4 16.0 %all-to-all-start.1 = ((bf16[16,16,640]{2,1,0:T(8,128)(2,1)}), bf16[16,16,640]{2,1,0:T(8,128)(2,1)S(1)}, u32[]{:S(2)}, u32[]{:S(2)}) async-start(bf16[16,16,640]{2,1,0:T(8,128)(2,1)} %shard_map.131), calls=%async_computation.1 | async-start | bytes 655360 | tf_op jit(solution)/shard_map/all_to_all | solution.py:472
  77.4 4.5 %collective-permute-start.9 = (bf16[4,136,640]{2,1,0:T(8,128)(2,1)}, bf16[4,136,640]{2,1,0:T(8,128)(2,1)S(1)}, u32[]{:S(2)}, u32[]{:S(2)}) collective-permute-start(bf16[4,136,640]{2,1,0:T(8,128)(2,1)} %get-tuple-element.60), channel_id=1, source_target_pairs={{0,16},{16,0},{1,17},{17,1},{2,18},{18,2},{3,19},{19,3},{4,20},{20... | collective-permute-start | bytes 2088968 | tf_op jit(solution)/shard_map/ppermute | solution.py:481
  82.1 7.7 %collective-permute-start.10 = (bf16[136,640]{1,0:T(8,128)(2,1)S(1)}, bf16[136,640]{1,0:T(8,128)(2,1)S(1)}, u32[]{:S(2)}, u32[]{:S(2)}) collective-permute-start(bf16[136,640]{1,0:T(8,128)(2,1)S(1)} %get-tuple-element.62), channel_id=1, source_target_pairs={{0,32},{32,64},{64,96},{96,0},{1,33},{33,65},{65,97},{97,1},{2,34}... | collective-permute-start | bytes 522248 | tf_op jit(solution)/shard_map/ppermute | solution.py:488
  82.2 9.8 %collective-permute-start.11 = (bf16[136,640]{1,0:T(8,128)(2,1)S(1)}, bf16[136,640]{1,0:T(8,128)(2,1)S(1)}, u32[]{:S(2)}, u32[]{:S(2)}) collective-permute-start(bf16[136,640]{1,0:T(8,128)(2,1)S(1)} %get-tuple-element.63), channel_id=1, source_target_pairs={{0,64},{32,96},{64,0},{96,32},{1,65},{33,97},{65,1},{97,33},{2,66}... | collective-permute-start | bytes 522248 | tf_op jit(solution)/shard_map/ppermute | solution.py:488
  84.1 9.0 %collective-permute-start.12 = (bf16[136,640]{1,0:T(8,128)(2,1)S(1)}, bf16[136,640]{1,0:T(8,128)(2,1)S(1)}, u32[]{:S(2)}, u32[]{:S(2)}) collective-permute-start(bf16[136,640]{1,0:T(8,128)(2,1)S(1)} %get-tuple-element.64), channel_id=1, source_target_pairs={{0,96},{32,0},{64,32},{96,64},{1,97},{33,1},{65,33},{97,65},{2,98}... | collective-permute-start | bytes 522248 | tf_op jit(solution)/shard_map/ppermute | solution.py:488
  93.3 7.6 %collective-permute-start.13 = (bf16[128,640]{1,0:T(8,128)(2,1)S(1)}, bf16[128,640]{1,0:T(8,128)(2,1)S(1)}, u32[]{:S(2)}, u32[]{:S(2)}) collective-permute-start(bf16[128,640]{1,0:T(8,128)(2,1)S(1)} %shard_map.134), channel_id=1, source_target_pairs={{0,128},{1,129},{2,130},{3,131},{4,132},{5,133},{6,134},{7,135},{8... | collective-permute-start | bytes 491528 | tf_op jit(solution)/shard_map/ppermute | solution.py:543
  94.6 0.7 collective-permute-start.14
  100.9 7.1 %collective-permute-start.17 = (bf16[136,640]{1,0:T(8,128)(2,1)S(1)}, bf16[136,640]{1,0:T(8,128)(2,1)S(1)}, u32[]{:S(2)}, u32[]{:S(2)}) collective-permute-start(bf16[136,640]{1,0:T(8,128)(2,1)S(1)} %constant_dynamic-update-slice_fusion.refs_0_), channel_id=1, source_target_pairs={{0,96},{32,0},{64,32},{96,64},{1,97},{33,1},{65,33},{97,65},{2,98}... | collective-permute-start | bytes 522248 | tf_op jit(solution)/shard_map/ppermute | solution.py:400
  104.5 10.1 %collective-permute-start.16 = (bf16[136,640]{1,0:T(8,128)(2,1)S(1)}, bf16[136,640]{1,0:T(8,128)(2,1)S(1)}, u32[]{:S(2)}, u32[]{:S(2)}) collective-permute-start(bf16[136,640]{1,0:T(8,128)(2,1)S(1)} %constant_dynamic-update-slice_fusion.refs_0_), channel_id=1, source_target_pairs={{0,32},{32,64},{64,96},{96,0},{1,33},{33,65},{65,97},{97,1},{2,34}... | collective-permute-start | bytes 522248 | tf_op jit(solution)/shard_map/ppermute | solution.py:400
  104.5 11.8 %collective-permute-start.15 = (bf16[136,640]{1,0:T(8,128)(2,1)S(1)}, bf16[136,640]{1,0:T(8,128)(2,1)S(1)}, u32[]{:S(2)}, u32[]{:S(2)}) collective-permute-start(bf16[136,640]{1,0:T(8,128)(2,1)S(1)} %constant_dynamic-update-slice_fusion.refs_0_), channel_id=1, source_target_pairs={{0,64},{32,96},{64,0},{96,32},{1,65},{33,97},{65,1},{97,33},{2,66}... | collective-permute-start | bytes 522248 | tf_op jit(solution)/shard_map/ppermute | solution.py:400
  105.8 10.5 %collective-permute-start.21 = (bf16[136,640]{1,0:T(8,128)(2,1)S(1)}, bf16[136,640]{1,0:T(8,128)(2,1)S(1)}, u32[]{:S(2)}, u32[]{:S(2)}) collective-permute-start(bf16[136,640]{1,0:T(8,128)(2,1)S(1)} %constant_dynamic-update-slice_fusion.refs_0_), channel_id=1, source_target_pairs={{0,16},{16,0},{1,17},{17,1},{2,18},{18,2},{3,19},{19,3},{4,20},{20... | collective-permute-start | bytes 522248 | tf_op jit(solution)/shard_map/ppermute | solution.py:406
  108.0 10.3 %collective-permute-start.20 = (bf16[136,640]{1,0:T(8,128)(2,1)S(1)}, bf16[136,640]{1,0:T(8,128)(2,1)S(1)}, u32[]{:S(2)}, u32[]{:S(2)}) collective-permute-start(bf16[136,640]{1,0:T(8,128)(2,1)S(1)} %collective-permute-done.17.refs_2_), channel_id=1, source_target_pairs={{0,16},{16,0},{1,17},{17,1},{2,18},{18,2},{3,19},{19,3},{4,20},{20... | collective-permute-start | bytes 522248 | tf_op jit(solution)/shard_map/ppermute | solution.py:406
  114.6 3.7 %collective-permute-start.19 = (bf16[136,640]{1,0:T(8,128)(2,1)S(1)}, bf16[136,640]{1,0:T(8,128)(2,1)S(1)}, u32[]{:S(2)}, u32[]{:S(2)}) collective-permute-start(bf16[136,640]{1,0:T(8,128)(2,1)S(1)} %collective-permute-done.16.refs_1_), channel_id=1, source_target_pairs={{0,16},{16,0},{1,17},{17,1},{2,18},{18,2},{3,19},{19,3},{4,20},{20... | collective-permute-start | bytes 522248 | tf_op jit(solution)/shard_map/ppermute | solution.py:406
  116.3 2.0 %collective-permute-start.18 = (bf16[136,640]{1,0:T(8,128)(2,1)S(1)}, bf16[136,640]{1,0:T(8,128)(2,1)S(1)}, u32[]{:S(2)}, u32[]{:S(2)}) collective-permute-start(bf16[136,640]{1,0:T(8,128)(2,1)S(1)} %collective-permute-done.15.refs_0_), channel_id=1, source_target_pairs={{0,16},{16,0},{1,17},{17,1},{2,18},{18,2},{3,19},{19,3},{4,20},{20... | collective-permute-start | bytes 522248 | tf_op jit(solution)/shard_map/ppermute | solution.py:406
  142.3 15.8 %all-to-all-start.3 = ((bf16[16,16,640]{2,1,0:T(8,128)(2,1)}), bf16[16,16,640]{2,1,0:T(8,128)(2,1)S(1)}, u32[]{:S(2)}, u32[]{:S(2)}) async-start(bf16[16,16,640]{2,1,0:T(8,128)(2,1)} %shard_map.139), calls=%async_computation.3 | async-start | bytes 655360 | tf_op jit(solution)/shard_map/all_to_all | solution.py:472
  161.4 4.3 %collective-permute-start.22 = (bf16[4,136,640]{2,1,0:T(8,128)(2,1)S(1)}, bf16[4,136,640]{2,1,0:T(8,128)(2,1)S(1)}, u32[]{:S(2)}, u32[]{:S(2)}) collective-permute-start(bf16[4,136,640]{2,1,0:T(8,128)(2,1)S(1)} %get-tuple-element.80), channel_id=1, source_target_pairs={{0,16},{16,0},{1,17},{17,1},{2,18},{18,2},{3,19},{19,3},{4,20},{20... | collective-permute-start | bytes 2088968 | tf_op jit(solution)/shard_map/ppermute | solution.py:481
  165.9 7.7 %collective-permute-start.23 = (bf16[136,640]{1,0:T(8,128)(2,1)S(1)}, bf16[136,640]{1,0:T(8,128)(2,1)S(1)}, u32[]{:S(2)}, u32[]{:S(2)}) collective-permute-start(bf16[136,640]{1,0:T(8,128)(2,1)S(1)} %get-tuple-element.82), channel_id=1, source_target_pairs={{0,32},{32,64},{64,96},{96,0},{1,33},{33,65},{65,97},{97,1},{2,34}... | collective-permute-start | bytes 522248 | tf_op jit(solution)/shard_map/ppermute | solution.py:488
  166.0 9.8 %collective-permute-start.24 = (bf16[136,640]{1,0:T(8,128)(2,1)S(1)}, bf16[136,640]{1,0:T(8,128)(2,1)S(1)}, u32[]{:S(2)}, u32[]{:S(2)}) collective-permute-start(bf16[136,640]{1,0:T(8,128)(2,1)S(1)} %get-tuple-element.83), channel_id=1, source_target_pairs={{0,64},{32,96},{64,0},{96,32},{1,65},{33,97},{65,1},{97,33},{2,66}... | collective-permute-start | bytes 522248 | tf_op jit(solution)/shard_map/ppermute | solution.py:488
  167.9 9.0 %collective-permute-start.25 = (bf16[136,640]{1,0:T(8,128)(2,1)S(1)}, bf16[136,640]{1,0:T(8,128)(2,1)S(1)}, u32[]{:S(2)}, u32[]{:S(2)}) collective-permute-start(bf16[136,640]{1,0:T(8,128)(2,1)S(1)} %get-tuple-element.84), channel_id=1, source_target_pairs={{0,96},{32,0},{64,32},{96,64},{1,97},{33,1},{65,33},{97,65},{2,98}... | collective-permute-start | bytes 522248 | tf_op jit(solution)/shard_map/ppermute | solution.py:488
  177.2 2.5 %collective-permute-start.26 = (bf16[128,320]{1,0:T(8,128)(2,1)S(1)}, bf16[128,320]{1,0:T(8,128)(2,1)S(1)}, u32[]{:S(2)}, u32[]{:S(2)}) collective-permute-start(bf16[128,320]{1,0:T(8,128)(2,1)S(1)} %get-tuple-element.88), channel_id=1, source_target_pairs={{0,16},{16,0},{1,17},{17,1},{2,18},{18,2},{3,19},{19,3},{4,20},{20... | collective-permute-start | bytes 245768 | tf_op jit(solution)/shard_map/ppermute | solution.py:555
  (7 other events, 98.3 us)

commit v4 on v3

--- a/solution.py
+++ b/solution.py
@@ -12,6 +12,7 @@
 NEAR = (0,)
 FAR = (2, 1, 3)
 SEQ = ("seq_0", "seq_1")
+CROSS = ("seq_1", "seq_0")
 TENSOR = ("chip", "core")
 SWAP = [(0, 1), (1, 0)]
 F32 = jnp.float32
@@ -299,7 +300,8 @@
     ends = arrived[:, :, width:].reshape(members * rows, arrived.shape[2] - width)
     factors = dot(ends, picks)
     running = jnp.zeros((rows, width), F32)
-    for s in range(members):
+    for position in range(members):
+        s = position % 2 * (members // 2) + position // 2
         back[s] = running.astype(BF16)
         factor = factors[s * rows : s * rows + 1] + factors[s * rows + 1 : s * rows + 2]
         running = running * factor + arrived[s, :, :width].astype(F32)
@@ -453,9 +455,7 @@
             *room(inner_weight, len(FAR), len(FAR) * block),
         ],
     )
-    arrived = lax.all_to_all(
-        sent.reshape(members, tall // members, -1), SEQ, 0, 0, tiled=True
-    )
+    arrived = lax.all_to_all(sent.reshape(members, tall // members, -1), CROSS, 0, 0, tiled=True)
     (gate,) = local(
         gate_project,
         [scaled, scaled_far, scales, gate_weight],
@@ -469,7 +469,7 @@
         [((2, rows, width), F32), ((2, rows, width), F32)],
     )
     (back,) = local(scan_states, [arrived], [((members, tall // members, width), BF16)])
-    back = lax.all_to_all(back, SEQ, 0, 0, tiled=True)
+    back = lax.all_to_all(back, CROSS, 0, 0, tiled=True)
     entering = back.reshape(2, rows, width)
     mine, given = local(
         output_terms,

time: 181 us -> 179 us (0.989)
  starting transfers between devices: 54.8 us -> 60.3 us
  waiting for transfers between devices: 45.7 us -> 40.8 us
  blocking collectives: 42 us -> 39.1 us
    all_to_all x2, waiting for transfers between devices: 15.2 us -> 10.4 us  [layer(): back = lax.all_to_all(back, CROSS, 0, 0, tiled=True)]
    all_to_all x2, starting transfers between devices: 8.34 us -> 12 us  [layer(): back = lax.all_to_all(back, CROSS, 0, 0, tiled=True)]
    all_to_all x2, blocking collectives: 42 us -> 39.1 us  [layer(): lax.all_to_all(sent.reshape(members, tall // members, -1), CROSS, 0, 0, t...]
where the time goes in v4:
time: 179 us; the launch traced here: 178 us
  starting transfers between devices  60.3 us (34%)
  waiting for transfers between devices  40.8 us (23%)
  blocking collectives  39.1 us (22%)
  Pallas kernels  33.7 us (19%)
  local copies, waits for them, and re-layouts  3.63 us (2%)
    all_to_all x2, blocking collectives, layer(): lax.all_to_all(sent.reshape(members, tall // members, -1), CROSS, 0, 0, t...  39.1 us
    pallas_call x16, Pallas kernels, local(): pl.pallas_call(body, out_shape=[jax.ShapeDtypeStruct(shape, kind) for sha...  33.7 us
    ppermute x8, starting transfers between devices, layer(): other = {k: lax.ppermute(part, 'core', SWAP) for k, part in own.items()}  18.5 us
    ppermute x6, waiting for transfers between devices, layer(): lax.ppermute(part, 'chip', ring(count, k + 1))  16.1 us
    all_to_all x2, starting transfers between devices, layer(): back = lax.all_to_all(back, CROSS, 0, 0, tiled=True)  12 us
    all_to_all x2, waiting for transfers between devices, layer(): back = lax.all_to_all(back, CROSS, 0, 0, tiled=True)  10.4 us
    ppermute x6, starting transfers between devices, moved(): return lax.ppermute(spread_rows, 'chip', ring(count, step))  9.85 us
    ppermute x2, starting transfers between devices, layer(): taken = lax.ppermute(given, 'core', SWAP)  6.22 us
  transfers between devices with their start and end apart: 29, of which 16 were waited for; matrix products, arithmetic and copies ran while one was open for 0% of the time, Pallas kernels for 7%

profile of v4, /device:TPU:5, one launch (start us, length us, event | category | flops | bytes accessed | tf_op | source)
XLA Modules:
  0.0 178.2 jit_solution(16472128082350781212)
XLA Ops:
  1.2 2.8 %collective-permute-start = (bf16[2,8,320]{2,1,0:T(8,128)(2,1)S(1)}, bf16[2,8,320]{2,1,0:T(8,128)(2,1)S(1)}, u32[]{:S(2)}, u32[]{:S(2)}) collective-permute-start(bf16[2,8,320]{2,1,0:T(8,128)(2,1)S(1)} %slice.32), channel_id=1, source_target_pairs={{0,1},{1,2},{2,3},{3,4},{4,5},{5,6},{6,7},{7,8},{8,9},{9,10},{10,1... | collective-permute-start | bytes 30728 | tf_op jit(solution)/shard_map/ppermute | solution.py:526
  7.6 2.8 %collective-permute-start.4 = (bf16[136,640]{1,0:T(8,128)(2,1)S(1)}, bf16[136,640]{1,0:T(8,128)(2,1)S(1)}, u32[]{:S(2)}, u32[]{:S(2)}) collective-permute-start(bf16[136,640]{1,0:T(8,128)(2,1)S(1)} %maximum_select_fusion.1.refs_0_), channel_id=1, source_target_pairs={{0,96},{32,0},{64,32},{96,64},{1,97},{33,1},{65,33},{97,65},{2,98}... | collective-permute-start | bytes 522248 | tf_op jit(solution)/shard_map/ppermute | solution.py:402
  13.8 5.0 %collective-permute-start.7 = (bf16[136,640]{1,0:T(8,128)(2,1)S(1)}, bf16[136,640]{1,0:T(8,128)(2,1)S(1)}, u32[]{:S(2)}, u32[]{:S(2)}) collective-permute-start(bf16[136,640]{1,0:T(8,128)(2,1)S(1)} %collective-permute-done.4.refs_2_), channel_id=1, source_target_pairs={{0,16},{16,0},{1,17},{17,1},{2,18},{18,2},{3,19},{19,3},{4,20},{20... | collective-permute-start | bytes 522248 | tf_op jit(solution)/shard_map/ppermute | solution.py:408
  18.8 3.4 %collective-permute-start.6 = (bf16[136,640]{1,0:T(8,128)(2,1)S(1)}, bf16[136,640]{1,0:T(8,128)(2,1)S(1)}, u32[]{:S(2)}, u32[]{:S(2)}) collective-permute-start(bf16[136,640]{1,0:T(8,128)(2,1)S(1)} %collective-permute-done.3.refs_1_), channel_id=1, source_target_pairs={{0,16},{16,0},{1,17},{17,1},{2,18},{18,2},{3,19},{19,3},{4,20},{20... | collective-permute-start | bytes 522248 | tf_op jit(solution)/shard_map/ppermute | solution.py:408
  23.8 2.0 %shard_map.127 = (bf16[1,272,640]{2,1,0:T(8,128)(2,1)S(1)}, f32[272,128]{1,0:T(8,128)S(1)}, f32[272,10]{1,0:T(8,128)S(1)}, f32[272,256]{1,0:T(8,128)S(1)}, f32[272,640]{1,0:T(8,128)S(1)}) custom-call(bf16[136,640]{1,0:T(8,128)(2,1)S(1)} %maximum_select_fusion.1.refs_0_, bf16[136,640]{1,0:T(8,128)(2,1)S(1)} %collective-permute-done.8.refs_1_, ...), custom_call_target="tpu_custom_call" | custom-call | flops 268435456 | bytes 4194304 | tf_op jit(solution)/shard_map/pallas_call | solution.py:44
  25.9 5.7 %shard_map.128 = (bf16[3,272,640]{2,1,0:T(8,128)(2,1)S(1)}, f32[256,128]{1,0:T(8,128)S(1)}, bf16[2,128,640]{2,1,0:T(8,128)(2,1)S(1)}, bf16[2,128,256]{2,1,0:T(8,...) custom-call(bf16[136,640]{1,0:T(8,128)(2,1)S(1)} %collective-permute-done.2.refs_0, ...), custom_call_target="tpu_custom_call" | custom-call | flops 268435456 | bytes 4194304 | tf_op jit(solution)/shard_map/pallas_call | solution.py:44
  31.6 22.5 %all_to_all.20.arrived = bf16[16,16,768]{2,1,0:T(8,128)(2,1)S(1)} all-to-all(bf16[16,16,768]{2,1,0:T(8,128)(2,1)S(1)} %bitcast.28), channel_id=1, replica_groups=mesh['pipe'=2,'chip'=4,'core'=2,'seq_0'=8,'seq_1'=2] {'seq_1','seq_0'}, dimensions={0} | all-to-all | bytes 786432 | tf_op jit(solution)/shard_map/all_to_all | solution.py:458
  55.1 6.1 %all-to-all-start.1 = ((bf16[16,16,640]{2,1,0:T(8,128)(2,1)}), bf16[16,16,640]{2,1,0:T(8,128)(2,1)S(1)}, u32[]{:S(2)}, u32[]{:S(2)}) async-start(bf16[16,16,640]{2,1,0:T(8,128)(2,1)} %shard_map.131), calls=%async_computation.1 | async-start | bytes 655360 | tf_op jit(solution)/shard_map/all_to_all | solution.py:472
  61.2 3.2 %shard_map.129.gate = f32[256,640]{1,0:T(8,128)S(1)} custom-call(bf16[1,272,640]{2,1,0:T(8,128)(2,1)S(1)} %get-tuple-element.53.near, bf16[3,272,640]{2,1,0:T(8,128)(2,1)S(1)} %get-tuple-element.54.far, f32[256,128]{1,0:T(8,128)S(1)} %get-tuple-element.55.scales, bf16[2560,640]{1,0:T(8,128)(2,1)} %bitcast.48), custom_call_target="tpu_custom_call" | custom-call | flops 268435456 | bytes 4194304 | tf_op jit(solution)/shard_map/pallas_call | solution.py:44
  65.3 5.2 %all-to-all-done.1 = bf16[16,16,640]{2,1,0:T(8,128)(2,1)S(1)} async-done(((bf16[16,16,640]{2,1,0:T(8,128)(2,1)}), bf16[16,16,640]{2,1,0:T(8,128)(2,1)S(1)}, u32[]{:S(2)}, u32[]{:S(2)}) %all-to-all-start.1) | async-done | bytes 327712 | tf_op jit(solution)/shard_map/all_to_all | solution.py:472
  70.5 4.0 %shard_map.132 = (bf16[4,136,640]{2,1,0:T(8,128)(2,1)S(1)}, bf16[4,136,640]{2,1,0:T(8,128)(2,1)}) custom-call(f32[2,128,640]{2,1,0:T(8,128)S(1)} %get-tuple-element.56.base, f32[2,128,640]{2,1,0:T(8,128)S(1)} %get-tuple-element.57.ahead, bf16[2,128,256]{2,1,0:T(8,128)(2,1)S(1)} %get-tuple-element.50.maps, bf16[2,128,640]{2,1,0:T(8,128)(2,1)S(1)} %bitcast.22, ...), custom_call_target="tpu_custom_call" | custom-call | flops 268435456 | bytes 4194304 | tf_op jit(solution)/shard_map/pallas_call | solution.py:44
  74.5 3.1 %collective-permute-start.9 = (bf16[4,136,640]{2,1,0:T(8,128)(2,1)}, bf16[4,136,640]{2,1,0:T(8,128)(2,1)S(1)}, u32[]{:S(2)}, u32[]{:S(2)}) collective-permute-start(bf16[4,136,640]{2,1,0:T(8,128)(2,1)} %get-tuple-element.60), channel_id=1, source_target_pairs={{0,16},{16,0},{1,17},{17,1},{2,18},{18,2},{3,19},{19,3},{4,20},{20... | collective-permute-start | bytes 2088968 | tf_op jit(solution)/shard_map/ppermute | solution.py:481
  77.6 2.0 %collective-permute-done.9.arrived = bf16[4,136,640]{2,1,0:T(8,128)(2,1)S(1)} collective-permute-done((bf16[4,136,640]{2,1,0:T(8,128)(2,1)}, bf16[4,136,640]{2,1,0:T(8,128)(2,1)S(1)}, u32[]{:S(2)}, u32[]{:S(2)}) %collective-permute-start.9) | collective-permute-done | bytes 696352 | tf_op jit(solution)/shard_map/ppermute | solution.py:481
  79.9 2.2 %collective-permute-start.11 = (bf16[136,640]{1,0:T(8,128)(2,1)S(1)}, bf16[136,640]{1,0:T(8,128)(2,1)S(1)}, u32[]{:S(2)}, u32[]{:S(2)}) collective-permute-start(bf16[136,640]{1,0:T(8,128)(2,1)S(1)} %get-tuple-element.63), channel_id=1, source_target_pairs={{0,64},{32,96},{64,0},{96,32},{1,65},{33,97},{65,1},{97,33},{2,66}... | collective-permute-start | bytes 522248 | tf_op jit(solution)/shard_map/ppermute | solution.py:488
  82.7 4.4 %collective-permute-done.10.refs_0_ = bf16[136,640]{1,0:T(8,128)(2,1)S(1)} collective-permute-done((bf16[136,640]{1,0:T(8,128)(2,1)S(1)}, bf16[136,640]{1,0:T(8,128)(2,1)S(1)}, u32[]{:S(2)}, u32[]{:S(2)}) %collective-permute-start.10) | collective-permute-done | bytes 174112 | tf_op jit(solution)/shard_map/ppermute | solution.py:488
  87.2 2.8 %collective-permute-done.11.refs_1_ = bf16[136,640]{1,0:T(8,128)(2,1)S(1)} collective-permute-done((bf16[136,640]{1,0:T(8,128)(2,1)S(1)}, bf16[136,640]{1,0:T(8,128)(2,1)S(1)}, u32[]{:S(2)}, u32[]{:S(2)}) %collective-permute-start.11) | collective-permute-done | bytes 174112 | tf_op jit(solution)/shard_map/ppermute | solution.py:488
  93.0 5.6 %collective-permute-done.13.piece = bf16[128,640]{1,0:T(8,128)(2,1)S(1)} collective-permute-done((bf16[128,640]{1,0:T(8,128)(2,1)S(1)}, bf16[128,640]{1,0:T(8,128)(2,1)S(1)}, u32[]{:S(2)}, u32[]{:S(2)}) %collective-permute-start.13) | collective-permute-done | bytes 163872 | tf_op jit(solution)/shard_map/ppermute | solution.py:543
  98.6 4.1 %collective-permute-start.17 = (bf16[136,640]{1,0:T(8,128)(2,1)S(1)}, bf16[136,640]{1,0:T(8,128)(2,1)S(1)}, u32[]{:S(2)}, u32[]{:S(2)}) collective-permute-start(bf16[136,640]{1,0:T(8,128)(2,1)S(1)} %constant_dynamic-update-slice_fusion.refs_0_), channel_id=1, source_target_pairs={{0,96},{32,0},{64,32},{96,64},{1,97},{33,1},{65,33},{97,65},{2,98}... | collective-permute-start | bytes 522248 | tf_op jit(solution)/shard_map/ppermute | solution.py:402
  104.0 2.0 %collective-permute-start.21 = (bf16[136,640]{1,0:T(8,128)(2,1)S(1)}, bf16[136,640]{1,0:T(8,128)(2,1)S(1)}, u32[]{:S(2)}, u32[]{:S(2)}) collective-permute-start(bf16[136,640]{1,0:T(8,128)(2,1)S(1)} %constant_dynamic-update-slice_fusion.refs_0_), channel_id=1, source_target_pairs={{0,16},{16,0},{1,17},{17,1},{2,18},{18,2},{3,19},{19,3},{4,20},{20... | collective-permute-start | bytes 522248 | tf_op jit(solution)/shard_map/ppermute | solution.py:408
  106.0 5.2 %collective-permute-start.20 = (bf16[136,640]{1,0:T(8,128)(2,1)S(1)}, bf16[136,640]{1,0:T(8,128)(2,1)S(1)}, u32[]{:S(2)}, u32[]{:S(2)}) collective-permute-start(bf16[136,640]{1,0:T(8,128)(2,1)S(1)} %collective-permute-done.17.refs_2_), channel_id=1, source_target_pairs={{0,16},{16,0},{1,17},{17,1},{2,18},{18,2},{3,19},{19,3},{4,20},{20... | collective-permute-start | bytes 522248 | tf_op jit(solution)/shard_map/ppermute | solution.py:408
  114.5 2.0 %shard_map.135 = (bf16[1,272,640]{2,1,0:T(8,128)(2,1)S(1)}, f32[272,128]{1,0:T(8,128)S(1)}, f32[272,10]{1,0:T(8,128)S(1)}, f32[272,256]{1,0:T(8,128)S(1)}, f32[272,640]{1,0:T(8,128)S(1)}) custom-call(bf16[136,640]{1,0:T(8,128)(2,1)S(1)} %constant_dynamic-update-slice_fusion.refs_0_, bf16[136,640]{1,0:T(8,128)(2,1)S(1)} %collective-permute-done.21.refs_1_, ...), custom_call_target="tpu_custom_call" | custom-call | flops 268435456 | bytes 4194304 | tf_op jit(solution)/shard_map/pallas_call | solution.py:44
  116.5 5.7 %shard_map.136 = (bf16[3,272,640]{2,1,0:T(8,128)(2,1)S(1)}, f32[256,128]{1,0:T(8,128)S(1)}, bf16[2,128,640]{2,1,0:T(8,128)(2,1)S(1)}, bf16[2,128,256]{2,1,0:T(8,...) custom-call(bf16[136,640]{1,0:T(8,128)(2,1)S(1)} %collective-permute-done.15.refs_, ...), custom_call_target="tpu_custom_call" | custom-call | flops 268435456 | bytes 4194304 | tf_op jit(solution)/shard_map/pallas_call | solution.py:44
  122.2 16.6 %all_to_all.21.arrived = bf16[16,16,768]{2,1,0:T(8,128)(2,1)S(1)} all-to-all(bf16[16,16,768]{2,1,0:T(8,128)(2,1)S(1)} %bitcast.29), channel_id=1, replica_groups=mesh['pipe'=2,'chip'=4,'core'=2,'seq_0'=8,'seq_1'=2] {'seq_1','seq_0'}, dimensions={0} | all-to-all | bytes 786432 | tf_op jit(solution)/shard_map/all_to_all | solution.py:458
  139.8 5.9 %all-to-all-start.3 = ((bf16[16,16,640]{2,1,0:T(8,128)(2,1)}), bf16[16,16,640]{2,1,0:T(8,128)(2,1)S(1)}, u32[]{:S(2)}, u32[]{:S(2)}) async-start(bf16[16,16,640]{2,1,0:T(8,128)(2,1)} %shard_map.139), calls=%async_computation.3 | async-start | bytes 655360 | tf_op jit(solution)/shard_map/all_to_all | solution.py:472
  145.8 3.2 %shard_map.137.gate = f32[256,640]{1,0:T(8,128)S(1)} custom-call(bf16[1,272,640]{2,1,0:T(8,128)(2,1)S(1)} %get-tuple-element.73.near, bf16[3,272,640]{2,1,0:T(8,128)(2,1)S(1)} %get-tuple-element.74.far, f32[256,128]{1,0:T(8,128)S(1)} %get-tuple-element.75.scales, bf16[2560,640]{1,0:T(8,128)(2,1)} %bitcast.49), custom_call_target="tpu_custom_call" | custom-call | flops 268435456 | bytes 4194304 | tf_op jit(solution)/shard_map/pallas_call | solution.py:44
  149.9 5.2 %all-to-all-done.3 = bf16[16,16,640]{2,1,0:T(8,128)(2,1)S(1)} async-done(((bf16[16,16,640]{2,1,0:T(8,128)(2,1)}), bf16[16,16,640]{2,1,0:T(8,128)(2,1)S(1)}, u32[]{:S(2)}, u32[]{:S(2)}) %all-to-all-start.3) | async-done | bytes 327712 | tf_op jit(solution)/shard_map/all_to_all | solution.py:472
  155.1 3.3 %shard_map.140 = (bf16[4,136,640]{2,1,0:T(8,128)(2,1)S(1)}, bf16[4,136,640]{2,1,0:T(8,128)(2,1)S(1)}) custom-call(f32[2,128,640]{2,1,0:T(8,128)S(1)} %get-tuple-element.76.base, f32[2,128,640]{2,1,0:T(8,128)S(1)} %get-tuple-element.77.ahead, bf16[2,128,256]{2,1,0:T(8,128)(2,1)S(1)} %get-tuple-element.70.maps, bf16[2,128,640]{2,1,0:T(8,128)(2,1)S(1)} %bitcast.23, ...), custom_call_target="tpu_custom_call" | custom-call | flops 268435456 | bytes 4194304 | tf_op jit(solution)/shard_map/pallas_call | solution.py:44
  158.4 3.1 %collective-permute-start.22 = (bf16[4,136,640]{2,1,0:T(8,128)(2,1)S(1)}, bf16[4,136,640]{2,1,0:T(8,128)(2,1)S(1)}, u32[]{:S(2)}, u32[]{:S(2)}) collective-permute-start(bf16[4,136,640]{2,1,0:T(8,128)(2,1)S(1)} %get-tuple-element.80), channel_id=1, source_target_pairs={{0,16},{16,0},{1,17},{17,1},{2,18},{18,2},{3,19},{19,3},{4,20},{20... | collective-permute-start | bytes 2088968 | tf_op jit(solution)/shard_map/ppermute | solution.py:481
  161.6 1.8 %collective-permute-done.22.arrived = bf16[4,136,640]{2,1,0:T(8,128)(2,1)S(1)} collective-permute-done((bf16[4,136,640]{2,1,0:T(8,128)(2,1)S(1)}, bf16[4,136,640]{2,1,0:T(8,128)(2,1)S(1)}, u32[]{:S(2)}, u32[]{:S(2)}) %collective-permute-start.22) | collective-permute-done | bytes 696352 | tf_op jit(solution)/shard_map/ppermute | solution.py:481
  163.6 1.8 collective-permute-start.24
  166.4 4.8 %collective-permute-done.23.refs_0_ = bf16[136,640]{1,0:T(8,128)(2,1)S(1)} collective-permute-done((bf16[136,640]{1,0:T(8,128)(2,1)S(1)}, bf16[136,640]{1,0:T(8,128)(2,1)S(1)}, u32[]{:S(2)}, u32[]{:S(2)}) %collective-permute-start.23) | collective-permute-done | bytes 174112 | tf_op jit(solution)/shard_map/ppermute | solution.py:488
  171.2 2.0 %collective-permute-done.24.refs_1_ = bf16[136,640]{1,0:T(8,128)(2,1)S(1)} collective-permute-done((bf16[136,640]{1,0:T(8,128)(2,1)S(1)}, bf16[136,640]{1,0:T(8,128)(2,1)S(1)}, u32[]{:S(2)}, u32[]{:S(2)}) %collective-permute-start.24) | collective-permute-done | bytes 174112 | tf_op jit(solution)/shard_map/ppermute | solution.py:488
  (76 shorter events, 28.3 us)
Async XLA Ops:
  0.0 25.8 %copy-start.8 = (f32[1,10]{1,0:T(1,128)S(1)}, f32[1,10]{1,0:T(1,128)}, u32[]{:S(2)}) copy-start(f32[1,10]{1,0:T(1,128)} %refs_14_.3) | copy-start | bytes 124
  0.0 25.8 %copy-start.5 = (f32[1,5,256]{2,0,1:T(1,128)S(1)}, f32[1,5,256]{2,0,1:T(1,128)}, u32[]{:S(2)}) copy-start(f32[1,5,256]{2,0,1:T(1,128)} %param.20) | copy-start | bytes 15364
  0.0 25.8 %copy-start.4 = (f32[1,5,640]{2,0,1:T(1,128)S(1)}, f32[1,5,640]{2,0,1:T(1,128)}, u32[]{:S(2)}) copy-start(f32[1,5,640]{2,0,1:T(1,128)} %param.19) | copy-start | bytes 38404
  1.2 3.6 %collective-permute-start = (bf16[2,8,320]{2,1,0:T(8,128)(2,1)S(1)}, bf16[2,8,320]{2,1,0:T(8,128)(2,1)S(1)}, u32[]{:S(2)}, u32[]{:S(2)}) collective-permute-start(bf16[2,8,320]{2,1,0:T(8,128)(2,1)S(1)} %slice.32), channel_id=1, source_target_pairs={{0,1},{1,2},{2,3},{3,4},{4,5},{5,6},{6,7},{7,8},{8,9},{9,10},{10,1... | collective-permute-start | bytes 30728 | tf_op jit(solution)/shard_map/ppermute | solution.py:526
  4.9 2.6 %collective-permute-start.1 = (bf16[136,320]{1,0:T(8,128)(2,1)S(1)}, bf16[136,320]{1,0:T(8,128)(2,1)S(1)}, u32[]{:S(2)}, u32[]{:S(2)}) collective-permute-start(bf16[136,320]{1,0:T(8,128)(2,1)S(1)} %get-tuple-element.86), channel_id=1, source_target_pairs={{0,16},{16,0},{1,17},{17,1},{2,18},{18,2},{3,19},{19,3},{4,20},{20... | collective-permute-start | bytes 261128 | tf_op jit(solution)/shard_map/ppermute | solution.py:529
  7.6 6.2 %collective-permute-start.4 = (bf16[136,640]{1,0:T(8,128)(2,1)S(1)}, bf16[136,640]{1,0:T(8,128)(2,1)S(1)}, u32[]{:S(2)}, u32[]{:S(2)}) collective-permute-start(bf16[136,640]{1,0:T(8,128)(2,1)S(1)} %maximum_select_fusion.1.refs_0_), channel_id=1, source_target_pairs={{0,96},{32,0},{64,32},{96,64},{1,97},{33,1},{65,33},{97,65},{2,98}... | collective-permute-start | bytes 522248 | tf_op jit(solution)/shard_map/ppermute | solution.py:402
  10.4 8.4 %collective-permute-start.3 = (bf16[136,640]{1,0:T(8,128)(2,1)S(1)}, bf16[136,640]{1,0:T(8,128)(2,1)S(1)}, u32[]{:S(2)}, u32[]{:S(2)}) collective-permute-start(bf16[136,640]{1,0:T(8,128)(2,1)S(1)} %maximum_select_fusion.1.refs_0_), channel_id=1, source_target_pairs={{0,32},{32,64},{64,96},{96,0},{1,33},{33,65},{65,97},{97,1},{2,34}... | collective-permute-start | bytes 522248 | tf_op jit(solution)/shard_map/ppermute | solution.py:402
  10.4 11.8 %collective-permute-start.2 = (bf16[136,640]{1,0:T(8,128)(2,1)S(1)}, bf16[136,640]{1,0:T(8,128)(2,1)S(1)}, u32[]{:S(2)}, u32[]{:S(2)}) collective-permute-start(bf16[136,640]{1,0:T(8,128)(2,1)S(1)} %maximum_select_fusion.1.refs_0_), channel_id=1, source_target_pairs={{0,64},{32,96},{64,0},{96,32},{1,65},{33,97},{65,1},{97,33},{2,66}... | collective-permute-start | bytes 522248 | tf_op jit(solution)/shard_map/ppermute | solution.py:402
  12.1 10.1 %collective-permute-start.8 = (bf16[136,640]{1,0:T(8,128)(2,1)S(1)}, bf16[136,640]{1,0:T(8,128)(2,1)S(1)}, u32[]{:S(2)}, u32[]{:S(2)}) collective-permute-start(bf16[136,640]{1,0:T(8,128)(2,1)S(1)} %maximum_select_fusion.1.refs_0_), channel_id=1, source_target_pairs={{0,16},{16,0},{1,17},{17,1},{2,18},{18,2},{3,19},{19,3},{4,20},{20... | collective-permute-start | bytes 522248 | tf_op jit(solution)/shard_map/ppermute | solution.py:408
  13.8 12.0 %collective-permute-start.7 = (bf16[136,640]{1,0:T(8,128)(2,1)S(1)}, bf16[136,640]{1,0:T(8,128)(2,1)S(1)}, u32[]{:S(2)}, u32[]{:S(2)}) collective-permute-start(bf16[136,640]{1,0:T(8,128)(2,1)S(1)} %collective-permute-done.4.refs_2_), channel_id=1, source_target_pairs={{0,16},{16,0},{1,17},{17,1},{2,18},{18,2},{3,19},{19,3},{4,20},{20... | collective-permute-start | bytes 522248 | tf_op jit(solution)/shard_map/ppermute | solution.py:408
  18.8 7.0 %collective-permute-start.6 = (bf16[136,640]{1,0:T(8,128)(2,1)S(1)}, bf16[136,640]{1,0:T(8,128)(2,1)S(1)}, u32[]{:S(2)}, u32[]{:S(2)}) collective-permute-start(bf16[136,640]{1,0:T(8,128)(2,1)S(1)} %collective-permute-done.3.refs_1_), channel_id=1, source_target_pairs={{0,16},{16,0},{1,17},{17,1},{2,18},{18,2},{3,19},{19,3},{4,20},{20... | collective-permute-start | bytes 522248 | tf_op jit(solution)/shard_map/ppermute | solution.py:408
  22.2 3.6 %collective-permute-start.5 = (bf16[136,640]{1,0:T(8,128)(2,1)S(1)}, bf16[136,640]{1,0:T(8,128)(2,1)S(1)}, u32[]{:S(2)}, u32[]{:S(2)}) collective-permute-start(bf16[136,640]{1,0:T(8,128)(2,1)S(1)} %collective-permute-done.2.refs_0_), channel_id=1, source_target_pairs={{0,16},{16,0},{1,17},{17,1},{2,18},{18,2},{3,19},{19,3},{4,20},{20... | collective-permute-start | bytes 522248 | tf_op jit(solution)/shard_map/ppermute | solution.py:408
  55.1 15.4 %all-to-all-start.1 = ((bf16[16,16,640]{2,1,0:T(8,128)(2,1)}), bf16[16,16,640]{2,1,0:T(8,128)(2,1)S(1)}, u32[]{:S(2)}, u32[]{:S(2)}) async-start(bf16[16,16,640]{2,1,0:T(8,128)(2,1)} %shard_map.131), calls=%async_computation.1 | async-start | bytes 655360 | tf_op jit(solution)/shard_map/all_to_all | solution.py:472
  74.5 5.1 %collective-permute-start.9 = (bf16[4,136,640]{2,1,0:T(8,128)(2,1)}, bf16[4,136,640]{2,1,0:T(8,128)(2,1)S(1)}, u32[]{:S(2)}, u32[]{:S(2)}) collective-permute-start(bf16[4,136,640]{2,1,0:T(8,128)(2,1)} %get-tuple-element.60), channel_id=1, source_target_pairs={{0,16},{16,0},{1,17},{17,1},{2,18},{18,2},{3,19},{19,3},{4,20},{20... | collective-permute-start | bytes 2088968 | tf_op jit(solution)/shard_map/ppermute | solution.py:481
  79.8 7.4 %collective-permute-start.10 = (bf16[136,640]{1,0:T(8,128)(2,1)S(1)}, bf16[136,640]{1,0:T(8,128)(2,1)S(1)}, u32[]{:S(2)}, u32[]{:S(2)}) collective-permute-start(bf16[136,640]{1,0:T(8,128)(2,1)S(1)} %get-tuple-element.62), channel_id=1, source_target_pairs={{0,32},{32,64},{64,96},{96,0},{1,33},{33,65},{65,97},{97,1},{2,34}... | collective-permute-start | bytes 522248 | tf_op jit(solution)/shard_map/ppermute | solution.py:488
  79.9 10.1 %collective-permute-start.11 = (bf16[136,640]{1,0:T(8,128)(2,1)S(1)}, bf16[136,640]{1,0:T(8,128)(2,1)S(1)}, u32[]{:S(2)}, u32[]{:S(2)}) collective-permute-start(bf16[136,640]{1,0:T(8,128)(2,1)S(1)} %get-tuple-element.63), channel_id=1, source_target_pairs={{0,64},{32,96},{64,0},{96,32},{1,65},{33,97},{65,1},{97,33},{2,66}... | collective-permute-start | bytes 522248 | tf_op jit(solution)/shard_map/ppermute | solution.py:488
  82.0 8.8 %collective-permute-start.12 = (bf16[136,640]{1,0:T(8,128)(2,1)S(1)}, bf16[136,640]{1,0:T(8,128)(2,1)S(1)}, u32[]{:S(2)}, u32[]{:S(2)}) collective-permute-start(bf16[136,640]{1,0:T(8,128)(2,1)S(1)} %get-tuple-element.64), channel_id=1, source_target_pairs={{0,96},{32,0},{64,32},{96,64},{1,97},{33,1},{65,33},{97,65},{2,98}... | collective-permute-start | bytes 522248 | tf_op jit(solution)/shard_map/ppermute | solution.py:488
  91.0 7.6 %collective-permute-start.13 = (bf16[128,640]{1,0:T(8,128)(2,1)S(1)}, bf16[128,640]{1,0:T(8,128)(2,1)S(1)}, u32[]{:S(2)}, u32[]{:S(2)}) collective-permute-start(bf16[128,640]{1,0:T(8,128)(2,1)S(1)} %shard_map.134), channel_id=1, source_target_pairs={{0,128},{1,129},{2,130},{3,131},{4,132},{5,133},{6,134},{7,135},{8... | collective-permute-start | bytes 491528 | tf_op jit(solution)/shard_map/ppermute | solution.py:543
  92.3 0.7 collective-permute-start.14
  98.6 7.4 %collective-permute-start.17 = (bf16[136,640]{1,0:T(8,128)(2,1)S(1)}, bf16[136,640]{1,0:T(8,128)(2,1)S(1)}, u32[]{:S(2)}, u32[]{:S(2)}) collective-permute-start(bf16[136,640]{1,0:T(8,128)(2,1)S(1)} %constant_dynamic-update-slice_fusion.refs_0_), channel_id=1, source_target_pairs={{0,96},{32,0},{64,32},{96,64},{1,97},{33,1},{65,33},{97,65},{2,98}... | collective-permute-start | bytes 522248 | tf_op jit(solution)/shard_map/ppermute | solution.py:402
  102.7 10.1 %collective-permute-start.16 = (bf16[136,640]{1,0:T(8,128)(2,1)S(1)}, bf16[136,640]{1,0:T(8,128)(2,1)S(1)}, u32[]{:S(2)}, u32[]{:S(2)}) collective-permute-start(bf16[136,640]{1,0:T(8,128)(2,1)S(1)} %constant_dynamic-update-slice_fusion.refs_0_), channel_id=1, source_target_pairs={{0,32},{32,64},{64,96},{96,0},{1,33},{33,65},{65,97},{97,1},{2,34}... | collective-permute-start | bytes 522248 | tf_op jit(solution)/shard_map/ppermute | solution.py:402
  102.7 11.8 %collective-permute-start.15 = (bf16[136,640]{1,0:T(8,128)(2,1)S(1)}, bf16[136,640]{1,0:T(8,128)(2,1)S(1)}, u32[]{:S(2)}, u32[]{:S(2)}) collective-permute-start(bf16[136,640]{1,0:T(8,128)(2,1)S(1)} %constant_dynamic-update-slice_fusion.refs_0_), channel_id=1, source_target_pairs={{0,64},{32,96},{64,0},{96,32},{1,65},{33,97},{65,1},{97,33},{2,66}... | collective-permute-start | bytes 522248 | tf_op jit(solution)/shard_map/ppermute | solution.py:402
  104.0 10.5 %collective-permute-start.21 = (bf16[136,640]{1,0:T(8,128)(2,1)S(1)}, bf16[136,640]{1,0:T(8,128)(2,1)S(1)}, u32[]{:S(2)}, u32[]{:S(2)}) collective-permute-start(bf16[136,640]{1,0:T(8,128)(2,1)S(1)} %constant_dynamic-update-slice_fusion.refs_0_), channel_id=1, source_target_pairs={{0,16},{16,0},{1,17},{17,1},{2,18},{18,2},{3,19},{19,3},{4,20},{20... | collective-permute-start | bytes 522248 | tf_op jit(solution)/shard_map/ppermute | solution.py:408
  106.0 10.5 %collective-permute-start.20 = (bf16[136,640]{1,0:T(8,128)(2,1)S(1)}, bf16[136,640]{1,0:T(8,128)(2,1)S(1)}, u32[]{:S(2)}, u32[]{:S(2)}) collective-permute-start(bf16[136,640]{1,0:T(8,128)(2,1)S(1)} %collective-permute-done.17.refs_2_), channel_id=1, source_target_pairs={{0,16},{16,0},{1,17},{17,1},{2,18},{18,2},{3,19},{19,3},{4,20},{20... | collective-permute-start | bytes 522248 | tf_op jit(solution)/shard_map/ppermute | solution.py:408
  112.8 3.7 %collective-permute-start.19 = (bf16[136,640]{1,0:T(8,128)(2,1)S(1)}, bf16[136,640]{1,0:T(8,128)(2,1)S(1)}, u32[]{:S(2)}, u32[]{:S(2)}) collective-permute-start(bf16[136,640]{1,0:T(8,128)(2,1)S(1)} %collective-permute-done.16.refs_1_), channel_id=1, source_target_pairs={{0,16},{16,0},{1,17},{17,1},{2,18},{18,2},{3,19},{19,3},{4,20},{20... | collective-permute-start | bytes 522248 | tf_op jit(solution)/shard_map/ppermute | solution.py:408
  114.5 2.0 %collective-permute-start.18 = (bf16[136,640]{1,0:T(8,128)(2,1)S(1)}, bf16[136,640]{1,0:T(8,128)(2,1)S(1)}, u32[]{:S(2)}, u32[]{:S(2)}) collective-permute-start(bf16[136,640]{1,0:T(8,128)(2,1)S(1)} %collective-permute-done.15.refs_0_), channel_id=1, source_target_pairs={{0,16},{16,0},{1,17},{17,1},{2,18},{18,2},{3,19},{19,3},{4,20},{20... | collective-permute-start | bytes 522248 | tf_op jit(solution)/shard_map/ppermute | solution.py:408
  139.8 15.3 %all-to-all-start.3 = ((bf16[16,16,640]{2,1,0:T(8,128)(2,1)}), bf16[16,16,640]{2,1,0:T(8,128)(2,1)S(1)}, u32[]{:S(2)}, u32[]{:S(2)}) async-start(bf16[16,16,640]{2,1,0:T(8,128)(2,1)} %shard_map.139), calls=%async_computation.3 | async-start | bytes 655360 | tf_op jit(solution)/shard_map/all_to_all | solution.py:472
  158.4 4.9 %collective-permute-start.22 = (bf16[4,136,640]{2,1,0:T(8,128)(2,1)S(1)}, bf16[4,136,640]{2,1,0:T(8,128)(2,1)S(1)}, u32[]{:S(2)}, u32[]{:S(2)}) collective-permute-start(bf16[4,136,640]{2,1,0:T(8,128)(2,1)S(1)} %get-tuple-element.80), channel_id=1, source_target_pairs={{0,16},{16,0},{1,17},{17,1},{2,18},{18,2},{3,19},{19,3},{4,20},{20... | collective-permute-start | bytes 2088968 | tf_op jit(solution)/shard_map/ppermute | solution.py:481
  163.5 7.7 %collective-permute-start.23 = (bf16[136,640]{1,0:T(8,128)(2,1)S(1)}, bf16[136,640]{1,0:T(8,128)(2,1)S(1)}, u32[]{:S(2)}, u32[]{:S(2)}) collective-permute-start(bf16[136,640]{1,0:T(8,128)(2,1)S(1)} %get-tuple-element.82), channel_id=1, source_target_pairs={{0,32},{32,64},{64,96},{96,0},{1,33},{33,65},{65,97},{97,1},{2,34}... | collective-permute-start | bytes 522248 | tf_op jit(solution)/shard_map/ppermute | solution.py:488
  163.6 9.7 %collective-permute-start.24 = (bf16[136,640]{1,0:T(8,128)(2,1)S(1)}, bf16[136,640]{1,0:T(8,128)(2,1)S(1)}, u32[]{:S(2)}, u32[]{:S(2)}) collective-permute-start(bf16[136,640]{1,0:T(8,128)(2,1)S(1)} %get-tuple-element.83), channel_id=1, source_target_pairs={{0,64},{32,96},{64,0},{96,32},{1,65},{33,97},{65,1},{97,33},{2,66}... | collective-permute-start | bytes 522248 | tf_op jit(solution)/shard_map/ppermute | solution.py:488
  165.4 9.2 %collective-permute-start.25 = (bf16[136,640]{1,0:T(8,128)(2,1)S(1)}, bf16[136,640]{1,0:T(8,128)(2,1)S(1)}, u32[]{:S(2)}, u32[]{:S(2)}) collective-permute-start(bf16[136,640]{1,0:T(8,128)(2,1)S(1)} %get-tuple-element.84), channel_id=1, source_target_pairs={{0,96},{32,0},{64,32},{96,64},{1,97},{33,1},{65,33},{97,65},{2,98}... | collective-permute-start | bytes 522248 | tf_op jit(solution)/shard_map/ppermute | solution.py:488
  174.8 2.5 %collective-permute-start.26 = (bf16[128,320]{1,0:T(8,128)(2,1)S(1)}, bf16[128,320]{1,0:T(8,128)(2,1)S(1)}, u32[]{:S(2)}, u32[]{:S(2)}) collective-permute-start(bf16[128,320]{1,0:T(8,128)(2,1)S(1)} %get-tuple-element.88), channel_id=1, source_target_pairs={{0,16},{16,0},{1,17},{17,1},{2,18},{18,2},{3,19},{19,3},{4,20},{20... | collective-permute-start | bytes 245768 | tf_op jit(solution)/shard_map/ppermute | solution.py:555
  (7 other events, 97.7 us)

commit v5 on v4

--- a/solution.py
+++ b/solution.py
@@ -149,9 +149,11 @@
     span = slice(part * block, (part + 1) * block)
     value = scaled[...]
     step = dot(value, step_w, ((1,), (1,)))
-    copies[0][part].wait()
+    if copies is not None:
+        copies[0][part].wait()
     state = dot(value, state_w[span, :])
-    copies[1][part].wait()
+    if copies is not None:
+        copies[1][part].wait()
     return step, state, dot(value, inner_w[span, :])
 
 
@@ -159,12 +161,16 @@
     count = len(NEAR)
     sides = refs[:count], refs[count : 2 * count]
     gain, step_w, state_hbm, inner_hbm = refs[2 * count :][:4]
-    scaled, squares, step, state, inner = refs[2 * count + 4 :][:5]
-    state_w, state_sems, inner_w, inner_sems = refs[2 * count + 9 :]
+    scaled, squares, step, state, inner, state_rest, inner_rest = refs[2 * count + 4 :][:7]
+    state_w, state_sems, inner_w, inner_sems, state_rest_sems, inner_rest_sems = refs[
+        2 * count + 11 :
+    ]
     blocks = blocks_of(NEAR)
     copies = fetch(state_hbm, state_w, state_sems, blocks), fetch(
         inner_hbm, inner_w, inner_sems, blocks
     )
+    rest = fetch(state_hbm, state_rest, state_rest_sems, blocks_of(FAR))
+    rest += fetch(inner_hbm, inner_rest, inner_rest_sems, blocks_of(FAR))
     edge = EDGE
     rows = sides[0][0].shape[0] - edge
     width = sides[0][0].shape[1]
@@ -183,6 +189,8 @@
         squares[side * rows : (side + 1) * rows, :] = sums[side][edge:]
         squares[2 * rows + side * edge : 2 * rows + (side + 1) * edge, :] = sums[side][:edge]
     step[...], state[...], inner[...] = totals
+    for copy in rest:
+        copy.wait()
 
 
 def enter_far(*refs):
@@ -190,13 +198,9 @@
     sides = refs[:count], refs[count : 2 * count]
     squares_in, step_in, state_in, inner_in = refs[2 * count :][:4]
     refs = refs[2 * count + 4 :]
-    gain, step_w, inner_taps, state_taps, bias, rate, state_hbm, inner_hbm = refs[:8]
-    scaled, scales, x, maps, steps, sums, sent = refs[8:15]
-    state_w, state_sems, inner_w, inner_sems = refs[15:]
+    gain, step_w, inner_taps, state_taps, bias, rate, state_w, inner_w = refs[:8]
+    scaled, scales, x, maps, steps, sums, sent = refs[8:]
     blocks = blocks_of(FAR)
-    copies = fetch(state_hbm, state_w, state_sems, blocks), fetch(
-        inner_hbm, inner_w, inner_sems, blocks
-    )
     edge = EDGE
     rows, width = x.shape[1:]
     block = sides[0][0].shape[1]
@@ -216,7 +220,7 @@
     scales[...] = jnp.broadcast_to(scale[: 2 * rows], scales.shape)
     totals = [step_in[...], state_in[...], inner_in[...]]
     for k, b in enumerate(blocks):
-        parts = multiply(scaled.at[k], k, columns(step_w, b, block), state_w, inner_w, copies)
+        parts = multiply(scaled.at[k], k, columns(step_w, b, block), state_w, inner_w, None)
         totals = [total + part for total, part in zip(totals, parts)]
     step, state, inner = totals
     raw = (step * scale)[: 2 * rows] + bias[...]
@@ -409,7 +413,7 @@
     near = [own[k] for k in NEAR] + [other[k] for k in NEAR]
     far = [own[k] for k in FAR] + [other[k] for k in FAR]
     high = 2 * spread_rows.shape[0]
-    scaled, squares, *partial = local(
+    scaled, squares, *partial, state_rest, inner_rest = local(
         enter_near,
         [*near, gain, steps_weight, state_weight, inner_weight],
         [
@@ -418,11 +422,15 @@
             ((high, heads), F32),
             ((high, maps_width), F32),
             ((high, width), F32),
+            ((len(FAR) * block, maps_width), BF16),
+            ((len(FAR) * block, width), BF16),
         ],
         weights=2,
         scratch=[
             *room(state_weight, len(NEAR), len(NEAR) * block),
             *room(inner_weight, len(NEAR), len(NEAR) * block),
+            pltpu.SemaphoreType.DMA((len(FAR),)),
+            pltpu.SemaphoreType.DMA((len(FAR),)),
         ],
     )
     scaled_far, scales, x, maps, steps, sums, sent = local(
@@ -437,8 +445,8 @@
             state_taps[:, None],
             step_bias[None],
             decay_rate[None],
-            state_weight,
-            inner_weight,
+            state_rest,
+            inner_rest,
         ],
         [
             ((len(FAR), high, block), BF16),
@@ -448,11 +456,6 @@
             ((2, rows, heads), F32),
             ((2, rows, heads), F32),
             ((tall, width + 128), BF16),
-        ],
-        weights=2,
-        scratch=[
-            *room(state_weight, len(FAR), len(FAR) * block),
-            *room(inner_weight, len(FAR), len(FAR) * block),
         ],
     )
     arrived = lax.all_to_all(sent.reshape(members, tall // members, -1), CROSS, 0, 0, tiled=True)

time: 179 us -> 176 us (0.983)
  Pallas kernels: 33.7 us -> 30.7 us
    pallas_call x16, Pallas kernels: 33.7 us -> 30.7 us  [local(): pl.pallas_call(body, out_shape=[jax.ShapeDtypeStruct(shape, kind) for sha...]
  transfers between devices with their start and end apart: 29 -> 29, of which waited for: 16 -> 16; matrix products, arithmetic and copies ran while one was open for 0% -> 0% of each run, Pallas kernels for 7% -> 8%
where the time goes in v5:
time: 176 us; the launch traced here: 175 us
  starting transfers between devices  60.2 us (34%)
  waiting for transfers between devices  40.8 us (23%)
  blocking collectives  39.1 us (22%)
  Pallas kernels  30.7 us (17%)
  local copies, waits for them, and re-layouts  3.63 us (2%)
    all_to_all x2, blocking collectives, layer(): lax.all_to_all(sent.reshape(members, tall // members, -1), CROSS, 0, 0, t...  39.1 us
    pallas_call x16, Pallas kernels, local(): pl.pallas_call(body, out_shape=[jax.ShapeDtypeStruct(shape, kind) for sha...  30.7 us
    ppermute x8, starting transfers between devices, layer(): other = {k: lax.ppermute(part, 'core', SWAP) for k, part in own.items()}  18.5 us
    ppermute x6, waiting for transfers between devices, layer(): lax.ppermute(part, 'chip', ring(count, k + 1))  16.2 us
    all_to_all x2, starting transfers between devices, layer(): back = lax.all_to_all(back, CROSS, 0, 0, tiled=True)  12 us
    all_to_all x2, waiting for transfers between devices, layer(): back = lax.all_to_all(back, CROSS, 0, 0, tiled=True)  10.4 us
    ppermute x6, starting transfers between devices, moved(): return lax.ppermute(spread_rows, 'chip', ring(count, step))  9.81 us
    ppermute x2, starting transfers between devices, layer(): taken = lax.ppermute(given, 'core', SWAP)  6.2 us
  transfers between devices with their start and end apart: 29, of which 16 were waited for; matrix products, arithmetic and copies ran while one was open for 0% of the time, Pallas kernels for 8%

profile of v5, /device:TPU:5, one launch (start us, length us, event | category | flops | bytes accessed | tf_op | source)
XLA Modules:
  0.0 175.2 jit_solution(14111555813451270672)
XLA Ops:
  1.2 2.8 %collective-permute-start = (bf16[2,8,320]{2,1,0:T(8,128)(2,1)S(1)}, bf16[2,8,320]{2,1,0:T(8,128)(2,1)S(1)}, u32[]{:S(2)}, u32[]{:S(2)}) collective-permute-start(bf16[2,8,320]{2,1,0:T(8,128)(2,1)S(1)} %slice.32), channel_id=1, source_target_pairs={{0,1},{1,2},{2,3},{3,4},{4,5},{5,6},{6,7},{7,8},{8,9},{9,10},{10,1... | collective-permute-start | bytes 30728 | tf_op jit(solution)/shard_map/ppermute | solution.py:529
  7.6 2.8 %collective-permute-start.4 = (bf16[136,640]{1,0:T(8,128)(2,1)S(1)}, bf16[136,640]{1,0:T(8,128)(2,1)S(1)}, u32[]{:S(2)}, u32[]{:S(2)}) collective-permute-start(bf16[136,640]{1,0:T(8,128)(2,1)S(1)} %maximum_select_fusion.1.refs_0_), channel_id=1, source_target_pairs={{0,96},{32,0},{64,32},{96,64},{1,97},{33,1},{65,33},{97,65},{2,98}... | collective-permute-start | bytes 522248 | tf_op jit(solution)/shard_map/ppermute | solution.py:406
  13.8 5.0 %collective-permute-start.7 = (bf16[136,640]{1,0:T(8,128)(2,1)S(1)}, bf16[136,640]{1,0:T(8,128)(2,1)S(1)}, u32[]{:S(2)}, u32[]{:S(2)}) collective-permute-start(bf16[136,640]{1,0:T(8,128)(2,1)S(1)} %collective-permute-done.4.refs_2_), channel_id=1, source_target_pairs={{0,16},{16,0},{1,17},{17,1},{2,18},{18,2},{3,19},{19,3},{4,20},{20... | collective-permute-start | bytes 522248 | tf_op jit(solution)/shard_map/ppermute | solution.py:412
  18.8 3.4 %collective-permute-start.6 = (bf16[136,640]{1,0:T(8,128)(2,1)S(1)}, bf16[136,640]{1,0:T(8,128)(2,1)S(1)}, u32[]{:S(2)}, u32[]{:S(2)}) collective-permute-start(bf16[136,640]{1,0:T(8,128)(2,1)S(1)} %collective-permute-done.3.refs_1_), channel_id=1, source_target_pairs={{0,16},{16,0},{1,17},{17,1},{2,18},{18,2},{3,19},{19,3},{4,20},{20... | collective-permute-start | bytes 522248 | tf_op jit(solution)/shard_map/ppermute | solution.py:412
  23.8 2.8 %shard_map.127 = (bf16[1,272,640]{2,1,0:T(8,128)(2,1)S(1)}, f32[272,128]{1,0:T(8,128)S(1)}, f32[272,10]{1,0:T(8,128)S(1)}, f32[272,256]{1,0:T(8,128)S(1)}, f32[2...) custom-call(bf16[136,640]{1,0:T(8,128)(2,1)S(1)} %maximum_select_fusion.1.refs_0_, ...), custom_call_target="tpu_custom_call" | custom-call | flops 268435456 | bytes 4194304 | tf_op jit(solution)/shard_map/pallas_call | solution.py:44
  26.7 3.4 %shard_map.128 = (bf16[3,272,640]{2,1,0:T(8,128)(2,1)S(1)}, f32[256,128]{1,0:T(8,128)S(1)}, bf16[2,128,640]{2,1,0:T(8,128)(2,1)S(1)}, bf16[2,128,256]{2,1,0:T(8,...) custom-call(bf16[136,640]{1,0:T(8,128)(2,1)S(1)} %collective-permute-done.2.refs_0, ...), custom_call_target="tpu_custom_call" | custom-call | flops 268435456 | bytes 4194304 | tf_op jit(solution)/shard_map/pallas_call | solution.py:44
  30.1 22.5 %all_to_all.20.arrived = bf16[16,16,768]{2,1,0:T(8,128)(2,1)S(1)} all-to-all(bf16[16,16,768]{2,1,0:T(8,128)(2,1)S(1)} %bitcast.28), channel_id=1, replica_groups=mesh['pipe'=2,'chip'=4,'core'=2,'seq_0'=8,'seq_1'=2] {'seq_1','seq_0'}, dimensions={0} | all-to-all | bytes 786432 | tf_op jit(solution)/shard_map/all_to_all | solution.py:461
  53.6 6.1 %all-to-all-start.1 = ((bf16[16,16,640]{2,1,0:T(8,128)(2,1)}), bf16[16,16,640]{2,1,0:T(8,128)(2,1)S(1)}, u32[]{:S(2)}, u32[]{:S(2)}) async-start(bf16[16,16,640]{2,1,0:T(8,128)(2,1)} %shard_map.131), calls=%async_computation.1 | async-start | bytes 655360 | tf_op jit(solution)/shard_map/all_to_all | solution.py:475
  59.7 3.2 %shard_map.129.gate = f32[256,640]{1,0:T(8,128)S(1)} custom-call(bf16[1,272,640]{2,1,0:T(8,128)(2,1)S(1)} %get-tuple-element.59.near, bf16[3,272,640]{2,1,0:T(8,128)(2,1)S(1)} %get-tuple-element.60.far, f32[256,128]{1,0:T(8,128)S(1)} %get-tuple-element.61.scales, bf16[2560,640]{1,0:T(8,128)(2,1)} %bitcast.42), custom_call_target="tpu_custom_call" | custom-call | flops 268435456 | bytes 4194304 | tf_op jit(solution)/shard_map/pallas_call | solution.py:44
  63.9 5.2 %all-to-all-done.1 = bf16[16,16,640]{2,1,0:T(8,128)(2,1)S(1)} async-done(((bf16[16,16,640]{2,1,0:T(8,128)(2,1)}), bf16[16,16,640]{2,1,0:T(8,128)(2,1)S(1)}, u32[]{:S(2)}, u32[]{:S(2)}) %all-to-all-start.1) | async-done | bytes 327712 | tf_op jit(solution)/shard_map/all_to_all | solution.py:475
  69.1 4.0 %shard_map.132 = (bf16[4,136,640]{2,1,0:T(8,128)(2,1)S(1)}, bf16[4,136,640]{2,1,0:T(8,128)(2,1)}) custom-call(f32[2,128,640]{2,1,0:T(8,128)S(1)} %get-tuple-element.62.base, f32[2,128,640]{2,1,0:T(8,128)S(1)} %get-tuple-element.63.ahead, bf16[2,128,256]{2,1,0:T(8,128)(2,1)S(1)} %get-tuple-element.56.maps, bf16[2,128,640]{2,1,0:T(8,128)(2,1)S(1)} %bitcast.22, ...), custom_call_target="tpu_custom_call" | custom-call | flops 268435456 | bytes 4194304 | tf_op jit(solution)/shard_map/pallas_call | solution.py:44
  73.1 3.1 %collective-permute-start.9 = (bf16[4,136,640]{2,1,0:T(8,128)(2,1)}, bf16[4,136,640]{2,1,0:T(8,128)(2,1)S(1)}, u32[]{:S(2)}, u32[]{:S(2)}) collective-permute-start(bf16[4,136,640]{2,1,0:T(8,128)(2,1)} %get-tuple-element.66), channel_id=1, source_target_pairs={{0,16},{16,0},{1,17},{17,1},{2,18},{18,2},{3,19},{19,3},{4,20},{20... | collective-permute-start | bytes 2088968 | tf_op jit(solution)/shard_map/ppermute | solution.py:484
  76.2 2.0 %collective-permute-done.9.arrived = bf16[4,136,640]{2,1,0:T(8,128)(2,1)S(1)} collective-permute-done((bf16[4,136,640]{2,1,0:T(8,128)(2,1)}, bf16[4,136,640]{2,1,0:T(8,128)(2,1)S(1)}, u32[]{:S(2)}, u32[]{:S(2)}) %collective-permute-start.9) | collective-permute-done | bytes 696352 | tf_op jit(solution)/shard_map/ppermute | solution.py:484
  78.4 2.1 %collective-permute-start.11 = (bf16[136,640]{1,0:T(8,128)(2,1)S(1)}, bf16[136,640]{1,0:T(8,128)(2,1)S(1)}, u32[]{:S(2)}, u32[]{:S(2)}) collective-permute-start(bf16[136,640]{1,0:T(8,128)(2,1)S(1)} %get-tuple-element.69), channel_id=1, source_target_pairs={{0,64},{32,96},{64,0},{96,32},{1,65},{33,97},{65,1},{97,33},{2,66}... | collective-permute-start | bytes 522248 | tf_op jit(solution)/shard_map/ppermute | solution.py:491
  81.3 4.5 %collective-permute-done.10.refs_0_ = bf16[136,640]{1,0:T(8,128)(2,1)S(1)} collective-permute-done((bf16[136,640]{1,0:T(8,128)(2,1)S(1)}, bf16[136,640]{1,0:T(8,128)(2,1)S(1)}, u32[]{:S(2)}, u32[]{:S(2)}) %collective-permute-start.10) | collective-permute-done | bytes 174112 | tf_op jit(solution)/shard_map/ppermute | solution.py:491
  85.7 2.7 %collective-permute-done.11.refs_1_ = bf16[136,640]{1,0:T(8,128)(2,1)S(1)} collective-permute-done((bf16[136,640]{1,0:T(8,128)(2,1)S(1)}, bf16[136,640]{1,0:T(8,128)(2,1)S(1)}, u32[]{:S(2)}, u32[]{:S(2)}) %collective-permute-start.11) | collective-permute-done | bytes 174112 | tf_op jit(solution)/shard_map/ppermute | solution.py:491
  91.5 5.6 %collective-permute-done.13.piece = bf16[128,640]{1,0:T(8,128)(2,1)S(1)} collective-permute-done((bf16[128,640]{1,0:T(8,128)(2,1)S(1)}, bf16[128,640]{1,0:T(8,128)(2,1)S(1)}, u32[]{:S(2)}, u32[]{:S(2)}) %collective-permute-start.13) | collective-permute-done | bytes 163872 | tf_op jit(solution)/shard_map/ppermute | solution.py:546
  97.1 4.1 %collective-permute-start.17 = (bf16[136,640]{1,0:T(8,128)(2,1)S(1)}, bf16[136,640]{1,0:T(8,128)(2,1)S(1)}, u32[]{:S(2)}, u32[]{:S(2)}) collective-permute-start(bf16[136,640]{1,0:T(8,128)(2,1)S(1)} %constant_dynamic-update-slice_fusion.refs_0_), channel_id=1, source_target_pairs={{0,96},{32,0},{64,32},{96,64},{1,97},{33,1},{65,33},{97,65},{2,98}... | collective-permute-start | bytes 522248 | tf_op jit(solution)/shard_map/ppermute | solution.py:406
  102.5 2.0 %collective-permute-start.21 = (bf16[136,640]{1,0:T(8,128)(2,1)S(1)}, bf16[136,640]{1,0:T(8,128)(2,1)S(1)}, u32[]{:S(2)}, u32[]{:S(2)}) collective-permute-start(bf16[136,640]{1,0:T(8,128)(2,1)S(1)} %constant_dynamic-update-slice_fusion.refs_0_), channel_id=1, source_target_pairs={{0,16},{16,0},{1,17},{17,1},{2,18},{18,2},{3,19},{19,3},{4,20},{20... | collective-permute-start | bytes 522248 | tf_op jit(solution)/shard_map/ppermute | solution.py:412
  104.5 5.2 %collective-permute-start.20 = (bf16[136,640]{1,0:T(8,128)(2,1)S(1)}, bf16[136,640]{1,0:T(8,128)(2,1)S(1)}, u32[]{:S(2)}, u32[]{:S(2)}) collective-permute-start(bf16[136,640]{1,0:T(8,128)(2,1)S(1)} %collective-permute-done.17.refs_2_), channel_id=1, source_target_pairs={{0,16},{16,0},{1,17},{17,1},{2,18},{18,2},{3,19},{19,3},{4,20},{20... | collective-permute-start | bytes 522248 | tf_op jit(solution)/shard_map/ppermute | solution.py:412
  113.0 2.8 %shard_map.135 = (bf16[1,272,640]{2,1,0:T(8,128)(2,1)S(1)}, f32[272,128]{1,0:T(8,128)S(1)}, f32[272,10]{1,0:T(8,128)S(1)}, f32[272,256]{1,0:T(8,128)S(1)}, f32[2...) custom-call(bf16[136,640]{1,0:T(8,128)(2,1)S(1)} %constant_dynamic-update-slice_fusion.refs_0_, ...), custom_call_target="tpu_custom_call" | custom-call | flops 268435456 | bytes 4194304 | tf_op jit(solution)/shard_map/pallas_call | solution.py:44
  115.8 3.4 %shard_map.136 = (bf16[3,272,640]{2,1,0:T(8,128)(2,1)S(1)}, f32[256,128]{1,0:T(8,128)S(1)}, bf16[2,128,640]{2,1,0:T(8,128)(2,1)S(1)}, bf16[2,128,256]{2,1,0:T(8,...) custom-call(bf16[136,640]{1,0:T(8,128)(2,1)S(1)} %collective-permute-done.15.refs_, ...), custom_call_target="tpu_custom_call" | custom-call | flops 268435456 | bytes 4194304 | tf_op jit(solution)/shard_map/pallas_call | solution.py:44
  119.2 16.6 %all_to_all.21.arrived = bf16[16,16,768]{2,1,0:T(8,128)(2,1)S(1)} all-to-all(bf16[16,16,768]{2,1,0:T(8,128)(2,1)S(1)} %bitcast.29), channel_id=1, replica_groups=mesh['pipe'=2,'chip'=4,'core'=2,'seq_0'=8,'seq_1'=2] {'seq_1','seq_0'}, dimensions={0} | all-to-all | bytes 786432 | tf_op jit(solution)/shard_map/all_to_all | solution.py:461
  136.9 5.9 %all-to-all-start.3 = ((bf16[16,16,640]{2,1,0:T(8,128)(2,1)}), bf16[16,16,640]{2,1,0:T(8,128)(2,1)S(1)}, u32[]{:S(2)}, u32[]{:S(2)}) async-start(bf16[16,16,640]{2,1,0:T(8,128)(2,1)} %shard_map.139), calls=%async_computation.3 | async-start | bytes 655360 | tf_op jit(solution)/shard_map/all_to_all | solution.py:475
  142.8 3.2 %shard_map.137.gate = f32[256,640]{1,0:T(8,128)S(1)} custom-call(bf16[1,272,640]{2,1,0:T(8,128)(2,1)S(1)} %get-tuple-element.81.near, bf16[3,272,640]{2,1,0:T(8,128)(2,1)S(1)} %get-tuple-element.82.far, f32[256,128]{1,0:T(8,128)S(1)} %get-tuple-element.83.scales, bf16[2560,640]{1,0:T(8,128)(2,1)} %bitcast.43), custom_call_target="tpu_custom_call" | custom-call | flops 268435456 | bytes 4194304 | tf_op jit(solution)/shard_map/pallas_call | solution.py:44
  146.9 5.2 %all-to-all-done.3 = bf16[16,16,640]{2,1,0:T(8,128)(2,1)S(1)} async-done(((bf16[16,16,640]{2,1,0:T(8,128)(2,1)}), bf16[16,16,640]{2,1,0:T(8,128)(2,1)S(1)}, u32[]{:S(2)}, u32[]{:S(2)}) %all-to-all-start.3) | async-done | bytes 327712 | tf_op jit(solution)/shard_map/all_to_all | solution.py:475
  152.1 3.3 %shard_map.140 = (bf16[4,136,640]{2,1,0:T(8,128)(2,1)S(1)}, bf16[4,136,640]{2,1,0:T(8,128)(2,1)S(1)}) custom-call(f32[2,128,640]{2,1,0:T(8,128)S(1)} %get-tuple-element.84.base, f32[2,128,640]{2,1,0:T(8,128)S(1)} %get-tuple-element.85.ahead, bf16[2,128,256]{2,1,0:T(8,128)(2,1)S(1)} %get-tuple-element.78.maps, bf16[2,128,640]{2,1,0:T(8,128)(2,1)S(1)} %bitcast.23, ...), custom_call_target="tpu_custom_call" | custom-call | flops 268435456 | bytes 4194304 | tf_op jit(solution)/shard_map/pallas_call | solution.py:44
  155.5 3.1 %collective-permute-start.22 = (bf16[4,136,640]{2,1,0:T(8,128)(2,1)S(1)}, bf16[4,136,640]{2,1,0:T(8,128)(2,1)S(1)}, u32[]{:S(2)}, u32[]{:S(2)}) collective-permute-start(bf16[4,136,640]{2,1,0:T(8,128)(2,1)S(1)} %get-tuple-element.88), channel_id=1, source_target_pairs={{0,16},{16,0},{1,17},{17,1},{2,18},{18,2},{3,19},{19,3},{4,20},{20... | collective-permute-start | bytes 2088968 | tf_op jit(solution)/shard_map/ppermute | solution.py:484
  158.6 1.8 %collective-permute-done.22.arrived = bf16[4,136,640]{2,1,0:T(8,128)(2,1)S(1)} collective-permute-done((bf16[4,136,640]{2,1,0:T(8,128)(2,1)S(1)}, bf16[4,136,640]{2,1,0:T(8,128)(2,1)S(1)}, u32[]{:S(2)}, u32[]{:S(2)}) %collective-permute-start.22) | collective-permute-done | bytes 696352 | tf_op jit(solution)/shard_map/ppermute | solution.py:484
  160.6 1.7 collective-permute-start.24
  163.5 4.8 %collective-permute-done.23.refs_0_ = bf16[136,640]{1,0:T(8,128)(2,1)S(1)} collective-permute-done((bf16[136,640]{1,0:T(8,128)(2,1)S(1)}, bf16[136,640]{1,0:T(8,128)(2,1)S(1)}, u32[]{:S(2)}, u32[]{:S(2)}) %collective-permute-start.23) | collective-permute-done | bytes 174112 | tf_op jit(solution)/shard_map/ppermute | solution.py:491
  168.3 2.0 %collective-permute-done.24.refs_1_ = bf16[136,640]{1,0:T(8,128)(2,1)S(1)} collective-permute-done((bf16[136,640]{1,0:T(8,128)(2,1)S(1)}, bf16[136,640]{1,0:T(8,128)(2,1)S(1)}, u32[]{:S(2)}, u32[]{:S(2)}) %collective-permute-start.24) | collective-permute-done | bytes 174112 | tf_op jit(solution)/shard_map/ppermute | solution.py:491
  (76 shorter events, 28.3 us)
Async XLA Ops:
  0.0 26.7 %copy-start.8 = (f32[1,10]{1,0:T(1,128)S(1)}, f32[1,10]{1,0:T(1,128)}, u32[]{:S(2)}) copy-start(f32[1,10]{1,0:T(1,128)} %refs_14_.3) | copy-start | bytes 124
  0.0 26.7 %copy-start.5 = (f32[1,5,256]{2,0,1:T(1,128)S(1)}, f32[1,5,256]{2,0,1:T(1,128)}, u32[]{:S(2)}) copy-start(f32[1,5,256]{2,0,1:T(1,128)} %param.20) | copy-start | bytes 15364
  0.0 26.7 %copy-start.4 = (f32[1,5,640]{2,0,1:T(1,128)S(1)}, f32[1,5,640]{2,0,1:T(1,128)}, u32[]{:S(2)}) copy-start(f32[1,5,640]{2,0,1:T(1,128)} %param.19) | copy-start | bytes 38404
  1.2 3.6 %collective-permute-start = (bf16[2,8,320]{2,1,0:T(8,128)(2,1)S(1)}, bf16[2,8,320]{2,1,0:T(8,128)(2,1)S(1)}, u32[]{:S(2)}, u32[]{:S(2)}) collective-permute-start(bf16[2,8,320]{2,1,0:T(8,128)(2,1)S(1)} %slice.32), channel_id=1, source_target_pairs={{0,1},{1,2},{2,3},{3,4},{4,5},{5,6},{6,7},{7,8},{8,9},{9,10},{10,1... | collective-permute-start | bytes 30728 | tf_op jit(solution)/shard_map/ppermute | solution.py:529
  4.9 2.6 %collective-permute-start.1 = (bf16[136,320]{1,0:T(8,128)(2,1)S(1)}, bf16[136,320]{1,0:T(8,128)(2,1)S(1)}, u32[]{:S(2)}, u32[]{:S(2)}) collective-permute-start(bf16[136,320]{1,0:T(8,128)(2,1)S(1)} %get-tuple-element.94), channel_id=1, source_target_pairs={{0,16},{16,0},{1,17},{17,1},{2,18},{18,2},{3,19},{19,3},{4,20},{20... | collective-permute-start | bytes 261128 | tf_op jit(solution)/shard_map/ppermute | solution.py:532
  7.6 6.2 %collective-permute-start.4 = (bf16[136,640]{1,0:T(8,128)(2,1)S(1)}, bf16[136,640]{1,0:T(8,128)(2,1)S(1)}, u32[]{:S(2)}, u32[]{:S(2)}) collective-permute-start(bf16[136,640]{1,0:T(8,128)(2,1)S(1)} %maximum_select_fusion.1.refs_0_), channel_id=1, source_target_pairs={{0,96},{32,0},{64,32},{96,64},{1,97},{33,1},{65,33},{97,65},{2,98}... | collective-permute-start | bytes 522248 | tf_op jit(solution)/shard_map/ppermute | solution.py:406
  10.4 8.4 %collective-permute-start.3 = (bf16[136,640]{1,0:T(8,128)(2,1)S(1)}, bf16[136,640]{1,0:T(8,128)(2,1)S(1)}, u32[]{:S(2)}, u32[]{:S(2)}) collective-permute-start(bf16[136,640]{1,0:T(8,128)(2,1)S(1)} %maximum_select_fusion.1.refs_0_), channel_id=1, source_target_pairs={{0,32},{32,64},{64,96},{96,0},{1,33},{33,65},{65,97},{97,1},{2,34}... | collective-permute-start | bytes 522248 | tf_op jit(solution)/shard_map/ppermute | solution.py:406
  10.4 11.8 %collective-permute-start.2 = (bf16[136,640]{1,0:T(8,128)(2,1)S(1)}, bf16[136,640]{1,0:T(8,128)(2,1)S(1)}, u32[]{:S(2)}, u32[]{:S(2)}) collective-permute-start(bf16[136,640]{1,0:T(8,128)(2,1)S(1)} %maximum_select_fusion.1.refs_0_), channel_id=1, source_target_pairs={{0,64},{32,96},{64,0},{96,32},{1,65},{33,97},{65,1},{97,33},{2,66}... | collective-permute-start | bytes 522248 | tf_op jit(solution)/shard_map/ppermute | solution.py:406
  12.1 10.1 %collective-permute-start.8 = (bf16[136,640]{1,0:T(8,128)(2,1)S(1)}, bf16[136,640]{1,0:T(8,128)(2,1)S(1)}, u32[]{:S(2)}, u32[]{:S(2)}) collective-permute-start(bf16[136,640]{1,0:T(8,128)(2,1)S(1)} %maximum_select_fusion.1.refs_0_), channel_id=1, source_target_pairs={{0,16},{16,0},{1,17},{17,1},{2,18},{18,2},{3,19},{19,3},{4,20},{20... | collective-permute-start | bytes 522248 | tf_op jit(solution)/shard_map/ppermute | solution.py:412
  13.8 12.8 %collective-permute-start.7 = (bf16[136,640]{1,0:T(8,128)(2,1)S(1)}, bf16[136,640]{1,0:T(8,128)(2,1)S(1)}, u32[]{:S(2)}, u32[]{:S(2)}) collective-permute-start(bf16[136,640]{1,0:T(8,128)(2,1)S(1)} %collective-permute-done.4.refs_2_), channel_id=1, source_target_pairs={{0,16},{16,0},{1,17},{17,1},{2,18},{18,2},{3,19},{19,3},{4,20},{20... | collective-permute-start | bytes 522248 | tf_op jit(solution)/shard_map/ppermute | solution.py:412
  18.8 7.8 %collective-permute-start.6 = (bf16[136,640]{1,0:T(8,128)(2,1)S(1)}, bf16[136,640]{1,0:T(8,128)(2,1)S(1)}, u32[]{:S(2)}, u32[]{:S(2)}) collective-permute-start(bf16[136,640]{1,0:T(8,128)(2,1)S(1)} %collective-permute-done.3.refs_1_), channel_id=1, source_target_pairs={{0,16},{16,0},{1,17},{17,1},{2,18},{18,2},{3,19},{19,3},{4,20},{20... | collective-permute-start | bytes 522248 | tf_op jit(solution)/shard_map/ppermute | solution.py:412
  22.2 4.5 %collective-permute-start.5 = (bf16[136,640]{1,0:T(8,128)(2,1)S(1)}, bf16[136,640]{1,0:T(8,128)(2,1)S(1)}, u32[]{:S(2)}, u32[]{:S(2)}) collective-permute-start(bf16[136,640]{1,0:T(8,128)(2,1)S(1)} %collective-permute-done.2.refs_0_), channel_id=1, source_target_pairs={{0,16},{16,0},{1,17},{17,1},{2,18},{18,2},{3,19},{19,3},{4,20},{20... | collective-permute-start | bytes 522248 | tf_op jit(solution)/shard_map/ppermute | solution.py:412
  53.6 15.4 %all-to-all-start.1 = ((bf16[16,16,640]{2,1,0:T(8,128)(2,1)}), bf16[16,16,640]{2,1,0:T(8,128)(2,1)S(1)}, u32[]{:S(2)}, u32[]{:S(2)}) async-start(bf16[16,16,640]{2,1,0:T(8,128)(2,1)} %shard_map.131), calls=%async_computation.1 | async-start | bytes 655360 | tf_op jit(solution)/shard_map/all_to_all | solution.py:475
  73.1 5.1 %collective-permute-start.9 = (bf16[4,136,640]{2,1,0:T(8,128)(2,1)}, bf16[4,136,640]{2,1,0:T(8,128)(2,1)S(1)}, u32[]{:S(2)}, u32[]{:S(2)}) collective-permute-start(bf16[4,136,640]{2,1,0:T(8,128)(2,1)} %get-tuple-element.66), channel_id=1, source_target_pairs={{0,16},{16,0},{1,17},{17,1},{2,18},{18,2},{3,19},{19,3},{4,20},{20... | collective-permute-start | bytes 2088968 | tf_op jit(solution)/shard_map/ppermute | solution.py:484
  78.3 7.4 %collective-permute-start.10 = (bf16[136,640]{1,0:T(8,128)(2,1)S(1)}, bf16[136,640]{1,0:T(8,128)(2,1)S(1)}, u32[]{:S(2)}, u32[]{:S(2)}) collective-permute-start(bf16[136,640]{1,0:T(8,128)(2,1)S(1)} %get-tuple-element.68), channel_id=1, source_target_pairs={{0,32},{32,64},{64,96},{96,0},{1,33},{33,65},{65,97},{97,1},{2,34}... | collective-permute-start | bytes 522248 | tf_op jit(solution)/shard_map/ppermute | solution.py:491
  78.4 10.1 %collective-permute-start.11 = (bf16[136,640]{1,0:T(8,128)(2,1)S(1)}, bf16[136,640]{1,0:T(8,128)(2,1)S(1)}, u32[]{:S(2)}, u32[]{:S(2)}) collective-permute-start(bf16[136,640]{1,0:T(8,128)(2,1)S(1)} %get-tuple-element.69), channel_id=1, source_target_pairs={{0,64},{32,96},{64,0},{96,32},{1,65},{33,97},{65,1},{97,33},{2,66}... | collective-permute-start | bytes 522248 | tf_op jit(solution)/shard_map/ppermute | solution.py:491
  80.6 8.8 %collective-permute-start.12 = (bf16[136,640]{1,0:T(8,128)(2,1)S(1)}, bf16[136,640]{1,0:T(8,128)(2,1)S(1)}, u32[]{:S(2)}, u32[]{:S(2)}) collective-permute-start(bf16[136,640]{1,0:T(8,128)(2,1)S(1)} %get-tuple-element.70), channel_id=1, source_target_pairs={{0,96},{32,0},{64,32},{96,64},{1,97},{33,1},{65,33},{97,65},{2,98}... | collective-permute-start | bytes 522248 | tf_op jit(solution)/shard_map/ppermute | solution.py:491
  89.5 7.6 %collective-permute-start.13 = (bf16[128,640]{1,0:T(8,128)(2,1)S(1)}, bf16[128,640]{1,0:T(8,128)(2,1)S(1)}, u32[]{:S(2)}, u32[]{:S(2)}) collective-permute-start(bf16[128,640]{1,0:T(8,128)(2,1)S(1)} %shard_map.134), channel_id=1, source_target_pairs={{0,128},{1,129},{2,130},{3,131},{4,132},{5,133},{6,134},{7,135},{8... | collective-permute-start | bytes 491528 | tf_op jit(solution)/shard_map/ppermute | solution.py:546
  90.8 0.7 collective-permute-start.14
  97.1 7.4 %collective-permute-start.17 = (bf16[136,640]{1,0:T(8,128)(2,1)S(1)}, bf16[136,640]{1,0:T(8,128)(2,1)S(1)}, u32[]{:S(2)}, u32[]{:S(2)}) collective-permute-start(bf16[136,640]{1,0:T(8,128)(2,1)S(1)} %constant_dynamic-update-slice_fusion.refs_0_), channel_id=1, source_target_pairs={{0,96},{32,0},{64,32},{96,64},{1,97},{33,1},{65,33},{97,65},{2,98}... | collective-permute-start | bytes 522248 | tf_op jit(solution)/shard_map/ppermute | solution.py:406
  101.2 10.1 %collective-permute-start.16 = (bf16[136,640]{1,0:T(8,128)(2,1)S(1)}, bf16[136,640]{1,0:T(8,128)(2,1)S(1)}, u32[]{:S(2)}, u32[]{:S(2)}) collective-permute-start(bf16[136,640]{1,0:T(8,128)(2,1)S(1)} %constant_dynamic-update-slice_fusion.refs_0_), channel_id=1, source_target_pairs={{0,32},{32,64},{64,96},{96,0},{1,33},{33,65},{65,97},{97,1},{2,34}... | collective-permute-start | bytes 522248 | tf_op jit(solution)/shard_map/ppermute | solution.py:406
  101.2 11.8 %collective-permute-start.15 = (bf16[136,640]{1,0:T(8,128)(2,1)S(1)}, bf16[136,640]{1,0:T(8,128)(2,1)S(1)}, u32[]{:S(2)}, u32[]{:S(2)}) collective-permute-start(bf16[136,640]{1,0:T(8,128)(2,1)S(1)} %constant_dynamic-update-slice_fusion.refs_0_), channel_id=1, source_target_pairs={{0,64},{32,96},{64,0},{96,32},{1,65},{33,97},{65,1},{97,33},{2,66}... | collective-permute-start | bytes 522248 | tf_op jit(solution)/shard_map/ppermute | solution.py:406
  102.5 10.5 %collective-permute-start.21 = (bf16[136,640]{1,0:T(8,128)(2,1)S(1)}, bf16[136,640]{1,0:T(8,128)(2,1)S(1)}, u32[]{:S(2)}, u32[]{:S(2)}) collective-permute-start(bf16[136,640]{1,0:T(8,128)(2,1)S(1)} %constant_dynamic-update-slice_fusion.refs_0_), channel_id=1, source_target_pairs={{0,16},{16,0},{1,17},{17,1},{2,18},{18,2},{3,19},{19,3},{4,20},{20... | collective-permute-start | bytes 522248 | tf_op jit(solution)/shard_map/ppermute | solution.py:412
  104.5 11.3 %collective-permute-start.20 = (bf16[136,640]{1,0:T(8,128)(2,1)S(1)}, bf16[136,640]{1,0:T(8,128)(2,1)S(1)}, u32[]{:S(2)}, u32[]{:S(2)}) collective-permute-start(bf16[136,640]{1,0:T(8,128)(2,1)S(1)} %collective-permute-done.17.refs_2_), channel_id=1, source_target_pairs={{0,16},{16,0},{1,17},{17,1},{2,18},{18,2},{3,19},{19,3},{4,20},{20... | collective-permute-start | bytes 522248 | tf_op jit(solution)/shard_map/ppermute | solution.py:412
  111.3 4.6 %collective-permute-start.19 = (bf16[136,640]{1,0:T(8,128)(2,1)S(1)}, bf16[136,640]{1,0:T(8,128)(2,1)S(1)}, u32[]{:S(2)}, u32[]{:S(2)}) collective-permute-start(bf16[136,640]{1,0:T(8,128)(2,1)S(1)} %collective-permute-done.16.refs_1_), channel_id=1, source_target_pairs={{0,16},{16,0},{1,17},{17,1},{2,18},{18,2},{3,19},{19,3},{4,20},{20... | collective-permute-start | bytes 522248 | tf_op jit(solution)/shard_map/ppermute | solution.py:412
  113.0 2.9 %collective-permute-start.18 = (bf16[136,640]{1,0:T(8,128)(2,1)S(1)}, bf16[136,640]{1,0:T(8,128)(2,1)S(1)}, u32[]{:S(2)}, u32[]{:S(2)}) collective-permute-start(bf16[136,640]{1,0:T(8,128)(2,1)S(1)} %collective-permute-done.15.refs_0_), channel_id=1, source_target_pairs={{0,16},{16,0},{1,17},{17,1},{2,18},{18,2},{3,19},{19,3},{4,20},{20... | collective-permute-start | bytes 522248 | tf_op jit(solution)/shard_map/ppermute | solution.py:412
  136.9 15.3 %all-to-all-start.3 = ((bf16[16,16,640]{2,1,0:T(8,128)(2,1)}), bf16[16,16,640]{2,1,0:T(8,128)(2,1)S(1)}, u32[]{:S(2)}, u32[]{:S(2)}) async-start(bf16[16,16,640]{2,1,0:T(8,128)(2,1)} %shard_map.139), calls=%async_computation.3 | async-start | bytes 655360 | tf_op jit(solution)/shard_map/all_to_all | solution.py:475
  155.5 4.9 %collective-permute-start.22 = (bf16[4,136,640]{2,1,0:T(8,128)(2,1)S(1)}, bf16[4,136,640]{2,1,0:T(8,128)(2,1)S(1)}, u32[]{:S(2)}, u32[]{:S(2)}) collective-permute-start(bf16[4,136,640]{2,1,0:T(8,128)(2,1)S(1)} %get-tuple-element.88), channel_id=1, source_target_pairs={{0,16},{16,0},{1,17},{17,1},{2,18},{18,2},{3,19},{19,3},{4,20},{20... | collective-permute-start | bytes 2088968 | tf_op jit(solution)/shard_map/ppermute | solution.py:484
  160.5 7.7 %collective-permute-start.23 = (bf16[136,640]{1,0:T(8,128)(2,1)S(1)}, bf16[136,640]{1,0:T(8,128)(2,1)S(1)}, u32[]{:S(2)}, u32[]{:S(2)}) collective-permute-start(bf16[136,640]{1,0:T(8,128)(2,1)S(1)} %get-tuple-element.90), channel_id=1, source_target_pairs={{0,32},{32,64},{64,96},{96,0},{1,33},{33,65},{65,97},{97,1},{2,34}... | collective-permute-start | bytes 522248 | tf_op jit(solution)/shard_map/ppermute | solution.py:491
  160.6 9.7 %collective-permute-start.24 = (bf16[136,640]{1,0:T(8,128)(2,1)S(1)}, bf16[136,640]{1,0:T(8,128)(2,1)S(1)}, u32[]{:S(2)}, u32[]{:S(2)}) collective-permute-start(bf16[136,640]{1,0:T(8,128)(2,1)S(1)} %get-tuple-element.91), channel_id=1, source_target_pairs={{0,64},{32,96},{64,0},{96,32},{1,65},{33,97},{65,1},{97,33},{2,66}... | collective-permute-start | bytes 522248 | tf_op jit(solution)/shard_map/ppermute | solution.py:491
  162.4 9.2 %collective-permute-start.25 = (bf16[136,640]{1,0:T(8,128)(2,1)S(1)}, bf16[136,640]{1,0:T(8,128)(2,1)S(1)}, u32[]{:S(2)}, u32[]{:S(2)}) collective-permute-start(bf16[136,640]{1,0:T(8,128)(2,1)S(1)} %get-tuple-element.92), channel_id=1, source_target_pairs={{0,96},{32,0},{64,32},{96,64},{1,97},{33,1},{65,33},{97,65},{2,98}... | collective-permute-start | bytes 522248 | tf_op jit(solution)/shard_map/ppermute | solution.py:491
  171.8 2.5 %collective-permute-start.26 = (bf16[128,320]{1,0:T(8,128)(2,1)S(1)}, bf16[128,320]{1,0:T(8,128)(2,1)S(1)}, u32[]{:S(2)}, u32[]{:S(2)}) collective-permute-start(bf16[128,320]{1,0:T(8,128)(2,1)S(1)} %get-tuple-element.96), channel_id=1, source_target_pairs={{0,16},{16,0},{1,17},{17,1},{2,18},{18,2},{3,19},{19,3},{4,20},{20... | collective-permute-start | bytes 245768 | tf_op jit(solution)/shard_map/ppermute | solution.py:558
  (7 other events, 100.3 us)

commit v6 on v5

--- a/solution.py
+++ b/solution.py
@@ -11,6 +11,7 @@
 EDGE = 8
 NEAR = (0,)
 FAR = (2, 1, 3)
+LEAVING = (2, 1, 3, 0)
 SEQ = ("seq_0", "seq_1")
 CROSS = ("seq_1", "seq_0")
 TENSOR = ("chip", "core")
@@ -73,12 +74,12 @@
     return [lax.rem(chip - step + count, count) for step in steps]
 
 
-def fetch_columns(source, target, semaphores):
+def fetch_columns(source, target, semaphores, blocks):
     parts = semaphores.shape[0]
     size = target.shape[1] // parts
     copies = [
         pltpu.make_async_copy(
-            source.at[:, pl.ds(part * size, size)],
+            source.at[:, pl.ds(blocks[part] * size, size)],
             target.at[:, pl.ds(part * size, size)],
             semaphores.at[part],
         )
@@ -320,44 +321,42 @@
     return jnp.transpose(block)[:8]
 
 
-def output_terms(base, ahead, maps, entering, gain, out_hbm, mine, given, out_w, out_sems):
+def output_terms(base, ahead, maps, entering, gain, out_hbm, *refs):
+    count = len(LEAVING)
+    mine, given, (out_w, out_sems) = refs[:count], refs[count : 2 * count], refs[2 * count :]
     n = maps.shape[2] // 2
-    count, _, width = mine.shape
-    copies = fetch_columns(out_hbm, out_w, out_sems)
+    width = mine[0].shape[1]
+    copies = fetch_columns(out_hbm, out_w, out_sems, blocks_of([-step for step in LEAVING]))
     rows = base.shape[1]
     scaled = []
-    for m, term in enumerate((mine, given)):
+    for m, terms in enumerate((mine, given)):
         across = dot(maps[m, :, n:], entering[m])
         gated = base[m] + across * ahead[m]
         squares = jnp.sum(gated * gated, axis=1, keepdims=True)
         scaled.append((gated * gain[...]).astype(BF16))
         block = squares_rows(squares)
-        block = jnp.concatenate([block, jnp.zeros((8, width - 128), F32)], 1).astype(term.dtype)
-        for b in range(count):
-            term[b, rows:] = block
+        block = jnp.concatenate([block, jnp.zeros((8, width - 128), F32)], 1).astype(BF16)
+        for term in terms:
+            term[rows:] = block
     scaled = jnp.concatenate(scaled)
-    for b in range(count):
-        copies[b].wait()
-        value = dot(scaled, out_w[:, b * width : (b + 1) * width])
-        mine[b, :rows] = value[:rows].astype(mine.dtype)
-        given[b, :rows] = value[rows:].astype(given.dtype)
-
-
-def merge_cores(chip_ref, mine, arrived, kept, *sent):
-    count, tall, width = mine.shape
-    rows = tall - 8
-    chip = chip_ref[0]
-    kept[:rows] = mine[chip, :rows].astype(F32) + arrived[chip, :rows].astype(F32)
-    both = jnp.sum(mine[0, rows:].astype(F32) + arrived[0, rows:].astype(F32), axis=0, keepdims=True)
+    for part in range(count):
+        copies[part].wait()
+        value = dot(scaled, out_w[:, part * width : (part + 1) * width]).astype(BF16)
+        mine[part][:rows] = value[:rows]
+        given[part][:rows] = value[rows:]
+
+
+def merge_cores(mine, arrived, merged):
+    width = mine.shape[1]
+    rows = mine.shape[0] - 8
+    total = mine[...].astype(F32) + arrived[...].astype(F32)
+    merged[:rows] = total[:rows].astype(merged.dtype)
+    both = jnp.sum(total[rows:], axis=0, keepdims=True)
     row = iota((8, width), 0)
-    kept[rows:] = jnp.where(row == 0, both, 0.0)
     block = jnp.zeros((8, width), F32)
     for index, part in enumerate(split_bf16(both, 3)):
         block = jnp.where(row == index, part.astype(F32), block)
-    for k in range(1, count):
-        b = lax.rem(chip + k, count)
-        sent[k - 1][:rows] = (mine[b, :rows].astype(F32) + arrived[b, :rows].astype(F32)).astype(BF16)
-        sent[k - 1][rows:] = block.astype(BF16)
+    merged[rows:] = block.astype(merged.dtype)
 
 
 def finish(piece, kept, *refs):
@@ -390,7 +389,6 @@
         inner_gain,
         out_weight,
     ) = weights
-    chip = lax.axis_index("chip").reshape(1)
     count = lax.axis_size("chip")
     members = lax.axis_size(SEQ)
     rows, block = piece.shape
@@ -474,21 +472,23 @@
     (back,) = local(scan_states, [arrived], [((members, tall // members, width), BF16)])
     back = lax.all_to_all(back, CROSS, 0, 0, tiled=True)
     entering = back.reshape(2, rows, width)
-    mine, given = local(
+    terms = local(
         output_terms,
         [base, ahead, maps, entering, inner_gain[None], out_weight],
-        [((count, rows + 8, block), BF16)] * 2,
+        [((rows + 8, block), BF16)] * (2 * count),
         weights=1,
         scratch=room(out_weight, count),
     )
-    taken = lax.ppermute(given, "core", SWAP)
-    kept, *leaving = local(
-        merge_cores,
-        [chip, mine, taken],
-        [((rows + 8, block), F32)] + [((rows + 8, block), BF16)] * (count - 1),
-        scalars=1,
-    )
-    parts = [lax.ppermute(part, "chip", ring(count, k + 1)) for k, part in enumerate(leaving)]
+    parts = []
+    for step, mine, given in zip(LEAVING, terms[:count], terms[count:]):
+        kind = BF16 if step else F32
+        (part,) = local(
+            merge_cores,
+            [mine, lax.ppermute(given, "core", SWAP)],
+            [((rows + 8, block), kind)],
+        )
+        parts.append(lax.ppermute(part, "chip", ring(count, step)) if step else part)
+    kept = parts.pop()
     return local(finish, [piece, kept, *parts], [((rows, block), BF16)])[0]
 
 

time: 176 us -> 171 us (0.972)
  waiting for transfers between devices: 40.8 us -> 36.1 us
    ppermute x8 -> x14, waiting for transfers between devices: 19.9 us -> 15.5 us  [the longest x6 14.6 us: layer(): lax.ppermute(part, 'chip', ring(count, step))]
    ppermute x8 -> x14, starting transfers between devices: 12 us -> 15.7 us  [the longest x6 8.26 us: layer(): lax.ppermute(part, 'chip', ring(count, step))]
    ppermute x6, starting transfers between devices: 9.81 us -> 6.76 us  [moved(): return lax.ppermute(spread_rows, 'chip', ring(count, step))]
    pallas_call x16 -> x22, Pallas kernels: 30.7 us -> 30.2 us  [local(): pl.pallas_call(body, out_shape=[jax.ShapeDtypeStruct(shape, kind) for sha...]
  transfers between devices with their start and end apart: 29 -> 35, of which waited for: 16 -> 14; matrix products, arithmetic and copies ran while one was open for 0% -> 0% of each run, Pallas kernels for 8% -> 8%
where the time goes in v6:
time: 171 us; the launch traced here: 170 us
  starting transfers between devices  60.6 us (35%)
  blocking collectives  39.1 us (23%)
  waiting for transfers between devices  36.1 us (21%)
  Pallas kernels  30.2 us (18%)
  local copies, waits for them, and re-layouts  3.63 us (2%)
    all_to_all x2, blocking collectives, layer(): lax.all_to_all(sent.reshape(members, tall // members, -1), CROSS, 0, 0, t...  39.1 us
    pallas_call x22, Pallas kernels, local(): pl.pallas_call(body, out_shape=[jax.ShapeDtypeStruct(shape, kind) for sha...  30.2 us
    ppermute x8, starting transfers between devices, layer(): other = {k: lax.ppermute(part, 'core', SWAP) for k, part in own.items()}  19.2 us
    ppermute x6, waiting for transfers between devices, layer(): lax.ppermute(part, 'chip', ring(count, step))  14.6 us
    all_to_all x2, starting transfers between devices, layer(): back = lax.all_to_all(back, CROSS, 0, 0, tiled=True)  12 us
    all_to_all x2, waiting for transfers between devices, layer(): back = lax.all_to_all(back, CROSS, 0, 0, tiled=True)  10.4 us
    ppermute x6, starting transfers between devices, layer(): lax.ppermute(part, 'chip', ring(count, step))  8.26 us
    ppermute x8, starting transfers between devices, layer(): lax.ppermute(given, 'core', SWAP)  7.43 us
  transfers between devices with their start and end apart: 35, of which 14 were waited for; matrix products, arithmetic and copies ran while one was open for 0% of the time, Pallas kernels for 8%

profile of v6, /device:TPU:5, one launch (start us, length us, event | category | flops | bytes accessed | tf_op | source)
XLA Modules:
  0.0 170.5 jit_solution(8151331042856449952)
XLA Ops:
  1.2 2.8 %collective-permute-start = (bf16[2,8,320]{2,1,0:T(8,128)(2,1)S(1)}, bf16[2,8,320]{2,1,0:T(8,128)(2,1)S(1)}, u32[]{:S(2)}, u32[]{:S(2)}) collective-permute-start(bf16[2,8,320]{2,1,0:T(8,128)(2,1)S(1)} %slice.32), channel_id=1, source_target_pairs={{0,1},{1,2},{2,3},{3,4},{4,5},{5,6},{6,7},{7,8},{8,9},{9,10},{10,1... | collective-permute-start | bytes 30728 | tf_op jit(solution)/shard_map/ppermute | solution.py:529
  7.6 2.8 %collective-permute-start.4 = (bf16[136,640]{1,0:T(8,128)(2,1)S(1)}, bf16[136,640]{1,0:T(8,128)(2,1)S(1)}, u32[]{:S(2)}, u32[]{:S(2)}) collective-permute-start(bf16[136,640]{1,0:T(8,128)(2,1)S(1)} %maximum_select_fusion.1.refs_0_), channel_id=1, source_target_pairs={{0,96},{32,0},{64,32},{96,64},{1,97},{33,1},{65,33},{97,65},{2,98}... | collective-permute-start | bytes 522248 | tf_op jit(solution)/shard_map/ppermute | solution.py:404
  10.4 1.6 collective-permute-start.2
  13.8 5.0 %collective-permute-start.7 = (bf16[136,640]{1,0:T(8,128)(2,1)S(1)}, bf16[136,640]{1,0:T(8,128)(2,1)S(1)}, u32[]{:S(2)}, u32[]{:S(2)}) collective-permute-start(bf16[136,640]{1,0:T(8,128)(2,1)S(1)} %collective-permute-done.4.refs_2_), channel_id=1, source_target_pairs={{0,16},{16,0},{1,17},{17,1},{2,18},{18,2},{3,19},{19,3},{4,20},{20... | collective-permute-start | bytes 522248 | tf_op jit(solution)/shard_map/ppermute | solution.py:410
  18.8 3.4 %collective-permute-start.6 = (bf16[136,640]{1,0:T(8,128)(2,1)S(1)}, bf16[136,640]{1,0:T(8,128)(2,1)S(1)}, u32[]{:S(2)}, u32[]{:S(2)}) collective-permute-start(bf16[136,640]{1,0:T(8,128)(2,1)S(1)} %collective-permute-done.3.refs_1_), channel_id=1, source_target_pairs={{0,16},{16,0},{1,17},{17,1},{2,18},{18,2},{3,19},{19,3},{4,20},{20... | collective-permute-start | bytes 522248 | tf_op jit(solution)/shard_map/ppermute | solution.py:410
  23.8 2.8 %shard_map.127 = (bf16[1,272,640]{2,1,0:T(8,128)(2,1)S(1)}, f32[272,128]{1,0:T(8,128)S(1)}, f32[272,10]{1,0:T(8,128)S(1)}, f32[272,256]{1,0:T(8,128)S(1)}, f32[2...) custom-call(bf16[136,640]{1,0:T(8,128)(2,1)S(1)} %maximum_select_fusion.1.refs_0_, ...), custom_call_target="tpu_custom_call" | custom-call | flops 268435456 | bytes 4194304 | tf_op jit(solution)/shard_map/pallas_call | solution.py:45
  26.7 3.4 %shard_map.128 = (bf16[3,272,640]{2,1,0:T(8,128)(2,1)S(1)}, f32[256,128]{1,0:T(8,128)S(1)}, bf16[2,128,640]{2,1,0:T(8,128)(2,1)S(1)}, bf16[2,128,256]{2,1,0:T(8,...) custom-call(bf16[136,640]{1,0:T(8,128)(2,1)S(1)} %collective-permute-done.2.refs_0, ...), custom_call_target="tpu_custom_call" | custom-call | flops 268435456 | bytes 4194304 | tf_op jit(solution)/shard_map/pallas_call | solution.py:45
  30.1 22.5 %all_to_all.20.arrived = bf16[16,16,768]{2,1,0:T(8,128)(2,1)S(1)} all-to-all(bf16[16,16,768]{2,1,0:T(8,128)(2,1)S(1)} %bitcast.27), channel_id=1, replica_groups=mesh['pipe'=2,'chip'=4,'core'=2,'seq_0'=8,'seq_1'=2] {'seq_1','seq_0'}, dimensions={0} | all-to-all | bytes 786432 | tf_op jit(solution)/shard_map/all_to_all | solution.py:459
  53.6 6.1 %all-to-all-start.1 = ((bf16[16,16,640]{2,1,0:T(8,128)(2,1)}), bf16[16,16,640]{2,1,0:T(8,128)(2,1)S(1)}, u32[]{:S(2)}, u32[]{:S(2)}) async-start(bf16[16,16,640]{2,1,0:T(8,128)(2,1)} %shard_map.131), calls=%async_computation.1 | async-start | bytes 655360 | tf_op jit(solution)/shard_map/all_to_all | solution.py:473
  59.7 3.2 %shard_map.129.gate = f32[256,640]{1,0:T(8,128)S(1)} custom-call(bf16[1,272,640]{2,1,0:T(8,128)(2,1)S(1)} %get-tuple-element.63.near, bf16[3,272,640]{2,1,0:T(8,128)(2,1)S(1)} %get-tuple-element.64.far, f32[256,128]{1,0:T(8,128)S(1)} %get-tuple-element.65.scales, bf16[2560,640]{1,0:T(8,128)(2,1)} %bitcast.41), custom_call_target="tpu_custom_call" | custom-call | flops 268435456 | bytes 4194304 | tf_op jit(solution)/shard_map/pallas_call | solution.py:45
  63.9 5.2 %all-to-all-done.1 = bf16[16,16,640]{2,1,0:T(8,128)(2,1)S(1)} async-done(((bf16[16,16,640]{2,1,0:T(8,128)(2,1)}), bf16[16,16,640]{2,1,0:T(8,128)(2,1)S(1)}, u32[]{:S(2)}, u32[]{:S(2)}) %all-to-all-start.1) | async-done | bytes 327712 | tf_op jit(solution)/shard_map/all_to_all | solution.py:473
  69.1 3.3 %shard_map.132 = (bf16[136,640]{1,0:T(8,128)(2,1)S(1)}, bf16[136,640]{1,0:T(8,128)(2,1)S(1)}, bf16[136,640]{1,0:T(8,128)(2,1)S(1)}, bf16[136,640]{1,0:T(8,128)(2...) custom-call(f32[2,128,640]{2,1,0:T(8,128)S(1)} %get-tuple-element.66, ...), custom_call_target="tpu_custom_call" | custom-call | flops 268435456 | bytes 4194304 | tf_op jit(solution)/shard_map/pallas_call | solution.py:45
  72.4 3.1 %collective-permute-start.10 = (bf16[136,640]{1,0:T(8,128)(2,1)S(1)}, bf16[136,640]{1,0:T(8,128)(2,1)S(1)}, u32[]{:S(2)}, u32[]{:S(2)}) collective-permute-start(bf16[136,640]{1,0:T(8,128)(2,1)S(1)} %get-tuple-element.72), channel_id=1, source_target_pairs={{0,16},{16,0},{1,17},{17,1},{2,18},{18,2},{3,19},{19,3},{4,20},{20... | collective-permute-start | bytes 522248 | tf_op jit(solution)/shard_map/ppermute | solution.py:487
  78.5 2.0 %collective-permute-start.15 = (bf16[136,640]{1,0:T(8,128)(2,1)S(1)}, bf16[136,640]{1,0:T(8,128)(2,1)S(1)}, u32[]{:S(2)}, u32[]{:S(2)}) collective-permute-start(bf16[136,640]{1,0:T(8,128)(2,1)S(1)} %shard_map.136), channel_id=1, source_target_pairs={{0,96},{32,0},{64,32},{96,64},{1,97},{33,1},{65,33},{97,65},{2,98}... | collective-permute-start | bytes 522248 | tf_op jit(solution)/shard_map/ppermute | solution.py:490
  80.5 3.3 %collective-permute-done.11.refs_0_ = bf16[136,640]{1,0:T(8,128)(2,1)S(1)} collective-permute-done((bf16[136,640]{1,0:T(8,128)(2,1)S(1)}, bf16[136,640]{1,0:T(8,128)(2,1)S(1)}, u32[]{:S(2)}, u32[]{:S(2)}) %collective-permute-start.11) | collective-permute-done | bytes 174112 | tf_op jit(solution)/shard_map/ppermute | solution.py:490
  83.9 4.4 %collective-permute-done.13.refs_1_ = bf16[136,640]{1,0:T(8,128)(2,1)S(1)} collective-permute-done((bf16[136,640]{1,0:T(8,128)(2,1)S(1)}, bf16[136,640]{1,0:T(8,128)(2,1)S(1)}, u32[]{:S(2)}, u32[]{:S(2)}) %collective-permute-start.13) | collective-permute-done | bytes 174112 | tf_op jit(solution)/shard_map/ppermute | solution.py:490
  90.4 6.7 %collective-permute-done.16.piece = bf16[128,640]{1,0:T(8,128)(2,1)S(1)} collective-permute-done((bf16[128,640]{1,0:T(8,128)(2,1)S(1)}, bf16[128,640]{1,0:T(8,128)(2,1)S(1)}, u32[]{:S(2)}, u32[]{:S(2)}) %collective-permute-start.16) | collective-permute-done | bytes 163872 | tf_op jit(solution)/shard_map/ppermute | solution.py:546
  99.4 2.2 %collective-permute-start.24 = (bf16[136,640]{1,0:T(8,128)(2,1)S(1)}, bf16[136,640]{1,0:T(8,128)(2,1)S(1)}, u32[]{:S(2)}, u32[]{:S(2)}) collective-permute-start(bf16[136,640]{1,0:T(8,128)(2,1)S(1)} %constant_dynamic-update-slice_fusion.refs_0_), channel_id=1, source_target_pairs={{0,16},{16,0},{1,17},{17,1},{2,18},{18,2},{3,19},{19,3},{4,20},{20... | collective-permute-start | bytes 522248 | tf_op jit(solution)/shard_map/ppermute | solution.py:410
  101.8 3.9 %collective-permute-start.23 = (bf16[136,640]{1,0:T(8,128)(2,1)S(1)}, bf16[136,640]{1,0:T(8,128)(2,1)S(1)}, u32[]{:S(2)}, u32[]{:S(2)}) collective-permute-start(bf16[136,640]{1,0:T(8,128)(2,1)S(1)} %collective-permute-done.20.refs_2_), channel_id=1, source_target_pairs={{0,16},{16,0},{1,17},{17,1},{2,18},{18,2},{3,19},{19,3},{4,20},{20... | collective-permute-start | bytes 522248 | tf_op jit(solution)/shard_map/ppermute | solution.py:410
  105.8 3.6 %collective-permute-start.22 = (bf16[136,640]{1,0:T(8,128)(2,1)S(1)}, bf16[136,640]{1,0:T(8,128)(2,1)S(1)}, u32[]{:S(2)}, u32[]{:S(2)}) collective-permute-start(bf16[136,640]{1,0:T(8,128)(2,1)S(1)} %collective-permute-done.19.refs_1_), channel_id=1, source_target_pairs={{0,16},{16,0},{1,17},{17,1},{2,18},{18,2},{3,19},{19,3},{4,20},{20... | collective-permute-start | bytes 522248 | tf_op jit(solution)/shard_map/ppermute | solution.py:410
  109.4 2.8 %shard_map.138 = (bf16[1,272,640]{2,1,0:T(8,128)(2,1)S(1)}, f32[272,128]{1,0:T(8,128)S(1)}, f32[272,10]{1,0:T(8,128)S(1)}, f32[272,256]{1,0:T(8,128)S(1)}, f32[2...) custom-call(bf16[136,640]{1,0:T(8,128)(2,1)S(1)} %constant_dynamic-update-slice_fusion.refs_0_, ...), custom_call_target="tpu_custom_call" | custom-call | flops 268435456 | bytes 4194304 | tf_op jit(solution)/shard_map/pallas_call | solution.py:45
  112.2 3.4 %shard_map.139 = (bf16[3,272,640]{2,1,0:T(8,128)(2,1)S(1)}, f32[256,128]{1,0:T(8,128)S(1)}, bf16[2,128,640]{2,1,0:T(8,128)(2,1)S(1)}, bf16[2,128,256]{2,1,0:T(8,...) custom-call(bf16[136,640]{1,0:T(8,128)(2,1)S(1)} %collective-permute-done.18.refs_, ...), custom_call_target="tpu_custom_call" | custom-call | flops 268435456 | bytes 4194304 | tf_op jit(solution)/shard_map/pallas_call | solution.py:45
  115.6 16.6 %all_to_all.21.arrived = bf16[16,16,768]{2,1,0:T(8,128)(2,1)S(1)} all-to-all(bf16[16,16,768]{2,1,0:T(8,128)(2,1)S(1)} %bitcast.28), channel_id=1, replica_groups=mesh['pipe'=2,'chip'=4,'core'=2,'seq_0'=8,'seq_1'=2] {'seq_1','seq_0'}, dimensions={0} | all-to-all | bytes 786432 | tf_op jit(solution)/shard_map/all_to_all | solution.py:459
  133.3 5.9 %all-to-all-start.3 = ((bf16[16,16,640]{2,1,0:T(8,128)(2,1)}), bf16[16,16,640]{2,1,0:T(8,128)(2,1)S(1)}, u32[]{:S(2)}, u32[]{:S(2)}) async-start(bf16[16,16,640]{2,1,0:T(8,128)(2,1)} %shard_map.142), calls=%async_computation.3 | async-start | bytes 655360 | tf_op jit(solution)/shard_map/all_to_all | solution.py:473
  139.2 3.2 %shard_map.140.gate = f32[256,640]{1,0:T(8,128)S(1)} custom-call(bf16[1,272,640]{2,1,0:T(8,128)(2,1)S(1)} %get-tuple-element.87.near, bf16[3,272,640]{2,1,0:T(8,128)(2,1)S(1)} %get-tuple-element.88.far, f32[256,128]{1,0:T(8,128)S(1)} %get-tuple-element.89.scales, bf16[2560,640]{1,0:T(8,128)(2,1)} %bitcast.42), custom_call_target="tpu_custom_call" | custom-call | flops 268435456 | bytes 4194304 | tf_op jit(solution)/shard_map/pallas_call | solution.py:45
  143.3 5.2 %all-to-all-done.3 = bf16[16,16,640]{2,1,0:T(8,128)(2,1)S(1)} async-done(((bf16[16,16,640]{2,1,0:T(8,128)(2,1)}), bf16[16,16,640]{2,1,0:T(8,128)(2,1)S(1)}, u32[]{:S(2)}, u32[]{:S(2)}) %all-to-all-start.3) | async-done | bytes 327712 | tf_op jit(solution)/shard_map/all_to_all | solution.py:473
  148.6 3.3 %shard_map.143 = (bf16[136,640]{1,0:T(8,128)(2,1)S(1)}, bf16[136,640]{1,0:T(8,128)(2,1)S(1)}, bf16[136,640]{1,0:T(8,128)(2,1)S(1)}, bf16[136,640]{1,0:T(8,128)(2...) custom-call(f32[2,128,640]{2,1,0:T(8,128)S(1)} %get-tuple-element.90, ...), custom_call_target="tpu_custom_call" | custom-call | flops 268435456 | bytes 4194304 | tf_op jit(solution)/shard_map/pallas_call | solution.py:45
  151.9 3.1 %collective-permute-start.26 = (bf16[136,640]{1,0:T(8,128)(2,1)S(1)}, bf16[136,640]{1,0:T(8,128)(2,1)S(1)}, u32[]{:S(2)}, u32[]{:S(2)}) collective-permute-start(bf16[136,640]{1,0:T(8,128)(2,1)S(1)} %get-tuple-element.96), channel_id=1, source_target_pairs={{0,16},{16,0},{1,17},{17,1},{2,18},{18,2},{3,19},{19,3},{4,20},{20... | collective-permute-start | bytes 522248 | tf_op jit(solution)/shard_map/ppermute | solution.py:487
  156.1 1.8 %collective-permute-start.27 = (bf16[136,640]{1,0:T(8,128)(2,1)S(1)}, bf16[136,640]{1,0:T(8,128)(2,1)S(1)}, u32[]{:S(2)}, u32[]{:S(2)}) collective-permute-start(bf16[136,640]{1,0:T(8,128)(2,1)S(1)} %shard_map.145), channel_id=1, source_target_pairs={{0,64},{32,96},{64,0},{96,32},{1,65},{33,97},{65,1},{97,33},{2,66}... | collective-permute-start | bytes 522248 | tf_op jit(solution)/shard_map/ppermute | solution.py:490
  158.1 2.7 %collective-permute-start.31 = (bf16[136,640]{1,0:T(8,128)(2,1)S(1)}, bf16[136,640]{1,0:T(8,128)(2,1)S(1)}, u32[]{:S(2)}, u32[]{:S(2)}) collective-permute-start(bf16[136,640]{1,0:T(8,128)(2,1)S(1)} %shard_map.147), channel_id=1, source_target_pairs={{0,96},{32,0},{64,32},{96,64},{1,97},{33,1},{65,33},{97,65},{2,98}... | collective-permute-start | bytes 522248 | tf_op jit(solution)/shard_map/ppermute | solution.py:490
  160.9 2.4 %collective-permute-done.27.refs_0_ = bf16[136,640]{1,0:T(8,128)(2,1)S(1)} collective-permute-done((bf16[136,640]{1,0:T(8,128)(2,1)S(1)}, bf16[136,640]{1,0:T(8,128)(2,1)S(1)}, u32[]{:S(2)}, u32[]{:S(2)}) %collective-permute-start.27) | collective-permute-done | bytes 174112 | tf_op jit(solution)/shard_map/ppermute | solution.py:490
  163.3 4.5 %collective-permute-done.29.refs_1_ = bf16[136,640]{1,0:T(8,128)(2,1)S(1)} collective-permute-done((bf16[136,640]{1,0:T(8,128)(2,1)S(1)}, bf16[136,640]{1,0:T(8,128)(2,1)S(1)}, u32[]{:S(2)}, u32[]{:S(2)}) %collective-permute-start.29) | collective-permute-done | bytes 174112 | tf_op jit(solution)/shard_map/ppermute | solution.py:490
  (94 shorter events, 23.7 us)
Async XLA Ops:
  1.2 3.6 %collective-permute-start = (bf16[2,8,320]{2,1,0:T(8,128)(2,1)S(1)}, bf16[2,8,320]{2,1,0:T(8,128)(2,1)S(1)}, u32[]{:S(2)}, u32[]{:S(2)}) collective-permute-start(bf16[2,8,320]{2,1,0:T(8,128)(2,1)S(1)} %slice.32), channel_id=1, source_target_pairs={{0,1},{1,2},{2,3},{3,4},{4,5},{5,6},{6,7},{7,8},{8,9},{9,10},{10,1... | collective-permute-start | bytes 30728 | tf_op jit(solution)/shard_map/ppermute | solution.py:529
  4.9 2.6 %collective-permute-start.1 = (bf16[136,320]{1,0:T(8,128)(2,1)S(1)}, bf16[136,320]{1,0:T(8,128)(2,1)S(1)}, u32[]{:S(2)}, u32[]{:S(2)}) collective-permute-start(bf16[136,320]{1,0:T(8,128)(2,1)S(1)} %get-tuple-element.102), channel_id=1, source_target_pairs={{0,16},{16,0},{1,17},{17,1},{2,18},{18,2},{3,19},{19,3},{4,20},{20... | collective-permute-start | bytes 261128 | tf_op jit(solution)/shard_map/ppermute | solution.py:532
  7.6 6.2 %collective-permute-start.4 = (bf16[136,640]{1,0:T(8,128)(2,1)S(1)}, bf16[136,640]{1,0:T(8,128)(2,1)S(1)}, u32[]{:S(2)}, u32[]{:S(2)}) collective-permute-start(bf16[136,640]{1,0:T(8,128)(2,1)S(1)} %maximum_select_fusion.1.refs_0_), channel_id=1, source_target_pairs={{0,96},{32,0},{64,32},{96,64},{1,97},{33,1},{65,33},{97,65},{2,98}... | collective-permute-start | bytes 522248 | tf_op jit(solution)/shard_map/ppermute | solution.py:404
  10.4 8.4 %collective-permute-start.3 = (bf16[136,640]{1,0:T(8,128)(2,1)S(1)}, bf16[136,640]{1,0:T(8,128)(2,1)S(1)}, u32[]{:S(2)}, u32[]{:S(2)}) collective-permute-start(bf16[136,640]{1,0:T(8,128)(2,1)S(1)} %maximum_select_fusion.1.refs_0_), channel_id=1, source_target_pairs={{0,32},{32,64},{64,96},{96,0},{1,33},{33,65},{65,97},{97,1},{2,34}... | collective-permute-start | bytes 522248 | tf_op jit(solution)/shard_map/ppermute | solution.py:404
  10.4 11.8 %collective-permute-start.2 = (bf16[136,640]{1,0:T(8,128)(2,1)S(1)}, bf16[136,640]{1,0:T(8,128)(2,1)S(1)}, u32[]{:S(2)}, u32[]{:S(2)}) collective-permute-start(bf16[136,640]{1,0:T(8,128)(2,1)S(1)} %maximum_select_fusion.1.refs_0_), channel_id=1, source_target_pairs={{0,64},{32,96},{64,0},{96,32},{1,65},{33,97},{65,1},{97,33},{2,66}... | collective-permute-start | bytes 522248 | tf_op jit(solution)/shard_map/ppermute | solution.py:404
  12.1 10.1 %collective-permute-start.8 = (bf16[136,640]{1,0:T(8,128)(2,1)S(1)}, bf16[136,640]{1,0:T(8,128)(2,1)S(1)}, u32[]{:S(2)}, u32[]{:S(2)}) collective-permute-start(bf16[136,640]{1,0:T(8,128)(2,1)S(1)} %maximum_select_fusion.1.refs_0_), channel_id=1, source_target_pairs={{0,16},{16,0},{1,17},{17,1},{2,18},{18,2},{3,19},{19,3},{4,20},{20... | collective-permute-start | bytes 522248 | tf_op jit(solution)/shard_map/ppermute | solution.py:410
  13.8 12.8 %collective-permute-start.7 = (bf16[136,640]{1,0:T(8,128)(2,1)S(1)}, bf16[136,640]{1,0:T(8,128)(2,1)S(1)}, u32[]{:S(2)}, u32[]{:S(2)}) collective-permute-start(bf16[136,640]{1,0:T(8,128)(2,1)S(1)} %collective-permute-done.4.refs_2_), channel_id=1, source_target_pairs={{0,16},{16,0},{1,17},{17,1},{2,18},{18,2},{3,19},{19,3},{4,20},{20... | collective-permute-start | bytes 522248 | tf_op jit(solution)/shard_map/ppermute | solution.py:410
  18.8 7.8 %collective-permute-start.6 = (bf16[136,640]{1,0:T(8,128)(2,1)S(1)}, bf16[136,640]{1,0:T(8,128)(2,1)S(1)}, u32[]{:S(2)}, u32[]{:S(2)}) collective-permute-start(bf16[136,640]{1,0:T(8,128)(2,1)S(1)} %collective-permute-done.3.refs_1_), channel_id=1, source_target_pairs={{0,16},{16,0},{1,17},{17,1},{2,18},{18,2},{3,19},{19,3},{4,20},{20... | collective-permute-start | bytes 522248 | tf_op jit(solution)/shard_map/ppermute | solution.py:410
  22.2 4.5 %collective-permute-start.5 = (bf16[136,640]{1,0:T(8,128)(2,1)S(1)}, bf16[136,640]{1,0:T(8,128)(2,1)S(1)}, u32[]{:S(2)}, u32[]{:S(2)}) collective-permute-start(bf16[136,640]{1,0:T(8,128)(2,1)S(1)} %collective-permute-done.2.refs_0_), channel_id=1, source_target_pairs={{0,16},{16,0},{1,17},{17,1},{2,18},{18,2},{3,19},{19,3},{4,20},{20... | collective-permute-start | bytes 522248 | tf_op jit(solution)/shard_map/ppermute | solution.py:410
  53.6 15.4 %all-to-all-start.1 = ((bf16[16,16,640]{2,1,0:T(8,128)(2,1)}), bf16[16,16,640]{2,1,0:T(8,128)(2,1)S(1)}, u32[]{:S(2)}, u32[]{:S(2)}) async-start(bf16[16,16,640]{2,1,0:T(8,128)(2,1)} %shard_map.131), calls=%async_computation.1 | async-start | bytes 655360 | tf_op jit(solution)/shard_map/all_to_all | solution.py:473
  72.4 4.1 %collective-permute-start.10 = (bf16[136,640]{1,0:T(8,128)(2,1)S(1)}, bf16[136,640]{1,0:T(8,128)(2,1)S(1)}, u32[]{:S(2)}, u32[]{:S(2)}) collective-permute-start(bf16[136,640]{1,0:T(8,128)(2,1)S(1)} %get-tuple-element.72), channel_id=1, source_target_pairs={{0,16},{16,0},{1,17},{17,1},{2,18},{18,2},{3,19},{19,3},{4,20},{20... | collective-permute-start | bytes 522248 | tf_op jit(solution)/shard_map/ppermute | solution.py:487
  75.6 2.8 %collective-permute-start.14 = (bf16[136,640]{1,0:T(8,128)(2,1)S(1)}, bf16[136,640]{1,0:T(8,128)(2,1)S(1)}, u32[]{:S(2)}, u32[]{:S(2)}) collective-permute-start(bf16[136,640]{1,0:T(8,128)(2,1)S(1)} %get-tuple-element.76), channel_id=1, source_target_pairs={{0,16},{16,0},{1,17},{17,1},{2,18},{18,2},{3,19},{19,3},{4,20},{20... | collective-permute-start | bytes 522248 | tf_op jit(solution)/shard_map/ppermute | solution.py:487
  76.0 4.4 %collective-permute-start.9 = (bf16[136,640]{1,0:T(8,128)(2,1)S(1)}, bf16[136,640]{1,0:T(8,128)(2,1)S(1)}, u32[]{:S(2)}, u32[]{:S(2)}) collective-permute-start(bf16[136,640]{1,0:T(8,128)(2,1)S(1)} %get-tuple-element.70), channel_id=1, source_target_pairs={{0,16},{16,0},{1,17},{17,1},{2,18},{18,2},{3,19},{19,3},{4,20},{20... | collective-permute-start | bytes 522248 | tf_op jit(solution)/shard_map/ppermute | solution.py:487
  76.6 7.2 %collective-permute-start.11 = (bf16[136,640]{1,0:T(8,128)(2,1)S(1)}, bf16[136,640]{1,0:T(8,128)(2,1)S(1)}, u32[]{:S(2)}, u32[]{:S(2)}) collective-permute-start(bf16[136,640]{1,0:T(8,128)(2,1)S(1)} %shard_map.134), channel_id=1, source_target_pairs={{0,64},{32,96},{64,0},{96,32},{1,65},{33,97},{65,1},{97,33},{2,66}... | collective-permute-start | bytes 522248 | tf_op jit(solution)/shard_map/ppermute | solution.py:490
  77.5 10.8 %collective-permute-start.13 = (bf16[136,640]{1,0:T(8,128)(2,1)S(1)}, bf16[136,640]{1,0:T(8,128)(2,1)S(1)}, u32[]{:S(2)}, u32[]{:S(2)}) collective-permute-start(bf16[136,640]{1,0:T(8,128)(2,1)S(1)} %shard_map.135), channel_id=1, source_target_pairs={{0,32},{32,64},{64,96},{96,0},{1,33},{33,65},{65,97},{97,1},{2,34}... | collective-permute-start | bytes 522248 | tf_op jit(solution)/shard_map/ppermute | solution.py:490
  78.5 9.8 %collective-permute-start.15 = (bf16[136,640]{1,0:T(8,128)(2,1)S(1)}, bf16[136,640]{1,0:T(8,128)(2,1)S(1)}, u32[]{:S(2)}, u32[]{:S(2)}) collective-permute-start(bf16[136,640]{1,0:T(8,128)(2,1)S(1)} %shard_map.136), channel_id=1, source_target_pairs={{0,96},{32,0},{64,32},{96,64},{1,97},{33,1},{65,33},{97,65},{2,98}... | collective-permute-start | bytes 522248 | tf_op jit(solution)/shard_map/ppermute | solution.py:490
  88.4 8.7 %collective-permute-start.16 = (bf16[128,640]{1,0:T(8,128)(2,1)S(1)}, bf16[128,640]{1,0:T(8,128)(2,1)S(1)}, u32[]{:S(2)}, u32[]{:S(2)}) collective-permute-start(bf16[128,640]{1,0:T(8,128)(2,1)S(1)} %shard_map.137), channel_id=1, source_target_pairs={{0,128},{1,129},{2,130},{3,131},{4,132},{5,133},{6,134},{7,135},{8... | collective-permute-start | bytes 491528 | tf_op jit(solution)/shard_map/ppermute | solution.py:546
  97.1 4.7 %collective-permute-start.20 = (bf16[136,640]{1,0:T(8,128)(2,1)S(1)}, bf16[136,640]{1,0:T(8,128)(2,1)S(1)}, u32[]{:S(2)}, u32[]{:S(2)}) collective-permute-start(bf16[136,640]{1,0:T(8,128)(2,1)S(1)} %constant_dynamic-update-slice_fusion.refs_0_), channel_id=1, source_target_pairs={{0,96},{32,0},{64,32},{96,64},{1,97},{33,1},{65,33},{97,65},{2,98}... | collective-permute-start | bytes 522248 | tf_op jit(solution)/shard_map/ppermute | solution.py:404
  97.4 8.3 %collective-permute-start.19 = (bf16[136,640]{1,0:T(8,128)(2,1)S(1)}, bf16[136,640]{1,0:T(8,128)(2,1)S(1)}, u32[]{:S(2)}, u32[]{:S(2)}) collective-permute-start(bf16[136,640]{1,0:T(8,128)(2,1)S(1)} %constant_dynamic-update-slice_fusion.refs_0_), channel_id=1, source_target_pairs={{0,32},{32,64},{64,96},{96,0},{1,33},{33,65},{65,97},{97,1},{2,34}... | collective-permute-start | bytes 522248 | tf_op jit(solution)/shard_map/ppermute | solution.py:404
  98.7 10.7 %collective-permute-start.18 = (bf16[136,640]{1,0:T(8,128)(2,1)S(1)}, bf16[136,640]{1,0:T(8,128)(2,1)S(1)}, u32[]{:S(2)}, u32[]{:S(2)}) collective-permute-start(bf16[136,640]{1,0:T(8,128)(2,1)S(1)} %constant_dynamic-update-slice_fusion.refs_0_), channel_id=1, source_target_pairs={{0,64},{32,96},{64,0},{96,32},{1,65},{33,97},{65,1},{97,33},{2,66}... | collective-permute-start | bytes 522248 | tf_op jit(solution)/shard_map/ppermute | solution.py:404
  99.4 9.9 %collective-permute-start.24 = (bf16[136,640]{1,0:T(8,128)(2,1)S(1)}, bf16[136,640]{1,0:T(8,128)(2,1)S(1)}, u32[]{:S(2)}, u32[]{:S(2)}) collective-permute-start(bf16[136,640]{1,0:T(8,128)(2,1)S(1)} %constant_dynamic-update-slice_fusion.refs_0_), channel_id=1, source_target_pairs={{0,16},{16,0},{1,17},{17,1},{2,18},{18,2},{3,19},{19,3},{4,20},{20... | collective-permute-start | bytes 522248 | tf_op jit(solution)/shard_map/ppermute | solution.py:410
  101.8 10.4 %collective-permute-start.23 = (bf16[136,640]{1,0:T(8,128)(2,1)S(1)}, bf16[136,640]{1,0:T(8,128)(2,1)S(1)}, u32[]{:S(2)}, u32[]{:S(2)}) collective-permute-start(bf16[136,640]{1,0:T(8,128)(2,1)S(1)} %collective-permute-done.20.refs_2_), channel_id=1, source_target_pairs={{0,16},{16,0},{1,17},{17,1},{2,18},{18,2},{3,19},{19,3},{4,20},{20... | collective-permute-start | bytes 522248 | tf_op jit(solution)/shard_map/ppermute | solution.py:410
  105.8 6.4 %collective-permute-start.22 = (bf16[136,640]{1,0:T(8,128)(2,1)S(1)}, bf16[136,640]{1,0:T(8,128)(2,1)S(1)}, u32[]{:S(2)}, u32[]{:S(2)}) collective-permute-start(bf16[136,640]{1,0:T(8,128)(2,1)S(1)} %collective-permute-done.19.refs_1_), channel_id=1, source_target_pairs={{0,16},{16,0},{1,17},{17,1},{2,18},{18,2},{3,19},{19,3},{4,20},{20... | collective-permute-start | bytes 522248 | tf_op jit(solution)/shard_map/ppermute | solution.py:410
  109.3 2.9 %collective-permute-start.21 = (bf16[136,640]{1,0:T(8,128)(2,1)S(1)}, bf16[136,640]{1,0:T(8,128)(2,1)S(1)}, u32[]{:S(2)}, u32[]{:S(2)}) collective-permute-start(bf16[136,640]{1,0:T(8,128)(2,1)S(1)} %collective-permute-done.18.refs_0_), channel_id=1, source_target_pairs={{0,16},{16,0},{1,17},{17,1},{2,18},{18,2},{3,19},{19,3},{4,20},{20... | collective-permute-start | bytes 522248 | tf_op jit(solution)/shard_map/ppermute | solution.py:410
  133.3 15.2 %all-to-all-start.3 = ((bf16[16,16,640]{2,1,0:T(8,128)(2,1)}), bf16[16,16,640]{2,1,0:T(8,128)(2,1)S(1)}, u32[]{:S(2)}, u32[]{:S(2)}) async-start(bf16[16,16,640]{2,1,0:T(8,128)(2,1)} %shard_map.142), calls=%async_computation.3 | async-start | bytes 655360 | tf_op jit(solution)/shard_map/all_to_all | solution.py:473
  151.9 4.2 %collective-permute-start.26 = (bf16[136,640]{1,0:T(8,128)(2,1)S(1)}, bf16[136,640]{1,0:T(8,128)(2,1)S(1)}, u32[]{:S(2)}, u32[]{:S(2)}) collective-permute-start(bf16[136,640]{1,0:T(8,128)(2,1)S(1)} %get-tuple-element.96), channel_id=1, source_target_pairs={{0,16},{16,0},{1,17},{17,1},{2,18},{18,2},{3,19},{19,3},{4,20},{20... | collective-permute-start | bytes 522248 | tf_op jit(solution)/shard_map/ppermute | solution.py:487
  155.0 2.9 %collective-permute-start.28 = (bf16[136,640]{1,0:T(8,128)(2,1)S(1)}, bf16[136,640]{1,0:T(8,128)(2,1)S(1)}, u32[]{:S(2)}, u32[]{:S(2)}) collective-permute-start(bf16[136,640]{1,0:T(8,128)(2,1)S(1)} %get-tuple-element.98), channel_id=1, source_target_pairs={{0,16},{16,0},{1,17},{17,1},{2,18},{18,2},{3,19},{19,3},{4,20},{20... | collective-permute-start | bytes 522248 | tf_op jit(solution)/shard_map/ppermute | solution.py:487
  155.1 2.9 %collective-permute-start.30 = (bf16[136,640]{1,0:T(8,128)(2,1)S(1)}, bf16[136,640]{1,0:T(8,128)(2,1)S(1)}, u32[]{:S(2)}, u32[]{:S(2)}) collective-permute-start(bf16[136,640]{1,0:T(8,128)(2,1)S(1)} %get-tuple-element.100), channel_id=1, source_target_pairs={{0,16},{16,0},{1,17},{17,1},{2,18},{18,2},{3,19},{19,3},{4,20},{20... | collective-permute-start | bytes 522248 | tf_op jit(solution)/shard_map/ppermute | solution.py:487
  155.5 5.3 %collective-permute-start.25 = (bf16[136,640]{1,0:T(8,128)(2,1)S(1)}, bf16[136,640]{1,0:T(8,128)(2,1)S(1)}, u32[]{:S(2)}, u32[]{:S(2)}) collective-permute-start(bf16[136,640]{1,0:T(8,128)(2,1)S(1)} %get-tuple-element.94), channel_id=1, source_target_pairs={{0,16},{16,0},{1,17},{17,1},{2,18},{18,2},{3,19},{19,3},{4,20},{20... | collective-permute-start | bytes 522248 | tf_op jit(solution)/shard_map/ppermute | solution.py:487
  156.1 7.2 %collective-permute-start.27 = (bf16[136,640]{1,0:T(8,128)(2,1)S(1)}, bf16[136,640]{1,0:T(8,128)(2,1)S(1)}, u32[]{:S(2)}, u32[]{:S(2)}) collective-permute-start(bf16[136,640]{1,0:T(8,128)(2,1)S(1)} %shard_map.145), channel_id=1, source_target_pairs={{0,64},{32,96},{64,0},{96,32},{1,65},{33,97},{65,1},{97,33},{2,66}... | collective-permute-start | bytes 522248 | tf_op jit(solution)/shard_map/ppermute | solution.py:490
  158.0 9.8 %collective-permute-start.29 = (bf16[136,640]{1,0:T(8,128)(2,1)S(1)}, bf16[136,640]{1,0:T(8,128)(2,1)S(1)}, u32[]{:S(2)}, u32[]{:S(2)}) collective-permute-start(bf16[136,640]{1,0:T(8,128)(2,1)S(1)} %shard_map.146), channel_id=1, source_target_pairs={{0,32},{32,64},{64,96},{96,0},{1,33},{33,65},{65,97},{97,1},{2,34}... | collective-permute-start | bytes 522248 | tf_op jit(solution)/shard_map/ppermute | solution.py:490
  158.1 9.7 %collective-permute-start.31 = (bf16[136,640]{1,0:T(8,128)(2,1)S(1)}, bf16[136,640]{1,0:T(8,128)(2,1)S(1)}, u32[]{:S(2)}, u32[]{:S(2)}) collective-permute-start(bf16[136,640]{1,0:T(8,128)(2,1)S(1)} %shard_map.147), channel_id=1, source_target_pairs={{0,96},{32,0},{64,32},{96,64},{1,97},{33,1},{65,33},{97,65},{2,98}... | collective-permute-start | bytes 522248 | tf_op jit(solution)/shard_map/ppermute | solution.py:490
  (13 other events, 184.6 us)
